TPU v7x, 32 devices: a whole 2x2x4 slice. The times are simulated.
32 devices in a mesh: dp: 8 (over z, x), ctx: 4 (over y, core).
Axes of the slice: x: 2, y: 2, z: 4, core: 2. Of those that a mesh axis runs over, the one named last changes fastest.
Arguments:
- inputs: bfloat16 [16, 1024, 1536], P('dp', 'ctx'), may hold values from -6 to 6
- segments: int32 [16, 1024], P('dp', 'ctx'), may hold values from 0 to 5, never falling along the last dimension, each value on 1 to 512 neighbouring positions
- cotangent: bfloat16 [16, 1024, 1536], P('dp', 'ctx'), may hold values from -6 to 6
- w_query: bfloat16 [1536, 1536], P(('dp', 'ctx')), may hold values from -4 to 4
- w_key: bfloat16 [1536, 768], P(('dp', 'ctx')), may hold values from -0.15625 to 0.15625
- w_value: bfloat16 [1536, 768], P(('dp', 'ctx')), may hold values from -0.15625 to 0.15625
- w_out: bfloat16 [1536, 1536], P(('dp', 'ctx')), may hold values from -0.625 to 0.625
- w_gate: bfloat16 [1536, 4096], P(('dp', 'ctx')), may hold values from -0.15625 to 0.15625
- w_up: bfloat16 [1536, 4096], P(('dp', 'ctx')), may hold values from -0.15625 to 0.15625
- w_down: bfloat16 [4096, 1536], P(('dp', 'ctx')), may hold values from -0.09375 to 0.09375
- gain_attn: bfloat16 [1536], P(('dp', 'ctx')), may hold values from 0.5 to 1.5
- gain_ffn: bfloat16 [1536], P(('dp', 'ctx')), may hold values from 0.5 to 1.5
Outputs:
- outputs: float32 [16, 1024, 1536], P('dp', 'ctx')
- input_grad: float32 [16, 1024, 1536], P('dp', 'ctx')
- grad_query: float32 [1536, 1536], P(('dp', 'ctx'))
- grad_key: float32 [1536, 768], P(('dp', 'ctx'))
- grad_value: float32 [1536, 768], P(('dp', 'ctx'))
- grad_out: float32 [1536, 1536], P(('dp', 'ctx'))
- grad_gate: float32 [1536, 4096], P(('dp', 'ctx'))
- grad_up: float32 [1536, 4096], P(('dp', 'ctx'))
- grad_down: float32 [4096, 1536], P(('dp', 'ctx'))
- grad_gain_attn: float32 [1536], P(('dp', 'ctx'))
- grad_gain_ffn: float32 [1536], P(('dp', 'ctx'))
Inputs may be any that keep to these rules, and one draw needn't show every extreme that they name: `segments`: within each sequence the ids never fall; each document spans 1 to 512 tokens, and one spans exactly 512.
All inputs are finite; a program needn't handle non-finite values.
Results may differ from a plain program's by a relative error of at most 0.02.
The roundings to bfloat16 on the way count: a program that leaves them out, or rounds other values in their place, can miss the bound.
Values may be sent and summed in bfloat16 or wider, within the bound.
A program may use at most 384 MiB of HBM per device.

v0:
```python
import math

import jax
import jax.numpy as jnp
from jax import lax
from jax.sharding import PartitionSpec as P

H = 16
KV = 8
HD = 96


EPS = 1e-05
THETA = 100000.0
MASKED = -1e30


def matmul(left, right):
    return jnp.dot(left, right, preferred_element_type=jnp.float32)


def contract_rows(left, right):
    return lax.dot_general(
        left, right, (((0,), (0,)), ((), ())), preferred_element_type=jnp.float32
    )


def times_transpose(left, right):
    return lax.dot_general(
        left, right, (((1,), (1,)), ((), ())), preferred_element_type=jnp.float32
    )


def rope_tables(positions):
    half_dim = HD // 2
    frequency = THETA ** (-(jnp.arange(half_dim, dtype=jnp.float32) * (2.0 / HD)))
    angles = positions.astype(jnp.float32)[:, None] * frequency[None, :]
    return (jnp.cos(angles), jnp.sin(angles))


def rotate(vectors, cosine, sine_values):
    half_dim = HD // 2
    first_half = vectors[..., :half_dim]
    second_half = vectors[..., half_dim:]
    cos_b = cosine[:, None, :]
    sin_b = sine_values[:, None, :]
    return jnp.concatenate(
        [first_half * cos_b - second_half * sin_b, second_half * cos_b + first_half * sin_b],
        axis=-1,
    )


def rms_scale(values):
    return lax.rsqrt(jnp.mean(values * values, axis=-1, keepdims=True) + EPS)


def norm_back(d_normed, values, scale, gain):
    weighted = d_normed * gain.astype(jnp.float32)
    return scale * weighted - values * (scale * scale * scale) * jnp.mean(
        weighted * values, axis=-1, keepdims=True
    )


def allowed_pairs(positions, doc_ids, key_positions, key_docs):
    return (doc_ids[:, None] == key_docs[None, :]) & (key_positions[None, :] <= positions[:, None])


def block_scores(queries, keys_all, allowed):
    scores = jnp.einsum(
        "rkgd,lkd->kgrl", queries, keys_all, preferred_element_type=jnp.float32
    ) * HD ** (-0.5)
    return jnp.where(allowed[None, None], scores, MASKED)


def attend_block(queries, keys_all, values_all, allowed):
    scores = block_scores(queries, keys_all, allowed)
    row_max = jnp.max(scores, axis=-1, keepdims=True)
    summed = jnp.sum(jnp.exp(scores - row_max), axis=-1, keepdims=True)
    log_total = row_max + jnp.log(summed)
    probs_low = jnp.exp(scores - log_total).astype(jnp.bfloat16)
    attended = jnp.einsum(
        "kgrl,lkd->rkgd", probs_low, values_all, preferred_element_type=jnp.float32
    )
    return (attended.astype(jnp.bfloat16), log_total[..., 0])


def attend_back(queries, keys_all, values_all, allowed, log_total, attended, d_attended):
    scores = block_scores(queries, keys_all, allowed)
    probs = jnp.exp(scores - log_total[..., None])
    probs_low = probs.astype(jnp.bfloat16)
    row_delta = jnp.einsum(
        "rkgd,rkgd->kgr", d_attended, attended, preferred_element_type=jnp.float32
    )
    d_probs = jnp.einsum(
        "rkgd,lkd->kgrl", d_attended, values_all, preferred_element_type=jnp.float32
    )
    d_scores = (probs * (d_probs - row_delta[..., None]) * HD ** (-0.5)).astype(jnp.bfloat16)
    d_query = jnp.einsum("kgrl,lkd->rkgd", d_scores, keys_all, preferred_element_type=jnp.float32)
    d_keys = jnp.einsum("kgrl,rkgd->lkd", d_scores, queries, preferred_element_type=jnp.float32)
    d_values = jnp.einsum(
        "kgrl,rkgd->lkd", probs_low, d_attended, preferred_element_type=jnp.float32
    )
    return (d_query, d_keys, d_values)


def attention_forward(queries, keys_all, values_all, positions, doc_ids, key_positions, key_docs):
    row_count = queries.shape[0]
    block_rows = math.gcd(row_count, 512)

    def one_block(step_index):
        allowed = allowed_pairs(positions, doc_ids, key_positions, key_docs)
        return attend_block(queries, keys_all, values_all, allowed)

    attended, log_total = lax.map(one_block, jnp.arange(row_count // block_rows, dtype=jnp.int32))
    return (attended.reshape(queries.shape), log_total)


def attention_backward(
    queries,
    keys_all,
    values_all,
    positions,
    doc_ids,
    key_positions,
    key_docs,
    log_total,
    attended,
    d_attended,
):
    row_count = queries.shape[0]
    block_rows = math.gcd(row_count, 512)

    def step_fn(carried, step_index):
        key_sum, value_sum = carried
        allowed = allowed_pairs(positions, doc_ids, key_positions, key_docs)
        d_query, d_keys, d_values = attend_back(
            queries, keys_all, values_all, allowed, log_total[step_index], attended, d_attended
        )
        return ((key_sum + d_keys, value_sum + d_values), d_query)

    zero_sums = jnp.zeros(keys_all.shape, jnp.float32)
    (key_sum, value_sum), d_queries = lax.scan(
        step_fn, (zero_sums, zero_sums), jnp.arange(row_count // block_rows, dtype=jnp.int32)
    )
    return (d_queries.reshape(queries.shape), key_sum, value_sum)


def by_owner(terms, devices):
    return [term.reshape((devices, term.shape[0] // devices) + term.shape[1:]) for term in terms]


def per_device(
    inputs,
    segments,
    cotangent,
    w_query,
    w_key,
    w_value,
    w_out,
    w_gate,
    w_up,
    w_down,
    gain_attn,
    gain_ffn,
):
    micro_count = inputs.shape[0]
    stretch_rows = inputs.shape[1]
    groups = H // KV
    ctx_rank = lax.axis_index("ctx")
    positions = ctx_rank * stretch_rows + jnp.arange(stretch_rows, dtype=jnp.int32)
    cosine, sine_values = rope_tables(positions)
    doc_all = lax.all_gather(segments, "ctx", axis=1, tiled=True)
    length = doc_all.shape[1]
    key_positions = jnp.arange(length, dtype=jnp.int32)
    devices = lax.axis_size(("dp", "ctx"))
    shards = (w_query, w_key, w_value, w_out, w_gate, w_up, w_down, gain_attn, gain_ffn)
    totals = [
        jnp.zeros((weight_shard.shape[0] * devices,) + weight_shard.shape[1:], jnp.float32)
        for weight_shard in shards
    ]
    outputs_all = []
    input_grads = []
    for micro_index in range(micro_count):
        gathered = (
            lax.all_gather(w_query, ("dp", "ctx"), axis=0, tiled=True),
            lax.all_gather(w_key, ("dp", "ctx"), axis=0, tiled=True),
            lax.all_gather(w_value, ("dp", "ctx"), axis=0, tiled=True),
            lax.all_gather(w_out, ("dp", "ctx"), axis=0, tiled=True),
            lax.all_gather(w_gate, ("dp", "ctx"), axis=0, tiled=True),
            lax.all_gather(w_up, ("dp", "ctx"), axis=0, tiled=True),
            lax.all_gather(w_down, ("dp", "ctx"), axis=0, tiled=True),
            lax.all_gather(gain_attn, ("dp", "ctx"), axis=0, tiled=True),
            lax.all_gather(gain_ffn, ("dp", "ctx"), axis=0, tiled=True),
        )
        (
            full_query,
            full_key,
            full_value,
            full_out,
            full_gate,
            full_up,
            full_down,
            full_gain_attn,
            full_gain_ffn,
        ) = gathered
        doc_ids = segments[micro_index]
        key_docs = doc_all[micro_index]
        cot_rows = cotangent[micro_index]
        residual = inputs[micro_index].astype(jnp.float32)
        scale_attn = rms_scale(residual)
        normed_attn = (residual * scale_attn * full_gain_attn.astype(jnp.float32)).astype(
            jnp.bfloat16
        )
        queries = (
            rotate(
                matmul(normed_attn, full_query).reshape(stretch_rows, H, HD), cosine, sine_values
            )
            .astype(jnp.bfloat16)
            .reshape(stretch_rows, KV, groups, HD)
        )
        keys_local = (
            rotate(matmul(normed_attn, full_key).reshape(stretch_rows, KV, HD), cosine, sine_values)
            .astype(jnp.bfloat16)
            .reshape(stretch_rows, KV * HD)
        )
        values_local = matmul(normed_attn, full_value).astype(jnp.bfloat16)
        keys_flat, values_flat = (
            lax.all_gather(keys_local, "ctx", axis=0, tiled=True),
            lax.all_gather(values_local, "ctx", axis=0, tiled=True),
        )
        keys_all = keys_flat.reshape(length, KV, HD)
        values_all = values_flat.reshape(length, KV, HD)
        attended, log_total = attention_forward(
            queries, keys_all, values_all, positions, doc_ids, key_positions, key_docs
        )
        attended_flat = attended.reshape(stretch_rows, H * HD)
        mid = residual + matmul(attended_flat, full_out)
        scale_ffn = rms_scale(mid)
        normed_ffn = (mid * scale_ffn * full_gain_ffn.astype(jnp.float32)).astype(jnp.bfloat16)
        gate_act = matmul(normed_ffn, full_gate)
        up_act = matmul(normed_ffn, full_up)
        sigmoid_gate = jax.nn.sigmoid(gate_act)
        hidden = (gate_act * sigmoid_gate * up_act).astype(jnp.bfloat16)
        outputs_all.append(mid + matmul(hidden, full_down))
        regathered = (
            lax.all_gather(w_query, ("dp", "ctx"), axis=0, tiled=True),
            lax.all_gather(w_key, ("dp", "ctx"), axis=0, tiled=True),
            lax.all_gather(w_value, ("dp", "ctx"), axis=0, tiled=True),
            lax.all_gather(w_out, ("dp", "ctx"), axis=0, tiled=True),
            lax.all_gather(w_gate, ("dp", "ctx"), axis=0, tiled=True),
            lax.all_gather(w_up, ("dp", "ctx"), axis=0, tiled=True),
            lax.all_gather(w_down, ("dp", "ctx"), axis=0, tiled=True),
            lax.all_gather(gain_attn, ("dp", "ctx"), axis=0, tiled=True),
            lax.all_gather(gain_ffn, ("dp", "ctx"), axis=0, tiled=True),
        )
        keys_again, values_again = (
            lax.all_gather(keys_local, "ctx", axis=0, tiled=True),
            lax.all_gather(values_local, "ctx", axis=0, tiled=True),
        )
        keys_back = keys_again.reshape(length, KV, HD)
        values_back = values_again.reshape(length, KV, HD)
        (
            back_query,
            back_key,
            back_value,
            back_out,
            back_gate,
            back_up,
            back_down,
            back_gain_attn,
            back_gain_ffn,
        ) = regathered
        grad_down = contract_rows(hidden, cot_rows)
        d_hidden = times_transpose(cot_rows, back_down)
        d_gate = (
            d_hidden * up_act * sigmoid_gate * (1.0 + gate_act * (1.0 - sigmoid_gate))
        ).astype(jnp.bfloat16)
        d_up = (d_hidden * gate_act * sigmoid_gate).astype(jnp.bfloat16)
        grad_gate = contract_rows(normed_ffn, d_gate)
        grad_up = contract_rows(normed_ffn, d_up)
        d_normed_ffn = times_transpose(d_gate, back_gate) + times_transpose(d_up, back_up)
        grad_gain_ffn = jnp.sum(d_normed_ffn * mid * scale_ffn, axis=0)
        d_mid = cot_rows.astype(jnp.float32) + norm_back(
            d_normed_ffn, mid, scale_ffn, back_gain_ffn
        )
        d_mid_low = d_mid.astype(jnp.bfloat16)
        grad_out = contract_rows(attended_flat, d_mid_low)
        d_attended = (
            times_transpose(d_mid_low, back_out)
            .astype(jnp.bfloat16)
            .reshape(stretch_rows, KV, groups, HD)
        )
        d_query_rot, d_key_terms, d_value_terms = attention_backward(
            queries,
            keys_back,
            values_back,
            positions,
            doc_ids,
            key_positions,
            key_docs,
            log_total,
            attended,
            d_attended,
        )
        d_key_mine, d_value_mine = (
            lax.psum_scatter(
                d_key_terms.reshape(length, KV * HD).astype(jnp.bfloat16),
                "ctx",
                scatter_dimension=0,
                tiled=True,
            ).astype(jnp.float32),
            lax.psum_scatter(
                d_value_terms.reshape(length, KV * HD).astype(jnp.bfloat16),
                "ctx",
                scatter_dimension=0,
                tiled=True,
            ).astype(jnp.float32),
        )
        d_query = (
            rotate(d_query_rot.reshape(stretch_rows, H, HD), cosine, -sine_values)
            .astype(jnp.bfloat16)
            .reshape(stretch_rows, H * HD)
        )
        d_key = (
            rotate(d_key_mine.reshape(stretch_rows, KV, HD), cosine, -sine_values)
            .astype(jnp.bfloat16)
            .reshape(stretch_rows, KV * HD)
        )
        d_value = d_value_mine.astype(jnp.bfloat16)
        grad_query = contract_rows(normed_attn, d_query)
        grad_key = contract_rows(normed_attn, d_key)
        grad_value = contract_rows(normed_attn, d_value)
        d_normed_attn = (
            times_transpose(d_query, back_query)
            + times_transpose(d_key, back_key)
            + times_transpose(d_value, back_value)
        )
        grad_gain_attn = jnp.sum(d_normed_attn * residual * scale_attn, axis=0)
        input_grads.append(d_mid + norm_back(d_normed_attn, residual, scale_attn, back_gain_attn))
        grad_list = [
            grad_query,
            grad_key,
            grad_value,
            grad_out,
            grad_gate,
            grad_up,
            grad_down,
            grad_gain_attn,
            grad_gain_ffn,
        ]
        totals = [summed + grad_term for summed, grad_term in zip(totals, grad_list)]
    owned = by_owner(totals, devices)
    received = (
        lax.all_to_all(
            owned[0].astype(jnp.bfloat16), ("dp", "ctx"), split_axis=0, concat_axis=0, tiled=True
        ).astype(jnp.float32),
        lax.all_to_all(
            owned[1].astype(jnp.bfloat16), ("dp", "ctx"), split_axis=0, concat_axis=0, tiled=True
        ).astype(jnp.float32),
        lax.all_to_all(
            owned[2].astype(jnp.bfloat16), ("dp", "ctx"), split_axis=0, concat_axis=0, tiled=True
        ).astype(jnp.float32),
        lax.all_to_all(
            owned[3].astype(jnp.bfloat16), ("dp", "ctx"), split_axis=0, concat_axis=0, tiled=True
        ).astype(jnp.float32),
        lax.all_to_all(
            owned[4].astype(jnp.bfloat16), ("dp", "ctx"), split_axis=0, concat_axis=0, tiled=True
        ).astype(jnp.float32),
        lax.all_to_all(
            owned[5].astype(jnp.bfloat16), ("dp", "ctx"), split_axis=0, concat_axis=0, tiled=True
        ).astype(jnp.float32),
        lax.all_to_all(
            owned[6].astype(jnp.bfloat16), ("dp", "ctx"), split_axis=0, concat_axis=0, tiled=True
        ).astype(jnp.float32),
        lax.all_to_all(
            owned[7].astype(jnp.bfloat16), ("dp", "ctx"), split_axis=0, concat_axis=0, tiled=True
        ).astype(jnp.float32),
        lax.all_to_all(
            owned[8].astype(jnp.bfloat16), ("dp", "ctx"), split_axis=0, concat_axis=0, tiled=True
        ).astype(jnp.float32),
    )
    reduced = [jnp.sum(piece, axis=0) for piece in received]
    return (
        jnp.stack(outputs_all),
        jnp.stack(input_grads),
        reduced[0],
        reduced[1],
        reduced[2],
        reduced[3],
        reduced[4],
        reduced[5],
        reduced[6],
        reduced[7],
        reduced[8],
    )


def solution(mesh):
    return jax.shard_map(
        per_device,
        mesh=mesh,
        in_specs=(
            P("dp", "ctx", None),
            P("dp", "ctx"),
            P("dp", "ctx", None),
            P(("dp", "ctx"), None),
            P(("dp", "ctx"), None),
            P(("dp", "ctx"), None),
            P(("dp", "ctx"), None),
            P(("dp", "ctx"), None),
            P(("dp", "ctx"), None),
            P(("dp", "ctx"), None),
            P(("dp", "ctx")),
            P(("dp", "ctx")),
        ),
        out_specs=(
            P("dp", "ctx", None),
            P("dp", "ctx", None),
            P(("dp", "ctx"), None),
            P(("dp", "ctx"), None),
            P(("dp", "ctx"), None),
            P(("dp", "ctx"), None),
            P(("dp", "ctx"), None),
            P(("dp", "ctx"), None),
            P(("dp", "ctx"), None),
            P(("dp", "ctx")),
            P(("dp", "ctx")),
        ),
        check_vma=False,
    )
```

profile of v0, /device:TPU:0, one launch (start us, length us, event | category | flops | bytes accessed | tf_op | source)
XLA Modules:
  0.0 2081.6 jit_solution(10939846959269241301)
XLA Ops:
  10.4 42.1 %all-reduce.2 = (bf16[1536]{0:T(1024)(128)(2,1)S(1)}, bf16[1536]{0:T(1024)(128)(2,1)S(1)}) all-reduce(bf16[1536]{0:T(1024)(128)(2,1)S(1)} %dynamic-update-slice, bf16[1536]{0:T(1024)(128)(2,1)S(1)} %dynamic-update-slice.1), channel_id=1, replica_groups=mesh['dp'=8,'ctx'=4] {'dp','ctx'}, use_global_device_ids=true, to_apply=%add | all-reduce | flops 3072 | bytes 12288
  54.9 15.8 all-gather.12.cloned.1.call-done
  79.2 50.3 %all-gather.16.cloned.1.call-done = bf16[1536,768]{1,0:T(8,128)(2,1)} async-done(((bf16[48,768]{1,0:T(8,128)(2,1)}), bf16[1536,768]{1,0:T(8,128)(2,1)}) %all-gather.16.cloned.1.call-update) | async-done | bytes 2359312 | tf_op jit(solution)/shard_map/all_gather | solution.py:186
  142.1 5.8 all_gather.31
  152.7 19.1 all-gather.30.cloned.1.call-done
  174.4 63.8 %all-gather.20.cloned.1.call-done = bf16[1536,1536]{1,0:T(8,128)(2,1)} async-done(((bf16[48,1536]{1,0:T(8,128)(2,1)}), bf16[1536,1536]{1,0:T(8,128)(2,1)}) %all-gather.20.cloned.1.call-update) | async-done | bytes 4718608 | tf_op jit(solution)/shard_map/all_gather | solution.py:185
  238.1 6.6 copy.57
  251.9 5.8 all-gather.18.cloned.1.call-done
  257.7 8.8 fusion.8
  266.5 9.4 exponential_reduce_fusion.1
  275.9 9.0 convolution_convert_fusion.3
  284.9 39.3 %all-gather.22.cloned.1.call-done = bf16[1536,1536]{1,0:T(8,128)(2,1)} async-done(((bf16[48,1536]{1,0:T(8,128)(2,1)}), bf16[1536,1536]{1,0:T(8,128)(2,1)}) %all-gather.22.cloned.1.call-update) | async-done | bytes 4718608 | tf_op jit(solution)/shard_map/all_gather | solution.py:188
  328.3 16.2 all-gather.32.cloned.1.call-done
  344.5 10.1 fusion.9
  354.5 9.6 exponential_reduce_fusion
  364.1 10.4 convolution_convert_fusion.2
  377.5 65.1 %all-gather.24.cloned.1.call-done = bf16[1536,4096]{1,0:T(8,128)(2,1)} async-done(((bf16[48,4096]{1,0:T(8,128)(2,1)}), bf16[1536,4096]{1,0:T(8,128)(2,1)}) %all-gather.24.cloned.1.call-update) | async-done | bytes 12582928 | tf_op jit(solution)/shard_map/all_gather | solution.py:189
  442.6 9.5 fusion.117
  452.1 87.0 %all-gather.26.cloned.1.call-done = bf16[1536,4096]{1,0:T(8,128)(2,1)} async-done(((bf16[48,4096]{1,0:T(8,128)(2,1)}), bf16[1536,4096]{1,0:T(8,128)(2,1)}) %all-gather.26.cloned.1.call-update) | async-done | bytes 12582928 | tf_op jit(solution)/shard_map/all_gather | solution.py:190
  539.1 9.5 fusion.118
  548.7 87.2 %all-gather.28.cloned.1.call-done = bf16[4096,1536]{1,0:T(8,128)(2,1)} async-done(((bf16[128,1536]{1,0:T(8,128)(2,1)}), bf16[4096,1536]{1,0:T(8,128)(2,1)}) %all-gather.28.cloned.1.call-update) | async-done | bytes 12582928 | tf_op jit(solution)/shard_map/all_gather | solution.py:191
  635.8 10.6 multiply_convert_fusion.2
  646.5 8.0 fusion.121
  654.5 9.8 multiply_reduce_fusion.1
  664.4 6.8 fusion.120
  671.2 9.7 fusion.119
  680.9 15.2 multiply_convert_fusion
  696.1 7.4 fusion.124
  703.6 10.3 multiply_reduce_fusion
  722.4 10.0 fusion.2
  736.6 4.6 convolution_convert_fusion.1
  745.1 9.5 fusion.5
  758.5 9.3 bitcast_convert_fusion.2
  767.9 6.9 fusion.125
  778.6 9.5 bitcast_convert_fusion
  794.8 5.4 fusion.123
  811.3 12.8 reduce-scatter.7.cloned.1.call-done
  828.2 26.3 %reduce-scatter.11.cloned.1.call-done = bf16[256,768]{0,1:T(8,128)(2,1)} async-done(((bf16[1024,768]{0,1:T(8,128)(2,1)}), bf16[256,768]{0,1:T(8,128)(2,1)}) %reduce-scatter.11.cloned.1.call-update) | async-done | bytes 393232 | tf_op jit(solution)/shard_map/reduce_scatter | solution.py:312
  862.8 4.7 all-to-all-start.7
  867.6 4.8 add_convert_fusion.3
  881.6 51.0 %all-to-all-done.2 = bf16[32,48,768]{2,1,0:T(8,128)(2,1)} async-done(((bf16[32,48,768]{2,1,0:T(8,128)(2,1)}), bf16[32,48,768]{2,1,0:T(8,128)(2,1)}, u32[]{:S(2)}, u32[]{:S(2)}) %all-to-all-start.2) | async-done | bytes 2359328 | tf_op jit(solution)/shard_map/all_to_all | solution.py:360
  932.6 4.6 all-to-all-start.1
  943.4 48.0 %all-to-all-done.1 = bf16[32,48,768]{2,1,0:T(8,128)(2,1)} async-done(((bf16[32,48,768]{2,1,0:T(8,128)(2,1)}), bf16[32,48,768]{2,1,0:T(8,128)(2,1)}, u32[]{:S(2)}, u32[]{:S(2)}) %all-to-all-start.1) | async-done | bytes 2359328 | tf_op jit(solution)/shard_map/all_to_all | solution.py:357
  991.5 4.4 all-to-all-start.3
  1002.4 99.1 %all-to-all-done.3 = bf16[32,48,1536]{2,1,0:T(8,128)(2,1)} async-done(((bf16[32,48,1536]{2,1,0:T(8,128)(2,1)}), bf16[32,48,1536]{2,1,0:T(8,128)(2,1)}, u32[]{:S(2)}, u32[]{:S(2)}) %all-to-all-start.3) | async-done | bytes 4718624 | tf_op jit(solution)/shard_map/all_to_all | solution.py:363
  1101.4 5.2 all-to-all-start
  1106.7 13.6 fusion.128
  1120.3 15.8 add_convert_fusion.1
  1136.1 76.2 %all-to-all-done = bf16[32,48,1536]{2,1,0:T(8,128)(2,1)} async-done(((bf16[32,48,1536]{2,1,0:T(8,128)(2,1)}), bf16[32,48,1536]{2,1,0:T(8,128)(2,1)}, u32[]{:S(2)}, u32[]{:S(2)}) %all-to-all-start) | async-done | bytes 4718624 | tf_op jit(solution)/shard_map/all_to_all | solution.py:354
  1212.2 5.6 all-to-all-start.5
  1217.9 13.6 fusion.127
  1231.5 15.8 add_convert_fusion.2
  1247.3 246.0 %all-to-all-done.5 = bf16[32,48,4096]{2,1,0:T(8,128)(2,1)} async-done(((bf16[32,48,4096]{2,1,0:T(8,128)(2,1)}), bf16[32,48,4096]{2,1,0:T(8,128)(2,1)}, u32[]{:S(2)}, u32[]{:S(2)}) %all-to-all-start.5) | async-done | bytes 12582944 | tf_op jit(solution)/shard_map/all_to_all | solution.py:369
  1493.3 11.6 all-to-all-start.4
  1504.9 13.6 fusion.55
  1518.5 15.2 add_convert_fusion
  1533.7 246.7 %all-to-all-done.4 = bf16[32,48,4096]{2,1,0:T(8,128)(2,1)} async-done(((bf16[32,48,4096]{2,1,0:T(8,128)(2,1)}), bf16[32,48,4096]{2,1,0:T(8,128)(2,1)}, u32[]{:S(2)}, u32[]{:S(2)}) %all-to-all-start.4) | async-done | bytes 12582944 | tf_op jit(solution)/shard_map/all_to_all | solution.py:366
  1780.3 11.6 all-to-all-start.6
  1791.9 9.1 fusion.13
  1801.1 6.6 fusion.12
  1828.5 8.5 convert_reduce_fusion.1
  1837.0 8.5 convert_reduce_fusion.2
  1845.5 221.8 %all-to-all-done.6 = bf16[32,128,1536]{2,1,0:T(8,128)(2,1)} async-done(((bf16[32,128,1536]{2,1,0:T(8,128)(2,1)}), bf16[32,128,1536]{2,1,0:T(8,128)(2,1)}, u32[]{:S(2)}, u32[]{:S(2)}) %all-to-all-start.6) | async-done | bytes 12582944 | tf_op jit(solution)/shard_map/all_to_all | solution.py:372
  2067.4 7.5 convert_reduce_fusion
  (266 shorter events, 144.5 us)
Async XLA Ops:
  7.2 63.5 %all-gather.12.cloned.1.call-start = ((), (), s32[]{:S(2)}) async-start(), calls=%async_computation.13 | async-start | bytes 2433024 | tf_op jit(solution)/shard_map/all_gather | solution.py:187
  7.9 121.6 %all-gather.16.cloned.1.call-start = ((), (), s32[]{:S(2)}) async-start(), calls=%async_computation.15 | async-start | bytes 2433024 | tf_op jit(solution)/shard_map/all_gather | solution.py:186
  8.7 141.5 %all-gather.14.cloned.1.call-start = ((), (), s32[]{:S(2)}) async-start(), calls=%async_computation.14 | async-start | bytes 1966080 | tf_op jit(solution)/shard_map/all_gather | solution.py:229
  52.6 196.4 %copy-start.54 = (f32[1536]{0:T(1024)}, f32[1536]{0:T(1024)S(1)}, u32[]{:S(2)}) copy-start(f32[1536]{0:T(1024)S(1)} %convert_element_type.358) | copy-start | bytes 18436
  54.9 189.8 %copy-start.60 = (f32[256]{0:T(256)}, f32[256]{0:T(256)S(1)}, u32[]{:S(2)}) copy-start(f32[256]{0:T(256)S(1)} %get-tuple-element.214) | copy-start | bytes 3076
  54.9 194.0 %copy-start.58 = (f32[256]{0:T(256)}, f32[256]{0:T(256)S(1)}, u32[]{:S(2)}) copy-start(f32[256]{0:T(256)S(1)} %get-tuple-element.232) | copy-start | bytes 3076
  74.3 97.5 %all-gather.30.cloned.1.call-start = ((), (), s32[]{:S(2)}) async-start(), calls=%async_computation.22 | async-start | bytes 1966080 | tf_op jit(solution)/shard_map/all_gather | solution.py:229
  77.7 160.5 %all-gather.20.cloned.1.call-start = ((), (), s32[]{:S(2)}) async-start(), calls=%async_computation.17 | async-start | bytes 4866048 | tf_op jit(solution)/shard_map/all_gather | solution.py:185
  78.2 179.4 %all-gather.18.cloned.1.call-start = ((), (), s32[]{:S(2)}) async-start(), calls=%async_computation.16 | async-start | bytes 1966080 | tf_op jit(solution)/shard_map/all_gather | solution.py:228
  79.2 171.3 %copy-start.52 = (f32[256,48]{0,1:T(8,128)}, f32[256,48]{0,1:T(8,128)S(1)}, u32[]{:S(2)}) copy-start(f32[256,48]{0,1:T(8,128)S(1)} %get-tuple-element.210) | copy-start | bytes 147460
  138.4 185.8 %all-gather.22.cloned.1.call-start = ((), (), s32[]{:S(2)}) async-start(), calls=%async_computation.18 | async-start | bytes 4866048 | tf_op jit(solution)/shard_map/all_gather | solution.py:188
  139.2 205.3 %all-gather.32.cloned.1.call-start = ((), (), s32[]{:S(2)}) async-start(), calls=%async_computation.23 | async-start | bytes 1966080 | tf_op jit(solution)/shard_map/all_gather | solution.py:228
  140.0 302.6 %all-gather.24.cloned.1.call-start = ((), (), s32[]{:S(2)}) async-start(), calls=%async_computation.19 | async-start | bytes 12976128 | tf_op jit(solution)/shard_map/all_gather | solution.py:189
  140.7 398.4 %all-gather.26.cloned.1.call-start = ((), (), s32[]{:S(2)}) async-start(), calls=%async_computation.20 | async-start | bytes 12976128 | tf_op jit(solution)/shard_map/all_gather | solution.py:190
  141.3 494.5 %all-gather.28.cloned.1.call-start = ((), (), s32[]{:S(2)}) async-start(), calls=%async_computation.21 | async-start | bytes 12976128 | tf_op jit(solution)/shard_map/all_gather | solution.py:191
  142.1 660.7 %reduce-scatter.9.cloned.1.call-start = ((), (), s32[]{:S(2)}) async-start(), calls=%async_computation.26 | async-start | bytes 1966080 | tf_op jit(solution)/shard_map/reduce_scatter | solution.py:306
  148.7 127.2 %copy-start.26 = (pred[256,1024]{0,1:T(8,128)(4,1)}, pred[256,1024]{0,1:T(8,128)(4,1)S(1)}, u32[]{:S(2)}) copy-start(pred[256,1024]{0,1:T(8,128)(4,1)S(1)} %get-tuple-element.219) | copy-start | bytes 786436
  251.9 14.6 copy-start.28
  251.9 14.6 copy-start.30
  266.5 9.4 copy-start.48
  328.2 326.3 %copy-start.6 = (f32[256,1536]{1,0:T(8,128)}, f32[256,1536]{1,0:T(8,128)S(1)}, u32[]{:S(2)}) copy-start(f32[256,1536]{1,0:T(8,128)S(1)} %get-tuple-element.226) | copy-start | bytes 4718596
  354.5 20.0 slice-start
  364.1 10.4 slice-start.1
  377.5 161.6 %copy-start.16 = (bf16[256,1536]{1,0:T(8,128)(2,1)}, bf16[256,1536]{1,0:T(8,128)(2,1)S(1)}, u32[]{:S(2)}) copy-start(bf16[256,1536]{1,0:T(8,128)(2,1)S(1)} %multiply_convert_fusion.7) | copy-start | bytes 2359300
  646.5 8.0 copy-start.44
  646.5 8.1 copy-start.46
  646.5 8.1 copy-start.20
  664.4 6.8 copy-start.18
  671.2 9.7 copy-start.19
  696.1 7.5 copy-start.45
  696.1 22.2 %slice-start.2 = ((s8[4718592]{0:T(1024)(128)(4,1)}), s8[4194304]{0:T(1024)(128)(4,1)S(1)}, s32[]{:S(2)}) async-start(s8[4718592]{0:T(1024)(128)(4,1)} %bitcast.348), calls=%async_computation.30 | async-start | bytes 8388608
  703.6 10.3 copy-start.7
  703.6 14.8 slice-start.3
  722.1 10.3 copy-start.39
  722.4 10.0 copy-start.32
  722.4 10.0 copy-start.33
  736.3 67.6 %reduce-scatter.5.cloned.1.call-start = ((), (), s32[]{:S(2)}) async-start(), calls=%async_computation.24 | async-start | bytes 1966080 | tf_op jit(solution)/shard_map/reduce_scatter | solution.py:306
  745.1 9.6 copy-start.29
  745.1 9.6 copy-start.31
  758.5 65.6 %reduce-scatter.7.cloned.1.call-start = ((), (), s32[]{:S(2)}) async-start(), calls=%async_computation.25 | async-start | bytes 1966080 | tf_op jit(solution)/shard_map/reduce_scatter | solution.py:312
  767.9 6.9 copy-start.15
  767.9 86.6 %reduce-scatter.11.cloned.1.call-start = ((), (), s32[]{:S(2)}) async-start(), calls=%async_computation.27 | async-start | bytes 1966080 | tf_op jit(solution)/shard_map/reduce_scatter | solution.py:312
  767.9 8.0 copy-start.4
  778.6 14.0 copy-start.53
  778.6 14.0 copy-start.56
  788.8 74.1 %all-to-all-start.8 = ((bf16[32,1,48]{2,1,0:T(2,128)(2,1)}), bf16[32,1,48]{2,1,0:T(2,128)(2,1)}, u32[]{:S(2)}, u32[]{:S(2)}) async-start(bf16[32,1,48]{2,1,0:T(2,128)(2,1)} %convert_element_type.447), calls=%async_computation.12 | async-start | bytes 32768 | tf_op jit(solution)/shard_map/all_to_all | solution.py:378
  792.5 7.6 slice-start.4
  794.6 5.5 copy-start.38
  794.7 5.4 copy-start.36
  794.7 5.4 slice-start.5
  809.3 14.8 copy-start.1
  809.3 14.8 copy-start.55
  809.3 14.8 copy-start.59
  828.2 29.5 %copy-start.61 = (f32[256]{0:T(256)S(1)}, f32[256]{0:T(256)}, u32[]{:S(2)}) copy-start(f32[256]{0:T(256)} %copy-done.60) | copy-start | bytes 3076
  862.8 11.7 all-to-all-start.7
  874.5 58.1 %all-to-all-start.2 = ((bf16[32,48,768]{2,1,0:T(8,128)(2,1)}), bf16[32,48,768]{2,1,0:T(8,128)(2,1)}, u32[]{:S(2)}, u32[]{:S(2)}) async-start(bf16[32,48,768]{2,1,0:T(8,128)(2,1)} %bitcast.363), calls=%async_computation.6 | async-start | bytes 4718592 | tf_op jit(solution)/shard_map/all_to_all | solution.py:360
  932.6 58.9 %all-to-all-start.1 = ((bf16[32,48,768]{2,1,0:T(8,128)(2,1)}), bf16[32,48,768]{2,1,0:T(8,128)(2,1)}, u32[]{:S(2)}, u32[]{:S(2)}) async-start(bf16[32,48,768]{2,1,0:T(8,128)(2,1)} %bitcast.364), calls=%async_computation.5 | async-start | bytes 4718592 | tf_op jit(solution)/shard_map/all_to_all | solution.py:357
  991.5 110.0 %all-to-all-start.3 = ((bf16[32,48,1536]{2,1,0:T(8,128)(2,1)}), bf16[32,48,1536]{2,1,0:T(8,128)(2,1)}, u32[]{:S(2)}, u32[]{:S(2)}) async-start(bf16[32,48,1536]{2,1,0:T(8,128)(2,1)} %bitcast.352), calls=%async_computation.7 | async-start | bytes 9437184 | tf_op jit(solution)/shard_map/all_to_all | solution.py:363
  1101.4 110.8 %all-to-all-start = ((bf16[32,48,1536]{2,1,0:T(8,128)(2,1)}), bf16[32,48,1536]{2,1,0:T(8,128)(2,1)}, u32[]{:S(2)}, u32[]{:S(2)}) async-start(bf16[32,48,1536]{2,1,0:T(8,128)(2,1)} %bitcast.351), calls=%async_computation.4 | async-start | bytes 9437184 | tf_op jit(solution)/shard_map/all_to_all | solution.py:354
  1212.2 281.1 %all-to-all-start.5 = ((bf16[32,48,4096]{2,1,0:T(8,128)(2,1)}), bf16[32,48,4096]{2,1,0:T(8,128)(2,1)}, u32[]{:S(2)}, u32[]{:S(2)}) async-start(bf16[32,48,4096]{2,1,0:T(8,128)(2,1)} %bitcast.344), calls=%async_computation.9 | async-start | bytes 25165824 | tf_op jit(solution)/shard_map/all_to_all | solution.py:369
  1493.3 287.0 %all-to-all-start.4 = ((bf16[32,48,4096]{2,1,0:T(8,128)(2,1)}), bf16[32,48,4096]{2,1,0:T(8,128)(2,1)}, u32[]{:S(2)}, u32[]{:S(2)}) async-start(bf16[32,48,4096]{2,1,0:T(8,128)(2,1)} %bitcast.345), calls=%async_computation.8 | async-start | bytes 25165824 | tf_op jit(solution)/shard_map/all_to_all | solution.py:366
  1780.3 287.0 %all-to-all-start.6 = ((bf16[32,128,1536]{2,1,0:T(8,128)(2,1)}), bf16[32,128,1536]{2,1,0:T(8,128)(2,1)}, u32[]{:S(2)}, u32[]{:S(2)}) async-start(bf16[32,128,1536]{2,1,0:T(8,128)(2,1)} %bitcast.343), calls=%async_computation.10 | async-start | bytes 25165824 | tf_op jit(solution)/shard_map/all_to_all | solution.py:372
  1791.9 9.2 copy-start.21
  1791.9 9.2 copy-start.24
  (33 other events, 104.8 us)
Sparse Core Ops, SparseCore 0:
  10.9 59.7 all-gather.11
  73.6 55.8 all-gather.15
  131.6 18.4 all-gather.13
  152.1 19.6 all-gather.29
  174.5 63.5 all-gather.19
  239.5 18.1 all-gather.17
  260.6 63.5 all-gather.21
  326.3 18.1 all-gather.31
  347.4 95.1 all-gather.23
  445.3 93.7 all-gather.25
  542.0 93.7 all-gather.27
  736.4 26.6 reduce-scatter.8
  765.6 27.9 reduce-scatter.4
  796.1 27.9 reduce-scatter.6
  826.5 27.9 reduce-scatter.10
where the time goes:
time: 2090 us; the launch traced here: 2080 us
  waiting for transfers between devices  1490 us (71%)
  matrix products  366 us (18%)
  other arithmetic  81.6 us (4%)
  starting transfers between devices  56.1 us (3%)
  blocking collectives  48 us (2%)
  local copies, waits for them, and re-layouts  28.6 us (1%)
    all_to_all x1, waiting for transfers between devices, per_device(): lax.all_to_all(owned[4].astype(jnp.bfloat16), ('dp', 'ctx'), split_axis=0...  247 us
    all_to_all x1, waiting for transfers between devices, per_device(): lax.all_to_all(owned[5].astype(jnp.bfloat16), ('dp', 'ctx'), split_axis=0...  246 us
    all_to_all x1, waiting for transfers between devices, per_device(): lax.all_to_all(owned[6].astype(jnp.bfloat16), ('dp', 'ctx'), split_axis=0...  222 us
    dot_general x14, matrix products, contract_rows(): lax.dot_general(left, right, (((0,), (0,)), ((), ())), preferred_element_...  112 us
    all_to_all x1, waiting for transfers between devices, per_device(): lax.all_to_all(owned[3].astype(jnp.bfloat16), ('dp', 'ctx'), split_axis=0...  99.1 us
    all_gather x1, waiting for transfers between devices, per_device(): lax.all_gather(w_down, ('dp', 'ctx'), axis=0, tiled=True)  87.2 us
    all_gather x1, waiting for transfers between devices, per_device(): lax.all_gather(w_up, ('dp', 'ctx'), axis=0, tiled=True)  87 us
    dot_general x14, matrix products, times_transpose(): lax.dot_general(left, right, (((1,), (1,)), ((), ())), preferred_element_...  86.4 us
  transfers between devices with their start and end apart: 24, of which 21 were waited for; matrix products, arithmetic and copies ran while one was open for 18% of the time, Pallas kernels for 0%

commit v1 on v0

v1 whole, which is shorter than its diff:
```python
import functools

import jax
import jax.numpy as jnp
from jax import lax
from jax.experimental import pallas as pl
from jax.experimental.pallas import tpu as pltpu
from jax.sharding import PartitionSpec as P

H = 16
KV = 8
HD = 96
HALF = HD // 2
LANES = 128
SPAN = 512

EPS = 1e-05
THETA = 100000.0
MASKED = -1e30

BF = jnp.bfloat16
F32 = jnp.float32
MESH = pl.DeviceIdType.MESH
VMEM_LIMIT = 60 * 1024 * 1024


def sds(shape, dtype=BF):
    return jax.ShapeDtypeStruct(tuple(shape), dtype)


def dot_nn(a, b):
    return lax.dot_general(a, b, (((1,), (0,)), ((), ())), preferred_element_type=F32)


def dot_nt(a, b):
    return lax.dot_general(a, b, (((1,), (1,)), ((), ())), preferred_element_type=F32)


def dot_tn(a, b):
    return lax.dot_general(a, b, (((0,), (0,)), ((), ())), preferred_element_type=F32)


class Sizes:
    def __init__(self, dp, ctx):
        self.dp, self.ctx = dp, ctx
        self.outer = 4 if dp % 4 == 0 else dp
        self.inner = dp // self.outer
        self.ys = ctx // 2


class Link:
    def __init__(self, z, send_sems, recv_sems, local_sems):
        self.z = z
        self.d = lax.axis_index("dp")
        self.c = lax.axis_index("ctx")
        self.o, self.i = lax.div(self.d, z.inner), lax.rem(self.d, z.inner)
        self.y, self.k = lax.div(self.c, 2), lax.rem(self.c, 2)
        self.sems = (send_sems, recv_sems, local_sems)
        self.sent, self.inflight, self.local = 0, [], []

    def ctx_dev(self, y, k):
        return (self.d, y * 2 + k)

    def ctx_peers(self):
        n = self.z.ctx
        return [lax.rem(self.c + j, n) for j in range(1, n)]

    def y_peers(self):
        n = self.z.ys
        return [lax.rem(self.y + j, n) for j in range(1, n)]

    def outer_to(self, j):
        return lax.rem(self.o + j, self.z.outer)

    def outer_from(self, j):
        return lax.rem(self.o + self.z.outer - j, self.z.outer)

    def inner_to(self, j):
        return lax.rem(self.i + j, self.z.inner)

    def dp_dev(self, o, i):
        return (o * self.z.inner + i, self.c)

    def barrier(self):
        devices = [(self.d, c) for c in self.ctx_peers()]
        devices += [self.dp_dev(self.outer_to(j), self.i) for j in range(1, self.z.outer)]
        devices += [self.dp_dev(self.o, self.inner_to(j)) for j in range(1, self.z.inner)]
        barrier = pltpu.get_barrier_semaphore()
        for device in devices:
            pl.semaphore_signal(barrier, inc=1, device_id=device, device_id_type=MESH)
        pl.semaphore_wait(barrier, len(devices))

    def put(self, src, dst, device):
        n = self.sent
        self.sent += 1
        copy = pltpu.make_async_remote_copy(
            src_ref=src,
            dst_ref=dst,
            send_sem=self.sems[0].at[n],
            recv_sem=self.sems[1].at[n],
            device_id=device,
            device_id_type=MESH,
        )
        copy.start()
        self.inflight.append(copy)
        return copy

    def keep(self, src, dst):
        copy = pltpu.make_async_copy(src, dst, self.sems[2].at[len(self.local)])
        copy.start()
        self.local.append(copy)
        return copy

    def arrived(self, copy):
        copy.wait_recv()
        self.inflight = [other for other in self.inflight if other is not copy]
        self.landed.append(copy)

    def finish(self):
        for copy in self.inflight:
            copy.wait_recv()
        for copy in self.landed + self.inflight:
            copy.wait_send()
        for copy in self.local:
            copy.wait()

    landed = None


def communicate(z, name, cid, script, ins, outs, scratch=()):
    n_in, n_out = len(ins), len(outs)

    def kernel(*refs):
        in_refs, out_refs = refs[:n_in], refs[n_in : n_in + n_out]
        send, recv, local = refs[n_in + n_out : n_in + n_out + 3]
        link = Link(z, send, recv, local)
        link.landed = []
        link.barrier()
        script(link, in_refs, out_refs, refs[n_in + n_out + 3 :])
        link.finish()

    hbm = pl.BlockSpec(memory_space=pltpu.HBM)
    return pl.pallas_call(
        kernel,
        name=name,
        out_shape=list(outs),
        in_specs=[hbm] * n_in,
        out_specs=[hbm] * n_out,
        scratch_shapes=[
            pltpu.SemaphoreType.DMA((64,)),
            pltpu.SemaphoreType.DMA((64,)),
            pltpu.SemaphoreType.DMA((16,)),
        ]
        + list(scratch),
        compiler_params=pltpu.CompilerParams(
            collective_id=cid, has_side_effects=True, vmem_limit_bytes=VMEM_LIMIT
        ),
    )(*ins)


def gather_ctx_start(link, src, buf, wait_src=None):
    slot = buf.at[link.c]
    ways = []
    for j in range(1, link.z.ys):
        to = lax.rem(link.y + j, link.z.ys)
        frm = lax.rem(link.y + link.z.ys - j, link.z.ys)
        ways.append((frm, link.put(src, slot, link.ctx_dev(to, link.k))))
    link.put(src, slot, link.ctx_dev(link.y, 1 - link.k))
    return ways


def gather_ctx_forward(link, buf, ways):
    for frm, copy in ways:
        link.arrived(copy)
        slot = buf.at[frm * 2 + link.k]
        link.put(slot, slot, link.ctx_dev(link.y, 1 - link.k))


def exchange_ctx(link, pack, slot_of):
    return [link.put(pack.at[c], slot_of(link.c), (link.d, c)) for c in link.ctx_peers()]


def gather_dp_start(link, slot_of):
    own = slot_of(link.d)
    ways = []
    for j in range(1, link.z.outer):
        copy = link.put(own, own, link.dp_dev(link.outer_to(j), link.i))
        ways.append((link.outer_from(j), copy))
    for j in range(1, link.z.inner):
        link.put(own, own, link.dp_dev(link.o, link.inner_to(j)))
    return ways


def gather_dp_forward(link, slot_of, ways):
    for frm, copy in ways:
        link.arrived(copy)
        slot = slot_of(frm * link.z.inner + link.i)
        for j in range(1, link.z.inner):
            link.put(slot, slot, link.dp_dev(link.o, link.inner_to(j)))


def scatter_inner(link, src, dst):
    for j in range(1, link.z.inner):
        to = link.inner_to(j)
        link.put(src.at[:, to], dst.at[j - 1], link.dp_dev(link.o, to))


def scatter_outer(link, src, dst):
    for j in range(1, link.z.outer):
        to = link.outer_to(j)
        link.put(src.at[to], dst.at[j - 1], link.dp_dev(to, link.i))


def scatter_core(link, src, dst):
    link.put(src.at[:, 1 - link.k], dst, link.ctx_dev(link.y, 1 - link.k))


def scatter_y(link, src, dst):
    for j in range(1, link.z.ys):
        to = lax.rem(link.y + j, link.z.ys)
        link.put(src.at[to], dst.at[j - 1], link.ctx_dev(to, link.k))


def rotated(u, cos, sin):
    return u * cos + pltpu.roll(u, LANES // 2, 1) * sin


def qkv_kernel(hc, kvc, x_ref, gain_ref, w_ref, cos_ref, sin_ref, n_ref, q_ref, k_ref, v_ref):
    x = x_ref[0, 0].astype(F32)
    scale = lax.rsqrt(jnp.mean(x * x, axis=-1, keepdims=True) + EPS)
    normed = (x * scale * gain_ref[...]).astype(BF)
    n_ref[0, 0] = normed
    full = dot_nn(normed, w_ref[...])
    cos, sin = cos_ref[0], sin_ref[0]
    for h in range(hc + kvc):
        piece = rotated(full[:, h * LANES : (h + 1) * LANES], cos, sin).astype(BF)
        if h < hc:
            q_ref[0, 0, :, h * LANES : (h + 1) * LANES] = piece
        else:
            k_ref[0, 0, :, (h - hc) * LANES : (h - hc + 1) * LANES] = piece
    v_ref[0, 0] = full[:, (hc + kvc) * LANES :].astype(BF)


def qkv_call(z, x_all, gain, w, cos, sin, hc, kvc):
    ctx, m, r, d = x_all.shape
    row = lambda s, b: (s, b, 0, 0)
    whole = lambda s, b: (0, 0)
    table = pl.BlockSpec((1, r, LANES), lambda s, b: (s, 0, 0))
    return pl.pallas_call(
        functools.partial(qkv_kernel, hc, kvc),
        name="qkv",
        grid=(ctx, m),
        in_specs=[
            pl.BlockSpec((1, 1, r, d), row),
            pl.BlockSpec((1, d), whole),
            pl.BlockSpec(w.shape, whole, pipeline_mode=pl.Buffered(1)),
            table,
            table,
        ],
        out_specs=[
            pl.BlockSpec((1, 1, r, d), row),
            pl.BlockSpec((1, 1, r, hc * LANES), row),
            pl.BlockSpec((1, 1, r, kvc * LANES), row),
            pl.BlockSpec((1, 1, r, kvc * LANES), row),
        ],
        out_shape=[
            sds((ctx, m, r, d)),
            sds((ctx, m, r, hc * LANES)),
            sds((ctx, m, r, kvc * LANES)),
            sds((ctx, m, r, kvc * LANES)),
        ],
        compiler_params=pltpu.CompilerParams(vmem_limit_bytes=VMEM_LIMIT),
    )(x_all, gain, w, cos, sin)


def window_of(s, r, ctx):
    blocks = min(ctx, SPAN // r + 1)
    return jnp.maximum(s - (blocks - 1), 0), blocks


def bias_of(s, first, blocks, r, qdoc_ref, kdoc_ref):
    qdoc = qdoc_ref[0, 0]
    pieces = []
    for b in range(blocks):
        kdoc = kdoc_ref[first + b, 0]
        rows = lax.broadcasted_iota(jnp.int32, (r, r), 0) + s * r
        cols = lax.broadcasted_iota(jnp.int32, (r, r), 1) + (first + b) * r
        pieces.append(jnp.where((qdoc == kdoc) & (cols <= rows), 0.0, MASKED))
    return jnp.concatenate(pieces, axis=1)


def attend_kernel(hc, kvc, ctx, q_ref, k_ref, v_ref, qdoc_ref, kdoc_ref, out_ref, lse_ref):
    s = pl.program_id(1)
    r = q_ref.shape[2]
    first, blocks = window_of(s, r, ctx)
    bias = bias_of(s, first, blocks, r, qdoc_ref, kdoc_ref)
    lane = lax.broadcasted_iota(jnp.int32, (r, LANES), 1)
    lse_all = jnp.zeros((r, LANES), F32)
    outs = []
    for h in range(hc):
        g = h * kvc // hc
        q = q_ref[0, 0, :, h * LANES : (h + 1) * LANES]
        k = k_ref[pl.ds(first, blocks), 0, :, g * LANES : (g + 1) * LANES].reshape(blocks * r, LANES)
        v = v_ref[pl.ds(first, blocks), 0, :, g * LANES : (g + 1) * LANES].reshape(blocks * r, LANES)
        scores = dot_nt(q, k) * HD ** (-0.5) + bias
        top = jnp.max(scores, axis=-1, keepdims=True)
        e = jnp.exp(scores - top)
        total = jnp.sum(e, axis=-1, keepdims=True)
        probs = (e * (1.0 / total)).astype(BF)
        outs.append(dot_nn(probs, v)[:, :HD])
        lse_all = jnp.where(lane == h, top + jnp.log(total), lse_all)
    out_ref[0, 0] = jnp.concatenate(outs, axis=1).astype(BF)
    lse_ref[0, 0] = lse_all


def attend_call(z, q, k, v, qdoc, kdoc, hc, kvc):
    ctx, m, r, _ = q.shape
    row = lambda b, s: (s, b, 0, 0)
    seq = lambda b, s: (0, b, 0, 0)
    return pl.pallas_call(
        functools.partial(attend_kernel, hc, kvc, ctx),
        name="attend",
        grid=(m, ctx),
        in_specs=[
            pl.BlockSpec((1, 1, r, hc * LANES), row),
            pl.BlockSpec((ctx, 1, r, kvc * LANES), seq),
            pl.BlockSpec((ctx, 1, r, kvc * LANES), seq),
            pl.BlockSpec((1, 1, r, 1), row),
            pl.BlockSpec((ctx, 1, 1, r), seq),
        ],
        out_specs=[pl.BlockSpec((1, 1, r, hc * HD), row), pl.BlockSpec((1, 1, r, LANES), row)],
        out_shape=[sds((ctx, m, r, hc * HD)), sds((ctx, m, r, LANES), F32)],
        compiler_params=pltpu.CompilerParams(vmem_limit_bytes=VMEM_LIMIT),
    )(q, k, v, qdoc, kdoc)


def attend_back_kernel(
    hc, kvc, ctx, q_ref, k_ref, v_ref, qdoc_ref, kdoc_ref, o_ref, do_ref, lse_ref, cos_ref, sin_ref,
    out_ref, dk_acc, dv_acc,
):
    s = pl.program_id(1)
    r = q_ref.shape[2]
    first, blocks = window_of(s, r, ctx)
    bias = bias_of(s, first, blocks, r, qdoc_ref, kdoc_ref)

    @pl.when(s == 0)
    def _():
        dk_acc[...] = jnp.zeros_like(dk_acc)
        dv_acc[...] = jnp.zeros_like(dv_acc)

    cos, sin = cos_ref[s], sin_ref[s]
    lse_all = lse_ref[0, 0]
    for h in range(hc):
        g = h * kvc // hc
        q = q_ref[0, 0, :, h * LANES : (h + 1) * LANES]
        k = k_ref[pl.ds(first, blocks), 0, :, g * LANES : (g + 1) * LANES].reshape(blocks * r, LANES)
        v = v_ref[pl.ds(first, blocks), 0, :, g * LANES : (g + 1) * LANES].reshape(blocks * r, LANES)
        o = o_ref[0, 0, :, h * HD : (h + 1) * HD].astype(F32)
        do = do_ref[0, 0, :, h * HD : (h + 1) * HD]
        delta = jnp.sum(o * do.astype(F32), axis=-1, keepdims=True)
        do = jnp.concatenate([do, jnp.zeros((r, LANES - HD), BF)], axis=1)
        scores = dot_nt(q, k) * HD ** (-0.5) + bias
        probs = jnp.exp(scores - lse_all[:, h : h + 1])
        d_probs = dot_nt(do, v)
        d_scores = (probs * (d_probs - delta) * HD ** (-0.5)).astype(BF)
        dq = dot_nn(d_scores, k)
        out_ref[s, 0, :, h * LANES : (h + 1) * LANES] = rotated(dq, cos, -sin).astype(BF)
        dk = dot_tn(d_scores, q).reshape(blocks, r, LANES)
        dv = dot_tn(probs.astype(BF), do).reshape(blocks, r, LANES)
        here = slice(g * LANES, (g + 1) * LANES)
        dk_acc[pl.ds(first, blocks), :, here] += dk
        dv_acc[pl.ds(first, blocks), :, here] += dv

    @pl.when(s == ctx - 1)
    def _():
        for b in range(ctx):
            for g in range(kvc):
                here = slice(g * LANES, (g + 1) * LANES)
                at = (hc + g) * LANES
                dk = rotated(dk_acc[b, :, here], cos_ref[b], -sin_ref[b])
                out_ref[b, 0, :, at : at + LANES] = dk.astype(BF)
                at += kvc * LANES
                out_ref[b, 0, :, at : at + LANES] = dv_acc[b, :, here].astype(BF)


def attend_back_call(z, q, k, v, qdoc, kdoc, o, do, lse, cos, sin, hc, kvc):
    ctx, m, r, _ = q.shape
    row = lambda b, s: (s, b, 0, 0)
    seq = lambda b, s: (0, b, 0, 0)
    table = pl.BlockSpec((ctx, r, LANES), lambda b, s: (0, 0, 0))
    width = (hc + 2 * kvc) * LANES
    return pl.pallas_call(
        functools.partial(attend_back_kernel, hc, kvc, ctx),
        name="attend_back",
        grid=(m, ctx),
        in_specs=[
            pl.BlockSpec((1, 1, r, hc * LANES), row),
            pl.BlockSpec((ctx, 1, r, kvc * LANES), seq),
            pl.BlockSpec((ctx, 1, r, kvc * LANES), seq),
            pl.BlockSpec((1, 1, r, 1), row),
            pl.BlockSpec((ctx, 1, 1, r), seq),
            pl.BlockSpec((1, 1, r, hc * HD), row),
            pl.BlockSpec((1, 1, r, hc * HD), row),
            pl.BlockSpec((1, 1, r, LANES), row),
            table,
            table,
        ],
        out_specs=pl.BlockSpec((ctx, 1, r, width), seq),
        out_shape=sds((ctx, m, r, width)),
        scratch_shapes=[
            pltpu.VMEM((ctx, r, kvc * LANES), F32),
            pltpu.VMEM((ctx, r, kvc * LANES), F32),
        ],
        compiler_params=pltpu.CompilerParams(vmem_limit_bytes=VMEM_LIMIT),
    )(q, k, v, qdoc, kdoc, o, do, lse, cos, sin)


def mlp_kernel(x_ref, cot_ref, gu_ref, down_ref, hid_ref, dgu_ref, out_ref, dn_ref):
    x, cot = x_ref[0, 0], cot_ref[0, 0]
    f = down_ref.shape[0]
    both = dot_nn(x, gu_ref[...])
    gate, up = both[:, :f], both[:, f:]
    d_hidden = dot_nt(cot, down_ref[...])
    sg = jax.nn.sigmoid(gate)
    act = gate * sg
    hidden = (act * up).astype(BF)
    hid_ref[0, 0] = hidden
    d_gate = (d_hidden * up * sg * (1.0 + gate * (1.0 - sg))).astype(BF)
    d_up = (d_hidden * act).astype(BF)
    dgu_ref[0, 0, :, :f] = d_gate
    dgu_ref[0, 0, :, f:] = d_up
    out_ref[0, 0] = dot_nn(hidden, down_ref[...]).astype(BF)
    dn_ref[0, 0] = (dot_nt(d_gate, gu_ref[:, :f]) + dot_nt(d_up, gu_ref[:, f:])).astype(BF)


def mlp_call(z, x, cot, gu, down):
    ctx, m, r, d = x.shape
    f = down.shape[0]
    row = lambda s, b: (s, b, 0, 0)
    whole = lambda s, b: (0, 0)
    return pl.pallas_call(
        mlp_kernel,
        name="mlp",
        grid=(ctx, m),
        in_specs=[
            pl.BlockSpec((1, 1, r, d), row),
            pl.BlockSpec((1, 1, r, d), row),
            pl.BlockSpec(gu.shape, whole, pipeline_mode=pl.Buffered(1)),
            pl.BlockSpec(down.shape, whole, pipeline_mode=pl.Buffered(1)),
        ],
        out_specs=[
            pl.BlockSpec((1, 1, r, f), row),
            pl.BlockSpec((1, 1, r, 2 * f), row),
            pl.BlockSpec((1, 1, r, d), row),
            pl.BlockSpec((1, 1, r, d), row),
        ],
        out_shape=[
            sds((ctx, m, r, f)),
            sds((ctx, m, r, 2 * f)),
            sds((ctx, m, r, d)),
            sds((ctx, m, r, d)),
        ],
        compiler_params=pltpu.CompilerParams(vmem_limit_bytes=VMEM_LIMIT),
    )(x, cot, gu, down)


def pad_heads(w, heads, split):
    rows = w.shape[0]
    if split:
        w = jnp.pad(w.reshape(rows, heads, 2, HALF), ((0, 0), (0, 0), (0, 0), (0, LANES // 2 - HALF)))
    else:
        w = jnp.pad(w.reshape(rows, heads, HD), ((0, 0), (0, 0), (0, LANES - HD)))
    return w.reshape(rows, heads * LANES)


def unpad_heads(w, heads, split):
    if split:
        w = w.reshape(w.shape[:-1] + (heads, 2, LANES // 2))[..., :HALF]
    else:
        w = w.reshape(w.shape[:-1] + (heads, LANES))[..., :HD]
    return w.reshape(w.shape[: w.ndim - (3 if split else 2)] + (heads * HD,))


def rope_tables(ctx, r):
    frequency = THETA ** (-(jnp.arange(HALF, dtype=F32) * (2.0 / HD)))
    angles = jnp.arange(ctx * r, dtype=jnp.int32).astype(F32)[:, None] * frequency[None, :]
    pad = ((0, 0), (0, LANES // 2 - HALF))
    cos, sin = jnp.pad(jnp.cos(angles), pad), jnp.pad(jnp.sin(angles), pad)
    cos = jnp.concatenate([cos, cos], axis=1).reshape(ctx, r, LANES)
    sin = jnp.concatenate([-sin, sin], axis=1).reshape(ctx, r, LANES)
    return cos, sin


def per_device(
    inputs, segments, cotangent, w_query, w_key, w_value, w_out, w_gate, w_up, w_down, gain_attn, gain_ffn
):
    z = Sizes(lax.axis_size("dp"), lax.axis_size("ctx"))
    dp, ctx, outer, inner, ys = z.dp, z.ctx, z.outer, z.inner, z.ys
    m, r, d = inputs.shape
    rows = w_query.shape[0]
    frows, ff = w_down.shape[0], w_gate.shape[1]
    f = ff // ctx
    hc, kvc = H // ctx, KV // ctx
    width = (hc + 2 * kvc) * LANES
    c = lax.axis_index("ctx")
    di = lax.axis_index("dp")
    oi, ii = di // inner, di % inner
    yi, ki = c // 2, c % 2
    dyn = lambda a, at, axis: lax.dynamic_index_in_dim(a, at, axis, keepdims=False)

    pack_qkv = jnp.concatenate(
        [
            pad_heads(w_query, H, True).reshape(rows, ctx, hc * LANES),
            pad_heads(w_key, KV, True).reshape(rows, ctx, kvc * LANES),
            pad_heads(w_value, KV, False).reshape(rows, ctx, kvc * LANES),
        ],
        axis=2,
    ).transpose(1, 0, 2)
    by_rank = lambda w: w.reshape(rows, dp, ctx, frows).transpose(2, 0, 1, 3).reshape(ctx, rows, f)
    pack_gu = jnp.concatenate([by_rank(w_gate), by_rank(w_up)], axis=2)
    gains = jnp.stack([gain_attn, gain_ffn]).astype(F32)
    gains = jnp.pad(gains, ((0, 6), (0, LANES - rows)))

    def first_script(link, ins, outs, scratch):
        x, seg, qkv, gain = ins
        x_all, seg_all, g_qkv, g_gain = outs
        (hold,) = scratch
        load = pltpu.make_async_copy(x, hold, link.sems[2].at[15])
        load.start()
        link.keep(qkv.at[link.c], g_qkv.at[link.d, link.c])
        link.keep(gain, g_gain.at[link.d, link.c])
        link.keep(seg, seg_all.at[link.c])
        a2a = exchange_ctx(link, qkv, lambda s: g_qkv.at[link.d, s])
        a2a += [link.put(gain, g_gain.at[link.d, link.c], (link.d, p)) for p in link.ctx_peers()]
        for p in link.ctx_peers():
            link.put(seg, seg_all.at[link.c], (link.d, p))
        ways_x = gather_ctx_start(link, x, x_all)
        for copy in a2a:
            link.arrived(copy)
        for copy in link.local:
            copy.wait()
        link.local = []
        slots = (lambda s: g_qkv.at[s], lambda s: g_gain.at[s])
        ways = [gather_dp_start(link, slot) for slot in slots]
        load.wait()
        store = pltpu.make_async_copy(hold, x_all.at[link.c], link.sems[2].at[14])
        store.start()
        for slot, way in zip(slots, ways):
            gather_dp_forward(link, slot, way)
        gather_ctx_forward(link, x_all, ways_x)
        store.wait()

    x_all, seg_all, g_qkv, g_gain = communicate(
        z,
        "gather_first",
        1,
        first_script,
        (inputs, segments, pack_qkv, gains),
        (
            sds((ctx, m, r, d)),
            sds((ctx, m, r), jnp.int32),
            sds((dp, ctx, rows, width)),
            sds((dp, ctx, 8, LANES), F32),
        ),
        [pltpu.VMEM((m, r, d), BF)],
    )
    gain_a = g_gain[:, :, 0, :rows].reshape(1, d)
    gain_f = g_gain[:, :, 1, :rows].reshape(1, d)
    wqkv = g_qkv.reshape(d, width)
    cos, sin = rope_tables(ctx, r)
    qdoc = seg_all.reshape(ctx, m, r, 1)
    kdoc = seg_all.reshape(ctx, m, 1, r)

    normed_a, q, k, v = qkv_call(z, x_all, gain_a, wqkv, cos, sin, hc, kvc)
    att, lse = attend_call(z, q, k, v, qdoc, kdoc, hc, kvc)

    def second_script(link, ins, outs, scratch):
        att, wo, gu, wd, cot = ins
        att_all, g_out, g_gu, g_down, cot_all = outs
        (hold,) = scratch
        load = pltpu.make_async_copy(cot, hold, link.sems[2].at[15])
        load.start()
        link.keep(gu.at[link.c], g_gu.at[link.d, link.c])
        link.keep(wo, g_out.at[link.d, link.y, link.k])
        link.keep(wd, g_down.at[link.d])
        link.keep(att.at[link.c], att_all.at[link.c])
        exchange_ctx(link, att, lambda s: att_all.at[s])
        a2a = exchange_ctx(link, gu, lambda s: g_gu.at[link.d, s])
        for p in link.y_peers():
            a2a.append(link.put(wo, g_out.at[link.d, link.y, link.k], link.ctx_dev(p, link.k)))
        ways_c = gather_ctx_start(link, cot, cot_all)
        load.wait()
        store = pltpu.make_async_copy(hold, cot_all.at[link.c], link.sems[2].at[14])
        store.start()
        for copy in link.local:
            copy.wait()
        link.local = []
        slots = [
            lambda s: g_down.at[s],
            lambda s: g_gu.at[s],
            lambda s: g_out.at[s, :, link.k],
        ]
        ways = [gather_dp_start(link, slots[0])]
        for copy in a2a:
            link.arrived(copy)
        ways += [gather_dp_start(link, slot) for slot in slots[1:]]
        gather_ctx_forward(link, cot_all, ways_c)
        done = 0
        for slot, way in zip(slots, ways):
            gather_dp_forward(link, slot, way)
        for copy in list(link.inflight):
            link.arrived(copy)
        mine = g_out.at[:, :, link.k]
        link.put(mine, mine, link.ctx_dev(link.y, 1 - link.k))
        store.wait()

    att_all, g_out, g_gu, g_down, cot_all = communicate(
        z,
        "gather_second",
        2,
        second_script,
        (att, w_out, pack_gu, w_down, cotangent),
        (
            sds(att.shape),
            sds((dp, ys, 2, rows, d)),
            sds((dp, ctx, rows, 2 * f)),
            sds((dp, frows, d)),
            sds((ctx, m, r, d)),
        ),
        [pltpu.VMEM((m, r, d), BF)],
    )
    wo = g_out.reshape(d, d)
    wgu = g_gu.reshape(d, 2 * f)
    wd = g_down.reshape(f, d)

    att_rows = att_all.transpose(1, 2, 0, 3).reshape(m * r, H * HD)
    residual = inputs.astype(F32)
    mid = residual + dot_nn(att_rows, wo).reshape(m, r, d)
    scale_f = lax.rsqrt(jnp.mean(mid * mid, axis=-1, keepdims=True) + EPS)
    normed = (mid * scale_f * gain_f).astype(BF)

    def third_script(link, ins, outs, scratch):
        (x,), (x_all,), (hold,) = ins, outs, scratch
        load = pltpu.make_async_copy(x, hold, link.sems[2].at[15])
        load.start()
        ways = gather_ctx_start(link, x, x_all)
        load.wait()
        store = pltpu.make_async_copy(hold, x_all.at[link.c], link.sems[2].at[14])
        store.start()
        gather_ctx_forward(link, x_all, ways)
        store.wait()

    (normed_all,) = communicate(
        z, "gather_third", 3, third_script, (normed,), (sds((ctx, m, r, d)),), [pltpu.VMEM((m, r, d), BF)]
    )

    hidden, dgu, out_part, dn_part = mlp_call(z, normed_all, cot_all, wgu, wd)

    flat = lambda a: a.reshape(ctx * m * r, a.shape[-1])
    part_down = dot_tn(flat(hidden), flat(cot_all)).astype(BF).reshape(outer, inner, frows, d)
    part_gu = dot_tn(flat(normed_all), flat(dgu)).astype(BF).reshape(outer, inner, ctx, rows, 2 * f)

    halves = lambda a: a.reshape((ys, 2) + a.shape[1:])
    out_part, dn_part = halves(out_part), halves(dn_part)
    shape_y = (ys, m, r, d)

    def core_script(link, ins, outs, scratch):
        for src, dst in zip(ins, outs):
            scatter_core(link, src, dst)

    def y_script(link, ins, outs, scratch):
        for src, dst in zip(ins, outs):
            scatter_y(link, src, dst)

    dn_in, out_in = communicate(
        z, "reduce_core", 4, core_script, (dn_part, out_part), (sds(shape_y), sds(shape_y))
    )
    pair = lambda part, got: (dyn(part, ki, 1).astype(F32) + got.astype(F32)).astype(BF)
    dn_pair, out_pair = pair(dn_part, dn_in), pair(out_part, out_in)
    shape_y = (ys - 1, m, r, d)
    dn_in, out_in = communicate(
        z, "reduce_y", 5, y_script, (dn_pair, out_pair), (sds(shape_y), sds(shape_y))
    )
    total = lambda part, got, at: dyn(part, at, 0).astype(F32) + jnp.sum(got.astype(F32), axis=0)
    d_normed = total(dn_pair, dn_in, yi)
    outputs = mid + total(out_pair, out_in, yi)

    grad_gain_f = jnp.sum(d_normed * mid * scale_f, axis=(0, 1))
    cot32 = cotangent.astype(F32)
    e = d_normed * gain_f
    d_mid = cot32 + (
        scale_f * e - mid * (scale_f * scale_f * scale_f) * jnp.mean(e * mid, axis=-1, keepdims=True)
    )
    d_mid_low = d_mid.astype(BF).reshape(m * r, d)
    d_att = dot_nt(d_mid_low, wo).astype(BF)
    d_att = d_att.reshape(m, r, ctx, hc * HD).transpose(2, 0, 1, 3)
    part_out = dot_tn(att_rows, d_mid_low).astype(BF).reshape(dp, ys, 2, rows, d)

    def fourth_script(link, ins, outs, scratch):
        link.keep(ins[0].at[link.c], outs[0].at[link.c])
        exchange_ctx(link, ins[0], lambda s: outs[0].at[s])
        link.put(ins[1].at[:, :, 1 - link.k], outs[1], link.ctx_dev(link.y, 1 - link.k))

    d_att_all, po_in = communicate(
        z,
        "exchange_back",
        6,
        fourth_script,
        (d_att, part_out),
        (sds(d_att.shape), sds((dp, ys, rows, d))),
    )
    po_pair = (dyn(part_out, ki, 2).astype(F32) + po_in.astype(F32)).astype(BF)
    po_pair = po_pair.transpose(1, 0, 2, 3)

    dqkv = attend_back_call(z, q, k, v, qdoc, kdoc, att, d_att_all, lse, cos, sin, hc, kvc)
    part_qkv = dot_tn(flat(normed_a), flat(dqkv)).astype(BF).reshape(outer, inner, ctx, rows, width)
    da_part = halves(dot_nt(flat(dqkv), wqkv).astype(BF).reshape(ctx, m, r, d))

    def fifth_script(link, ins, outs, scratch):
        scatter_core(link, ins[0], outs[0])
        scatter_y(link, ins[1], outs[1])
        for n in (2, 3, 4):
            scatter_inner(link, ins[n], outs[n])

    da_in, po_y, down_in, gu_in, qkv_in = communicate(
        z,
        "reduce_inner",
        7,
        fifth_script,
        (da_part, po_pair, part_down, part_gu, part_qkv),
        (
            sds((ys, m, r, d)),
            sds((ys - 1, dp, rows, d)),
            sds((inner - 1, outer, frows, d)),
            sds((inner - 1, outer, ctx, rows, 2 * f)),
            sds((inner - 1, outer, ctx, rows, width)),
        ),
    )
    da_pair = pair(da_part, da_in)
    po_quarter = total(po_pair, po_y, yi).astype(BF).reshape(outer, inner, rows, d)
    column = lambda part, got: (dyn(part, ii, 1).astype(F32) + jnp.sum(got.astype(F32), axis=0)).astype(BF)
    down_col, gu_col, qkv_col = column(part_down, down_in), column(part_gu, gu_in), column(part_qkv, qkv_in)

    def sixth_script(link, ins, outs, scratch):
        scatter_y(link, ins[0], outs[0])
        scatter_inner(link, ins[1], outs[1])
        for n in (2, 3, 4):
            scatter_outer(link, ins[n], outs[n])

    da_in, po_in, down_in, gu_in, qkv_in = communicate(
        z,
        "reduce_outer",
        8,
        sixth_script,
        (da_pair, po_quarter, down_col, gu_col, qkv_col),
        (
            sds((ys - 1, m, r, d)),
            sds((inner - 1, outer, rows, d)),
            sds((outer - 1, frows, d)),
            sds((outer - 1, ctx, rows, 2 * f)),
            sds((outer - 1, ctx, rows, width)),
        ),
    )
    d_normed_a = total(da_pair, da_in, yi)
    scale_a = lax.rsqrt(jnp.mean(residual * residual, axis=-1, keepdims=True) + EPS)
    grad_gain_a = jnp.sum(d_normed_a * residual * scale_a, axis=(0, 1))
    e = d_normed_a * gain_a
    input_grad = d_mid + (
        scale_a * e - residual * (scale_a * scale_a * scale_a) * jnp.mean(e * residual, axis=-1, keepdims=True)
    )
    grad_down = total(down_col, down_in, oi)
    gu_mine = total(gu_col, gu_in, oi).astype(BF)
    qkv_mine = total(qkv_col, qkv_in, oi).astype(BF)
    po_col = column(po_quarter, po_in)

    def seventh_script(link, ins, outs, scratch):
        for n in (0, 1):
            link.keep(ins[n].at[link.c], outs[n].at[link.c])
            exchange_ctx(link, ins[n], lambda s: outs[n].at[s])
        scatter_outer(link, ins[2], outs[2])

    gu_all, qkv_all, po_in = communicate(
        z,
        "reduce_last",
        9,
        seventh_script,
        (gu_mine, qkv_mine, po_col),
        (sds((ctx, rows, 2 * f)), sds((ctx, rows, width)), sds((outer - 1, rows, d))),
    )
    grad_out = total(po_col, po_in, oi)
    gu_all = gu_all.astype(F32)
    spread = lambda a: a.reshape(ctx, rows, dp, frows).transpose(1, 2, 0, 3).reshape(rows, ff)
    grad_gate, grad_up = spread(gu_all[:, :, :f]), spread(gu_all[:, :, f:])
    qkv_all = qkv_all.astype(F32)
    cols = lambda a, heads, split: unpad_heads(a, heads, split).transpose(1, 0, 2).reshape(rows, ctx * heads * HD)
    grad_query = cols(qkv_all[:, :, : hc * LANES], hc, True)
    grad_key = cols(qkv_all[:, :, hc * LANES : (hc + kvc) * LANES], kvc, True)
    grad_value = cols(qkv_all[:, :, (hc + kvc) * LANES :], kvc, False)
    both = lax.psum_scatter(
        jnp.stack([grad_gain_a, grad_gain_f], axis=1), ("dp", "ctx"), scatter_dimension=0, tiled=True
    )
    return (
        outputs,
        input_grad,
        grad_query,
        grad_key,
        grad_value,
        grad_out,
        grad_gate,
        grad_up,
        grad_down,
        both[:, 0],
        both[:, 1],
    )


def solution(mesh):
    rows, vec, tok = P(("dp", "ctx"), None), P(("dp", "ctx")), P("dp", "ctx", None)
    return jax.shard_map(
        per_device,
        mesh=mesh,
        in_specs=(tok, P("dp", "ctx"), tok) + (rows,) * 7 + (vec, vec),
        out_specs=(tok, tok) + (rows,) * 7 + (vec, vec),
        check_vma=False,
    )
```

time: 2090 us -> 1080 us (0.52)
  waiting for transfers between devices: 1490 us -> 41.3 us
  Pallas kernels: 0 us -> 843 us
  matrix products: 366 us -> 64.2 us
  starting transfers between devices: 56.1 us -> 0.04 us
  blocking collectives: 48 us -> 0 us
    all_to_all x9 -> x0, waiting for transfers between devices: 991 us -> none  [the longest x1 247 us: per_device(): lax.all_to_all(owned[4].astype(jnp.bfloat16), ('dp', 'ctx'), split_axis=0...]
    pallas_call x0 -> x13, Pallas kernels: none -> 843 us  [the longest x9 726 us: communicate(): pl.pallas_call(kernel, name=name, out_shape=list(outs), in_specs=[hbm] *...]
    all_gather x11 -> x0, waiting for transfers between devices: 451 us -> none  [the longest x1 87.2 us: per_device(): lax.all_gather(w_down, ('dp', 'ctx'), axis=0, tiled=True)]
    dot_general x54 -> x7, matrix products: 366 us -> 64.2 us  [the longest x4 45.5 us: dot_tn(): lax.dot_general(a, b, (((0,), (0,)), ((), ())), preferred_element_type=F32)]
    all_to_all x9 -> x0, starting transfers between devices: 55.3 us -> none  [the longest x1 11.6 us: per_device(): lax.all_to_all(owned[4].astype(jnp.bfloat16), ('dp', 'ctx'), split_axis=0...]
    reduce_sum x12 -> x7, other arithmetic: 61.3 us -> 16 us  [the longest x4 7.44 us: per_device(): jnp.sum(got.astype(F32), axis=0)]
    unnamed x1 -> x0, blocking collectives: 42.1 us -> none
    reduce_scatter x4 -> x0, waiting for transfers between devices: 39.2 us -> none  [the longest x2 39.1 us: per_device(): lax.psum_scatter(d_value_terms.reshape(length, KV * HD).astype(jnp.bfloat...]
  transfers between devices with their start and end apart: 24 -> 1, of which waited for: 21 -> 1; matrix products, arithmetic and copies ran while one was open for 18% -> 3% of each run, Pallas kernels for 0% -> 2%
where the time goes in v1:
time: 1080 us
  Pallas kernels  843 us (78%)
  other arithmetic  69.2 us (6%)
  matrix products  64.2 us (6%)
  local copies, waits for them, and re-layouts  45.4 us (4%)
  waiting for transfers between devices  41.3 us (4%)
  between operations  15.3 us (1%)
    pallas_call x9, Pallas kernels, communicate(): pl.pallas_call(kernel, name=name, out_shape=list(outs), in_specs=[hbm] *...  726 us
    pallas_call x1, Pallas kernels, mlp_call(): pl.pallas_call(mlp_kernel, name='mlp', grid=(ctx, m), in_specs=[pl.BlockS...  48.6 us
    dot_general x4, matrix products, dot_tn(): lax.dot_general(a, b, (((0,), (0,)), ((), ())), preferred_element_type=F32)  45.5 us
    unnamed x2, waiting for transfers between devices  41.3 us
    pallas_call x1, Pallas kernels, attend_back_call(): pl.pallas_call(functools.partial(attend_back_kernel, hc, kvc, ctx), name=...  32.1 us
    pallas_call x1, Pallas kernels, attend_call(): pl.pallas_call(functools.partial(attend_kernel, hc, kvc, ctx), name='atte...  21.6 us
  transfers between devices with their start and end apart: 1, of which 1 were waited for; matrix products, arithmetic and copies ran while one was open for 3% of the time, Pallas kernels for 2%

profile of v1, /device:TPU:0, one launch (start us, length us, event | category | flops | bytes accessed | tf_op | source)
XLA Modules:
  0.0 1078.6 jit_solution(16068128776062133568)
XLA Ops:
  7.3 1.8 fusion.5
  9.2 1.0 reshape.245
  10.3 1.1 reshape.244
  14.0 1.9 multiply_sine_fusion
  16.0 1.0 pad_maximum_fusion.1
  18.5 62.2 %gather_first.1 = (bf16[4,2,256,1536]{3,2,1,0:T(8,128)(2,1)}, s32[4,2,256]{2,1,0:T(2,128)}, bf16[8,4,48,1024]{3,2,1,0:T(8,128)(2,1)}, f32[8,4,8,128]{3,2,1,0:T(8,128)}) custom-call(bf16[2,256,1536]{2,1,0:T(8,128)(2,1)} %refs_0_.1, s32[2,256]{1,0:T(2,128)} %refs_1_.2, bf16[4,48,1024]{2,1,0:T(8,128)(2,1)} %maximum_bitcast_fusion.refs_2_, f32[8,128]{1,0:T(8,128)} %fusion.26.refs_3_), custom_call_target="tpu_custom_call" | custom-call | tf_op jit(solution)/shard_map/gather_first/pallas_call | solution.py:143
  80.7 1.3 reshape.250.kdoc_ref
  82.0 1.1 slice_reduce_fusion
  83.8 2.0 copy.75.qdoc_ref
  86.8 1.0 pad_maximum_fusion.2
  87.8 14.5 %qkv.1 = (bf16[4,2,256,1536]{3,2,1,0:T(8,128)(2,1)}, bf16[4,2,256,512]{3,2,1,0:T(8,128)(2,1)}, bf16[4,2,256,256]{3,2,1,0:T(8,128)(2,1)}, bf16[4,2,256,256]{3,2,1,0:T(8,128)(2,1)}) custom-call(bf16[4,2,256,1536]{3,2,1,0:T(8,128)(2,1)} %get-tuple-element.49.x_ref, f32[1,1536]{1,0:T(1,128)} %reshape_squeeze.3.gain_ref, bf16[1536,1024]{1,0:T(8,128)(2,1)} %bitcast.227, ...), custom_call_target="tpu_custom_call" | custom-call | tf_op jit(solution)/shard_map/qkv/pallas_call | solution.py:249
  102.3 21.6 %attend.1 = (bf16[4,2,256,384]{3,2,1,0:T(8,128)(2,1)}, f32[4,2,256,128]{3,2,1,0:T(8,128)}) custom-call(bf16[4,2,256,512]{3,2,1,0:T(8,128)(2,1)} %get-tuple-element.52.q_ref, bf16[4,2,256,256]{3,2,1,0:T(8,128)(2,1)} %get-tuple-element.53.k_ref, bf16[4,2,256,256]{3,2,1,0:T(8,128)(2,1)} %get-tuple-element.54.v_ref, s32[4,2,256,1]{3,2,1,0:T(8,128)} %copy.75.qdoc_ref, ...), custom_call_target="tpu_custom_call" | custom-call | tf_op jit(solution)/shard_map/attend/pallas_call | solution.py:320
  124.0 201.5 %gather_second.1 = (bf16[4,2,256,384]{3,2,1,0:T(8,128)(2,1)}, bf16[8,2,2,48,1536]{4,3,2,1,0:T(8,128)(2,1)}, bf16[8,4,48,2048]{3,2,1,0:T(8,128)(2,1)}, bf16[8,128...) custom-call(bf16[4,2,256,384]{3,2,1,0:T(8,128)(2,1)} %get-tuple-element.56.refs_0_.o_ref, bf16[48,1536]{1,0:T(8,128)(2,1)} %refs_1_.3, ...), custom_call_target="tpu_custom_call" | custom-call | tf_op jit(solution)/shard_map/gather_second/pallas_call | solution.py:143
  325.5 2.7 copy.83
  328.2 1.6 copy.78
  330.0 1.4 copy.120
  331.9 5.7 multiply_reduce_fusion.1
  337.7 1.5 multiply_convert_fusion.refs_0_
  339.1 58.7 %gather_third.1.x_ref = bf16[4,2,256,1536]{3,2,1,0:T(8,128)(2,1)} custom-call(bf16[2,256,1536]{2,1,0:T(8,128)(2,1)} %multiply_convert_fusion.refs_0_), custom_call_target="tpu_custom_call" | custom-call | tf_op jit(solution)/shard_map/gather_third/pallas_call | solution.py:143
  397.9 48.6 %mlp.1 = (bf16[4,2,256,1024]{3,2,1,0:T(8,128)(2,1)}, bf16[4,2,256,2048]{3,2,1,0:T(8,128)(2,1)}, bf16[4,2,256,1536]{3,2,1,0:T(8,128)(2,1)}, bf16[4,2,256,1536]{3,2,1,0:T(8,128)(2,1)}) custom-call(bf16[4,2,256,1536]{3,2,1,0:T(8,128)(2,1)} %gather_third.1.x_ref, bf16[4,2,256,1536]{3,2,1,0:T(8,128)(2,1)} %get-tuple-element.59.cot_ref, ...), custom_call_target="tpu_custom_call" | custom-call | tf_op jit(solution)/shard_map/mlp/pallas_call | solution.py:441
  446.5 19.2 %bitcast_convert_fusion = bf16[1536,2048]{1,0:T(8,128)(2,1)} fusion(bf16[4,2,256,1536]{3,2,1,0:T(8,128)(2,1)} %gather_third.1.x_ref, bf16[4,2,256,2048]{3,2,1,0:T(8,128)(2,1)} %get-tuple-element.72), kind=kOutput, calls=%fused_computation | convolution fusion | flops 12888047616 | bytes 20971520 | tf_op jit(solution)/shard_map/dot_general | solution.py:40
  465.7 10.5 bitcast_convert_fusion.2
  476.3 13.0 %reduce_core.1 = (bf16[2,2,256,1536]{3,2,1,0:T(8,128)(2,1)}, bf16[2,2,256,1536]{3,2,1,0:T(8,128)(2,1)}) custom-call(bf16[2,2,2,256,1536]{4,3,2,1,0:T(8,128)(2,1)} %bitcast.192, bf16[2,2,2,256,1536]{4,3,2,1,0:T(8,128)(2,1)} %bitcast.190), custom_call_target="tpu_custom_call" | custom-call | tf_op jit(solution)/shard_map/reduce_core/pallas_call | solution.py:143
  489.3 9.3 fusion.2
  498.6 73.8 %reduce_y.1 = (bf16[1,2,256,1536]{3,2,1,0:T(8,128)(2,1)}, bf16[1,2,256,1536]{3,2,1,0:T(8,128)(2,1)}) custom-call(bf16[2,2,256,1536]{3,2,1,0:T(8,128)(2,1)} %get-tuple-element.112.refs_0_, bf16[2,2,256,1536]{3,2,1,0:T(8,128)(2,1)} %get-tuple-element.113.refs_1_), custom_call_target="tpu_custom_call" | custom-call | tf_op jit(solution)/shard_map/reduce_y/pallas_call | solution.py:143
  572.4 3.1 fusion.15
  576.2 1.2 fusion.27
  577.3 1.2 copy-done.25
  578.5 3.8 convolution_convert_fusion.2
  582.3 3.9 reshape.261
  586.3 2.9 copy.137
  589.2 4.4 convolution_convert_fusion.1
  593.6 19.6 %exchange_back.1 = (bf16[4,2,256,384]{3,2,1,0:T(8,128)(2,1)}, bf16[8,2,48,1536]{3,2,1,0:T(8,128)(2,1)}) custom-call(bf16[4,2,256,384]{3,2,1,0:T(8,128)(2,1)} %bitcast.209, bf16[8,2,2,48,1536]{4,3,2,1,0:T(8,128)(2,1)} %bitcast.200), custom_call_target="tpu_custom_call" | custom-call | tf_op jit(solution)/shard_map/exchange_back/pallas_call | solution.py:143
  613.2 4.5 fusion.4
  617.7 32.1 %attend_back.1 = bf16[4,2,256,1024]{3,2,1,0:T(8,128)(2,1)} custom-call(bf16[4,2,256,512]{3,2,1,0:T(8,128)(2,1)} %get-tuple-element.52.q_ref, bf16[4,2,256,256]{3,2,1,0:T(8,128)(2,1)} %get-tuple-element.53.k_ref, bf16[4,2,256,256]{3,2,1,0:T(8,128)(2,1)} %get-tuple-element.54.v_ref, s32[4,2,256,1]{3,2,1,0:T(8,128)} %copy.75.qdoc_ref, ...), custom_call_target="tpu_custom_call" | custom-call | tf_op jit(solution)/shard_map/attend_back/pallas_call | solution.py:392
  649.8 11.4 %bitcast_convert_fusion.1 = bf16[1536,1024]{1,0:T(8,128)(2,1)} fusion(bf16[4,2,256,1536]{3,2,1,0:T(8,128)(2,1)} %get-tuple-element.73, bf16[4,2,256,1024]{3,2,1,0:T(8,128)(2,1)} %attend_back.1), kind=kOutput, calls=%fused_computation.5 | convolution fusion | flops 6444023808 | bytes 13631488 | tf_op jit(solution)/shard_map/dot_general | solution.py:40
  661.2 9.2 convolution_convert_fusion
  670.4 1.1 constant_dynamic-slice_fusion
  671.5 141.6 %reduce_inner.1 = (bf16[2,2,256,1536]{3,2,1,0:T(8,128)(2,1)}, bf16[1,8,48,1536]{3,2,1,0:T(8,128)(2,1)}, bf16[1,4,128,1536]{3,2,1,0:T(8,128)(2,1)}, bf16[1,4,4,48...) custom-call(bf16[2,2,2,256,1536]{4,3,2,1,0:T(8,128)(2,1)} %bitcast.196, bf16[2,8,48,1536]{3,2,1,0:T(8,128)(2,1)} %bitcast.189, ...), custom_call_target="tpu_custom_call" | custom-call | tf_op jit(solution)/shard_map/reduce_inner/pallas_call | solution.py:143
  813.1 3.9 fusion.12.refs_4_
  817.1 5.1 fusion.refs_3_
  822.2 1.6 fusion.13.refs_2_
  824.6 2.6 fusion.1.refs_0_
  827.5 1.0 copy-done.10
  828.6 1.1 copy.96.refs_1_
  829.7 132.5 %reduce_outer.1 = (bf16[1,2,256,1536]{3,2,1,0:T(8,128)(2,1)}, bf16[1,4,48,1536]{3,2,1,0:T(8,128)(2,1)}, bf16[3,128,1536]{2,1,0:T(8,128)(2,1)}, bf16[3,4,48,2048]{3,2,1,0:T(8,128)(2,1)}, bf16[3,4,48,1024]{3,2,1,0:T(8,128)(2,1)}) custom-call(bf16[2,2,256,1536]{3,2,1,0:T(8,128)(2,1)} %fusion.1.refs_0_, bf16[4,2,48,1536]{3,2,1,0:T(8,128)(2,1)} %copy.96.refs_1_, ...), custom_call_target="tpu_custom_call" | custom-call | tf_op jit(solution)/shard_map/reduce_outer/pallas_call | solution.py:143
  962.2 3.6 fusion.11
  965.8 1.2 copy.109
  967.1 2.3 fusion.18.refs_2_
  969.4 3.5 convert_reduce_fusion
  972.9 1.1 convert_reduce_fusion.2
  974.0 2.7 fusion.17.refs_0_
  976.7 1.8 fusion.19.refs_1_
  978.5 23.2 %reduce_last.1 = (bf16[4,48,2048]{2,1,0:T(8,128)(2,1)}, bf16[4,48,1024]{2,1,0:T(8,128)(2,1)}, bf16[3,48,1536]{2,1,0:T(8,128)(2,1)}) custom-call(bf16[4,48,2048]{2,1,0:T(8,128)(2,1)} %fusion.17.refs_0_, bf16[4,48,1024]{2,1,0:T(8,128)(2,1)} %fusion.19.refs_1_, bf16[4,48,1536]{2,1,0:T(8,128)(2,1)} %fusion.18.refs_2_), custom_call_target="tpu_custom_call" | custom-call | tf_op jit(solution)/shard_map/reduce_last/pallas_call | solution.py:143
  1001.7 1.2 convert_reduce_fusion.3
  1002.9 1.7 convert_add_fusion.14
  1004.6 1.7 convert_reduce_fusion.1
  1006.3 2.1 convert_add_fusion.12
  1008.4 1.4 fusion.28
  1013.0 6.2 fusion.8
  1022.6 1.0 reshape.269
  1024.9 1.2 reshape.280
  1026.6 1.2 reshape.278
  1027.8 41.3 %reduce-scatter.4.cloned.1.call-done = f32[48,2]{1,0:T(8,128)} async-done(((f32[1536,2]{1,0:T(8,128)}), f32[48,2]{1,0:T(8,128)}) %reduce-scatter.4.cloned.1.call-update) | async-done | bytes 400
  (136 shorter events, 18.7 us)
Async XLA Ops:
  7.2 4.7 copy-start.31
  7.2 5.8 copy-start.29
  7.2 1062.0 %reduce-scatter.4.cloned.1.call-start = ((), (), s32[]{:S(2)}) async-start(), calls=%async_computation.1 | async-start | bytes 811008
  10.2 3.3 copy-start.30
  13.8 3.3 copy-start.32
  13.8 3.3 copy-start.33
  325.5 2.8 copy-start.12
  330.0 1.9 copy-start.13
  446.5 19.2 %copy-start.34 = (bf16[4,2,256,1024]{3,2,1,0:T(8,128)(2,1)S(1)}, bf16[4,2,256,1024]{3,2,1,0:T(8,128)(2,1)}, u32[]{:S(2)}) copy-start(bf16[4,2,256,1024]{3,2,1,0:T(8,128)(2,1)} %get-tuple-element.71) | copy-start | bytes 12582916
  572.4 3.2 copy-start.1
  572.4 3.3 copy-start.6
  572.4 3.8 copy-start.8
  572.4 6.1 slice-start.2
  576.2 2.4 slice-start.3
  577.3 1.2 copy-start.25
  586.3 2.9 copy-start.23
  586.3 2.9 copy-start.26
  649.8 11.4 %copy-start.15 = (bf16[4,2,256,1024]{3,2,1,0:T(8,128)(2,1)S(1)}, bf16[4,2,256,1024]{3,2,1,0:T(8,128)(2,1)}, u32[]{:S(2)}) copy-start(bf16[4,2,256,1024]{3,2,1,0:T(8,128)(2,1)} %attend_back.1) | copy-start | bytes 12582916
  649.8 11.4 %copy-start.19 = (bf16[8,4,48,1024]{3,2,1,0:T(8,128)(2,1)S(1)}, bf16[8,4,48,1024]{3,2,1,0:T(8,128)(2,1)}, u32[]{:S(2)}) copy-start(bf16[8,4,48,1024]{3,2,1,0:T(8,128)(2,1)} %get-tuple-element.51) | copy-start | bytes 9437188
  661.2 9.2 copy-start.5
  813.1 3.9 copy-start.21
  813.1 10.7 slice-start
  817.0 5.1 copy-start.11
  817.0 5.1 copy-start.22
  817.0 6.7 slice-start.1
  822.2 2.5 copy-start.20
  824.6 2.6 copy-start.14
  824.6 2.6 copy-start.27
  827.5 1.0 copy-start.10
  967.1 5.8 copy-start.28
  974.0 2.7 copy-start.18
  1001.7 10.3 copy-start.9
  1004.6 7.4 copy-start.7
  1006.3 5.8 copy-start.4
  1008.4 3.6 copy-start.3
  1009.8 2.2 copy-start
  1009.9 3.1 copy-start.2
  1013.0 6.3 copy-start.24
  1019.6 4.8 copy-start.16
  1022.0 4.1 copy-start.17
Sparse Core Ops, SparseCore 0:
  967.2 101.9 reduce-scatter.3

commit v2 on v1

--- a/solution.py
+++ b/solution.py
@@ -127,8 +127,12 @@
     landed = None
 
 
-def communicate(z, name, cid, script, ins, outs, scratch=()):
+def communicate(z, name, cid, script, ins, outs, scratch=(), filled=()):
+    filled = tuple(filled)
+    outs = [sds(a.shape, a.dtype) for a in filled] + list(outs)
+    ins = tuple(ins) + filled
     n_in, n_out = len(ins), len(outs)
+    aliases = {n_in - len(filled) + n: n for n in range(len(filled))}
 
     def kernel(*refs):
         in_refs, out_refs = refs[:n_in], refs[n_in : n_in + n_out]
@@ -146,6 +150,7 @@
         out_shape=list(outs),
         in_specs=[hbm] * n_in,
         out_specs=[hbm] * n_out,
+        input_output_aliases=aliases,
         scratch_shapes=[
             pltpu.SemaphoreType.DMA((64,)),
             pltpu.SemaphoreType.DMA((64,)),
@@ -219,6 +224,106 @@
     for j in range(1, link.z.ys):
         to = lax.rem(link.y + j, link.z.ys)
         link.put(src.at[to], dst.at[j - 1], link.ctx_dev(to, link.k))
+
+
+class Cargo(Link):
+    def put(self, src, dst, device):
+        n = self.sent
+        self.sent += 1
+        copy = pltpu.make_async_remote_copy(
+            src_ref=src,
+            dst_ref=dst,
+            send_sem=self.sems[0].at[n],
+            recv_sem=self.sems[1].at[n],
+            device_id=device,
+            device_id_type=MESH,
+        )
+        self.inflight.append(copy)
+        return copy
+
+
+def fused_call(z, name, cid, body, grid, in_specs, out_specs, out_shape, args, script, moved, new=(), filled=(), scratch=()):
+    filled, moved = tuple(filled), tuple(moved)
+    n_arg, n_moved, n_fill = len(args), len(moved), len(filled)
+    n_cargo = n_fill + len(new)
+    n_out = n_cargo + len(out_shape)
+    steps = 1
+    for extent in grid:
+        steps *= extent
+
+    def kernel(*refs):
+        step = 0
+        for axis, extent in enumerate(grid):
+            step = step * extent + pl.program_id(axis)
+        n_in = n_arg + n_moved + n_fill
+        arg_refs, moved_refs = refs[:n_arg], refs[n_arg : n_arg + n_moved]
+        cargo_refs, out_refs = refs[n_in : n_in + n_cargo], refs[n_in + n_cargo : n_in + n_out]
+        send, recv = refs[n_in + n_out : n_in + n_out + 2]
+        cargo = Cargo(z, send, recv, None)
+        script(cargo, moved_refs, cargo_refs)
+
+        @pl.when(step == 0)
+        def _():
+            cargo.barrier()
+            for copy in cargo.inflight:
+                copy.start()
+
+        body(*arg_refs, *out_refs, *refs[n_in + n_out + 2 :])
+
+        @pl.when(step == steps - 1)
+        def _():
+            for copy in cargo.inflight:
+                copy.wait_recv()
+            for copy in cargo.inflight:
+                copy.wait_send()
+
+    hbm = pl.BlockSpec(memory_space=pltpu.HBM)
+    first = n_arg + n_moved
+    return pl.pallas_call(
+        kernel,
+        name=name,
+        grid=grid,
+        in_specs=list(in_specs) + [hbm] * (n_moved + n_fill),
+        out_specs=[hbm] * n_cargo + list(out_specs),
+        out_shape=[sds(a.shape, a.dtype) for a in filled] + list(new) + list(out_shape),
+        input_output_aliases={first + n: n for n in range(n_fill)},
+        scratch_shapes=[pltpu.SemaphoreType.DMA((32,)), pltpu.SemaphoreType.DMA((32,))] + list(scratch),
+        compiler_params=pltpu.CompilerParams(
+            collective_id=cid, has_side_effects=True, vmem_limit_bytes=VMEM_LIMIT
+        ),
+    )(*args, *moved, *filled)
+
+
+def own_outer(link, buf, js):
+    for j in js:
+        link.put(buf.at[link.d], buf.at[link.d], link.dp_dev(link.outer_to(j), link.i))
+
+
+def own_inner(link, buf):
+    for j in range(1, link.z.inner):
+        link.put(buf.at[link.d], buf.at[link.d], link.dp_dev(link.o, link.inner_to(j)))
+
+
+def pass_inner(link, buf, js):
+    for from_j in js:
+        slot = buf.at[link.outer_from(from_j) * link.z.inner + link.i]
+        for j in range(1, link.z.inner):
+            link.put(slot, slot, link.dp_dev(link.o, link.inner_to(j)))
+
+
+def pass_core(link, buf, parts):
+    for j in range(1, link.z.ys):
+        at = lax.rem(link.y + link.z.ys - j, link.z.ys) * 2 + link.k
+        for part in parts:
+            link.put(buf.at[at, part], buf.at[at, part], link.ctx_dev(link.y, 1 - link.k))
+
+
+def own_y(link, src, buf, parts):
+    for part in parts:
+        for j in range(1, link.z.ys):
+            to = lax.rem(link.y + j, link.z.ys)
+            link.put(src.at[part], buf.at[link.c, part], link.ctx_dev(to, link.k))
+        link.put(src.at[part], buf.at[link.c, part], link.ctx_dev(link.y, 1 - link.k))
 
 
 def rotated(u, cos, sin):
@@ -241,36 +346,42 @@
     v_ref[0, 0] = full[:, (hc + kvc) * LANES :].astype(BF)
 
 
-def qkv_call(z, x_all, gain, w, cos, sin, hc, kvc):
+def qkv_call(z, x_all, gain, w, cos, sin, hc, kvc, script, moved, new, filled):
     ctx, m, r, d = x_all.shape
     row = lambda s, b: (s, b, 0, 0)
     whole = lambda s, b: (0, 0)
     table = pl.BlockSpec((1, r, LANES), lambda s, b: (s, 0, 0))
-    return pl.pallas_call(
+    return fused_call(
+        z,
+        "qkv",
+        11,
         functools.partial(qkv_kernel, hc, kvc),
-        name="qkv",
-        grid=(ctx, m),
-        in_specs=[
+        (ctx, m),
+        [
             pl.BlockSpec((1, 1, r, d), row),
             pl.BlockSpec((1, d), whole),
             pl.BlockSpec(w.shape, whole, pipeline_mode=pl.Buffered(1)),
             table,
             table,
         ],
-        out_specs=[
+        [
             pl.BlockSpec((1, 1, r, d), row),
             pl.BlockSpec((1, 1, r, hc * LANES), row),
             pl.BlockSpec((1, 1, r, kvc * LANES), row),
             pl.BlockSpec((1, 1, r, kvc * LANES), row),
         ],
-        out_shape=[
+        [
             sds((ctx, m, r, d)),
             sds((ctx, m, r, hc * LANES)),
             sds((ctx, m, r, kvc * LANES)),
             sds((ctx, m, r, kvc * LANES)),
         ],
-        compiler_params=pltpu.CompilerParams(vmem_limit_bytes=VMEM_LIMIT),
-    )(x_all, gain, w, cos, sin)
+        (x_all, gain, w, cos, sin),
+        script,
+        moved,
+        new,
+        filled,
+    )
 
 
 def window_of(s, r, ctx):
@@ -313,30 +424,36 @@
     lse_ref[0, 0] = lse_all
 
 
-def attend_call(z, q, k, v, qdoc, kdoc, hc, kvc):
+def attend_call(z, q, k, v, qdoc, kdoc, hc, kvc, script, moved, new, filled):
     ctx, m, r, _ = q.shape
     row = lambda b, s: (s, b, 0, 0)
     seq = lambda b, s: (0, b, 0, 0)
-    return pl.pallas_call(
+    return fused_call(
+        z,
+        "attend",
+        12,
         functools.partial(attend_kernel, hc, kvc, ctx),
-        name="attend",
-        grid=(m, ctx),
-        in_specs=[
+        (m, ctx),
+        [
             pl.BlockSpec((1, 1, r, hc * LANES), row),
             pl.BlockSpec((ctx, 1, r, kvc * LANES), seq),
             pl.BlockSpec((ctx, 1, r, kvc * LANES), seq),
             pl.BlockSpec((1, 1, r, 1), row),
             pl.BlockSpec((ctx, 1, 1, r), seq),
         ],
-        out_specs=[pl.BlockSpec((1, 1, r, hc * HD), row), pl.BlockSpec((1, 1, r, LANES), row)],
-        out_shape=[sds((ctx, m, r, hc * HD)), sds((ctx, m, r, LANES), F32)],
-        compiler_params=pltpu.CompilerParams(vmem_limit_bytes=VMEM_LIMIT),
-    )(q, k, v, qdoc, kdoc)
+        [pl.BlockSpec((1, 1, r, hc * HD), row), pl.BlockSpec((1, 1, r, LANES), row)],
+        [sds((ctx, m, r, hc * HD)), sds((ctx, m, r, LANES), F32)],
+        (q, k, v, qdoc, kdoc),
+        script,
+        moved,
+        new,
+        filled,
+    )
 
 
 def attend_back_kernel(
     hc, kvc, ctx, q_ref, k_ref, v_ref, qdoc_ref, kdoc_ref, o_ref, do_ref, lse_ref, cos_ref, sin_ref,
-    out_ref, dk_acc, dv_acc,
+    dq_ref, dkv_ref, dk_acc, dv_acc,
 ):
     s = pl.program_id(1)
     r = q_ref.shape[2]
@@ -364,7 +481,7 @@
         d_probs = dot_nt(do, v)
         d_scores = (probs * (d_probs - delta) * HD ** (-0.5)).astype(BF)
         dq = dot_nn(d_scores, k)
-        out_ref[s, 0, :, h * LANES : (h + 1) * LANES] = rotated(dq, cos, -sin).astype(BF)
+        dq_ref[0, 0, :, h * LANES : (h + 1) * LANES] = rotated(dq, cos, -sin).astype(BF)
         dk = dot_tn(d_scores, q).reshape(blocks, r, LANES)
         dv = dot_tn(probs.astype(BF), do).reshape(blocks, r, LANES)
         here = slice(g * LANES, (g + 1) * LANES)
@@ -376,11 +493,11 @@
         for b in range(ctx):
             for g in range(kvc):
                 here = slice(g * LANES, (g + 1) * LANES)
-                at = (hc + g) * LANES
+                at = g * LANES
                 dk = rotated(dk_acc[b, :, here], cos_ref[b], -sin_ref[b])
-                out_ref[b, 0, :, at : at + LANES] = dk.astype(BF)
+                dkv_ref[b, 0, :, at : at + LANES] = dk.astype(BF)
                 at += kvc * LANES
-                out_ref[b, 0, :, at : at + LANES] = dv_acc[b, :, here].astype(BF)
+                dkv_ref[b, 0, :, at : at + LANES] = dv_acc[b, :, here].astype(BF)
 
 
 def attend_back_call(z, q, k, v, qdoc, kdoc, o, do, lse, cos, sin, hc, kvc):
@@ -388,7 +505,6 @@
     row = lambda b, s: (s, b, 0, 0)
     seq = lambda b, s: (0, b, 0, 0)
     table = pl.BlockSpec((ctx, r, LANES), lambda b, s: (0, 0, 0))
-    width = (hc + 2 * kvc) * LANES
     return pl.pallas_call(
         functools.partial(attend_back_kernel, hc, kvc, ctx),
         name="attend_back",
@@ -405,8 +521,11 @@
             table,
             table,
         ],
-        out_specs=pl.BlockSpec((ctx, 1, r, width), seq),
-        out_shape=sds((ctx, m, r, width)),
+        out_specs=[
+            pl.BlockSpec((1, 1, r, hc * LANES), row),
+            pl.BlockSpec((ctx, 1, r, 2 * kvc * LANES), seq),
+        ],
+        out_shape=[sds((ctx, m, r, hc * LANES)), sds((ctx, m, r, 2 * kvc * LANES))],
         scratch_shapes=[
             pltpu.VMEM((ctx, r, kvc * LANES), F32),
             pltpu.VMEM((ctx, r, kvc * LANES), F32),
@@ -415,11 +534,12 @@
     )(q, k, v, qdoc, kdoc, o, do, lse, cos, sin)
 
 
-def mlp_kernel(x_ref, cot_ref, gu_ref, down_ref, hid_ref, dgu_ref, out_ref, dn_ref):
+def mlp_kernel(
+    k_ref, x_ref, cot_ref, gate_ref, up_ref, down_ref,
+    hid_ref, dg_ref, du_ref, dn_other, dn_mine, out_other, out_mine,
+):
     x, cot = x_ref[0, 0], cot_ref[0, 0]
-    f = down_ref.shape[0]
-    both = dot_nn(x, gu_ref[...])
-    gate, up = both[:, :f], both[:, f:]
+    gate, up = dot_nn(x, gate_ref[...]), dot_nn(x, up_ref[...])
     d_hidden = dot_nt(cot, down_ref[...])
     sg = jax.nn.sigmoid(gate)
     act = gate * sg
@@ -427,41 +547,50 @@
     hid_ref[0, 0] = hidden
     d_gate = (d_hidden * up * sg * (1.0 + gate * (1.0 - sg))).astype(BF)
     d_up = (d_hidden * act).astype(BF)
-    dgu_ref[0, 0, :, :f] = d_gate
-    dgu_ref[0, 0, :, f:] = d_up
-    out_ref[0, 0] = dot_nn(hidden, down_ref[...]).astype(BF)
-    dn_ref[0, 0] = (dot_nt(d_gate, gu_ref[:, :f]) + dot_nt(d_up, gu_ref[:, f:])).astype(BF)
-
-
-def mlp_call(z, x, cot, gu, down):
+    dg_ref[0, 0] = d_gate
+    du_ref[0, 0] = d_up
+    out = dot_nn(hidden, down_ref[...]).astype(BF)
+    dn = (dot_nt(d_gate, gate_ref[...]) + dot_nt(d_up, up_ref[...])).astype(BF)
+
+    @pl.when(pl.program_id(0) == 0)
+    def _():
+        out_other[0, 0] = out
+        dn_other[0, 0] = dn
+
+    @pl.when(pl.program_id(0) == 1)
+    def _():
+        out_mine[0, 0] = out
+        dn_mine[0, 0] = dn
+
+
+def mlp_call(z, core, x, cot, gate, up, down):
     ctx, m, r, d = x.shape
     f = down.shape[0]
-    row = lambda s, b: (s, b, 0, 0)
-    whole = lambda s, b: (0, 0)
+    row = lambda a, y, b, k: (y * 2 + a * k[0] + (1 - a) * (1 - k[0]), b, 0, 0)
+    whole = lambda a, y, b, k: (0, 0)
+    other = lambda a, y, b, k: (y + a * (z.ys - 1 - y), b + a * (m - 1 - b), 0, 0)
+    mine = lambda a, y, b, k: (a * y, a * b, 0, 0)
+    block = lambda width, at: pl.BlockSpec((1, 1, r, width), at)
+    part = sds((z.ys, m, r, d))
     return pl.pallas_call(
         mlp_kernel,
         name="mlp",
-        grid=(ctx, m),
-        in_specs=[
-            pl.BlockSpec((1, 1, r, d), row),
-            pl.BlockSpec((1, 1, r, d), row),
-            pl.BlockSpec(gu.shape, whole, pipeline_mode=pl.Buffered(1)),
-            pl.BlockSpec(down.shape, whole, pipeline_mode=pl.Buffered(1)),
-        ],
-        out_specs=[
-            pl.BlockSpec((1, 1, r, f), row),
-            pl.BlockSpec((1, 1, r, 2 * f), row),
-            pl.BlockSpec((1, 1, r, d), row),
-            pl.BlockSpec((1, 1, r, d), row),
-        ],
-        out_shape=[
-            sds((ctx, m, r, f)),
-            sds((ctx, m, r, 2 * f)),
-            sds((ctx, m, r, d)),
-            sds((ctx, m, r, d)),
-        ],
+        grid_spec=pltpu.PrefetchScalarGridSpec(
+            num_scalar_prefetch=1,
+            grid=(2, z.ys, m),
+            in_specs=[
+                block(d, row),
+                block(d, row),
+                pl.BlockSpec(gate.shape, whole, pipeline_mode=pl.Buffered(1)),
+                pl.BlockSpec(up.shape, whole, pipeline_mode=pl.Buffered(1)),
+                pl.BlockSpec(down.shape, whole, pipeline_mode=pl.Buffered(1)),
+            ],
+            out_specs=[block(f, row), block(f, row), block(f, row)]
+            + [block(d, other), block(d, mine), block(d, other), block(d, mine)],
+        ),
+        out_shape=[sds((ctx, m, r, f))] * 3 + [part] * 4,
         compiler_params=pltpu.CompilerParams(vmem_limit_bytes=VMEM_LIMIT),
-    )(x, cot, gu, down)
+    )(core, x, cot, gate, up, down)
 
 
 def pad_heads(w, heads, split):
@@ -517,121 +646,141 @@
         axis=2,
     ).transpose(1, 0, 2)
     by_rank = lambda w: w.reshape(rows, dp, ctx, frows).transpose(2, 0, 1, 3).reshape(ctx, rows, f)
-    pack_gu = jnp.concatenate([by_rank(w_gate), by_rank(w_up)], axis=2)
+    pack_gate, pack_up = by_rank(w_gate), by_rank(w_up)
     gains = jnp.stack([gain_attn, gain_ffn]).astype(F32)
     gains = jnp.pad(gains, ((0, 6), (0, LANES - rows)))
 
+    far = list(range(1, outer))
+    near = [j for j in far if j in (1, outer - 1)]
+    mid_way = [j for j in far if j not in near]
+
     def first_script(link, ins, outs, scratch):
-        x, seg, qkv, gain = ins
-        x_all, seg_all, g_qkv, g_gain = outs
+        x, seg, qkv, gain, wo, pg, pu, wd = ins
+        x_all, seg_all, g_qkv, g_gain, g_out, g_gate, g_up, g_down = outs
         (hold,) = scratch
         load = pltpu.make_async_copy(x, hold, link.sems[2].at[15])
         load.start()
-        link.keep(qkv.at[link.c], g_qkv.at[link.d, link.c])
-        link.keep(gain, g_gain.at[link.d, link.c])
-        link.keep(seg, seg_all.at[link.c])
+        mine = [
+            link.keep(qkv.at[link.c], g_qkv.at[link.d, link.c]),
+            link.keep(gain, g_gain.at[link.d, link.c]),
+            link.keep(wo, g_out.at[link.d, link.y, link.k]),
+            link.keep(seg, seg_all.at[link.c]),
+        ]
         a2a = exchange_ctx(link, qkv, lambda s: g_qkv.at[link.d, s])
         a2a += [link.put(gain, g_gain.at[link.d, link.c], (link.d, p)) for p in link.ctx_peers()]
         for p in link.ctx_peers():
             link.put(seg, seg_all.at[link.c], (link.d, p))
+        over_y = [
+            link.put(wo, g_out.at[link.d, link.y, link.k], link.ctx_dev(p, link.k)) for p in link.y_peers()
+        ]
         ways_x = gather_ctx_start(link, x, x_all)
+        exchange_ctx(link, pg, lambda s: g_gate.at[link.d, s])
+        exchange_ctx(link, pu, lambda s: g_up.at[link.d, s])
         for copy in a2a:
             link.arrived(copy)
-        for copy in link.local:
+        for copy in mine:
             copy.wait()
         link.local = []
-        slots = (lambda s: g_qkv.at[s], lambda s: g_gain.at[s])
-        ways = [gather_dp_start(link, slot) for slot in slots]
+        small = [lambda s: g_qkv.at[s], lambda s: g_gain.at[s]]
+        ways = [gather_dp_start(link, slot) for slot in small]
+        for copy in over_y:
+            link.arrived(copy)
+        out_slot = lambda s: g_out.at[s, :, link.k]
+        ways_out = gather_dp_start(link, out_slot)
         load.wait()
         store = pltpu.make_async_copy(hold, x_all.at[link.c], link.sems[2].at[14])
         store.start()
-        for slot, way in zip(slots, ways):
+        link.keep(pg.at[link.c], g_gate.at[link.d, link.c])
+        link.keep(pu.at[link.c], g_up.at[link.d, link.c])
+        link.keep(wd, g_down.at[link.d])
+        for slot, way in zip(small, ways):
             gather_dp_forward(link, slot, way)
         gather_ctx_forward(link, x_all, ways_x)
+        gather_dp_forward(link, out_slot, ways_out)
+        for copy in list(link.inflight):
+            link.arrived(copy)
+        both = g_out.at[:, :, link.k]
+        link.put(both, both, link.ctx_dev(link.y, 1 - link.k))
         store.wait()
 
-    x_all, seg_all, g_qkv, g_gain = communicate(
+    x_all, seg_all, g_qkv, g_gain, g_out, g_gate, g_up, g_down = communicate(
         z,
         "gather_first",
         1,
         first_script,
-        (inputs, segments, pack_qkv, gains),
+        (inputs, segments, pack_qkv, gains, w_out, pack_gate, pack_up, w_down),
         (
             sds((ctx, m, r, d)),
             sds((ctx, m, r), jnp.int32),
             sds((dp, ctx, rows, width)),
             sds((dp, ctx, 8, LANES), F32),
+            sds((dp, ys, 2, rows, d)),
+            sds((dp, ctx, rows, f)),
+            sds((dp, ctx, rows, f)),
+            sds((dp, frows, d)),
         ),
         [pltpu.VMEM((m, r, d), BF)],
     )
     gain_a = g_gain[:, :, 0, :rows].reshape(1, d)
     gain_f = g_gain[:, :, 1, :rows].reshape(1, d)
     wqkv = g_qkv.reshape(d, width)
+    wo = g_out.reshape(d, d)
     cos, sin = rope_tables(ctx, r)
     qdoc = seg_all.reshape(ctx, m, r, 1)
     kdoc = seg_all.reshape(ctx, m, 1, r)
-
-    normed_a, q, k, v = qkv_call(z, x_all, gain_a, wqkv, cos, sin, hc, kvc)
-    att, lse = attend_call(z, q, k, v, qdoc, kdoc, hc, kvc)
+    early, late = range(m // 2), range(m // 2, m)
+
+    def qkv_cargo(cargo, moved, bufs):
+        (cot,), (g_gate, g_up, cot_all) = moved, bufs
+        own_y(cargo, cot, cot_all, early)
+        for buf in (g_gate, g_up):
+            own_outer(cargo, buf, near[:1])
+            own_inner(cargo, buf)
+
+    g_gate, g_up, cot_all, normed_a, q, k, v = qkv_call(
+        z, x_all, gain_a, wqkv, cos, sin, hc, kvc,
+        qkv_cargo, (cotangent,), (sds((ctx, m, r, d)),), (g_gate, g_up),
+    )
+
+    def attend_cargo(cargo, moved, bufs):
+        (cot,), (g_gate, g_up, cot_all) = moved, bufs
+        own_y(cargo, cot, cot_all, late)
+        pass_core(cargo, cot_all, early)
+        for buf in (g_gate, g_up):
+            own_outer(cargo, buf, near[1:])
+            pass_inner(cargo, buf, near[:1])
+
+    g_gate, g_up, cot_all, att, lse = attend_call(
+        z, q, k, v, qdoc, kdoc, hc, kvc, attend_cargo, (cotangent,), (), (g_gate, g_up, cot_all)
+    )
 
     def second_script(link, ins, outs, scratch):
-        att, wo, gu, wd, cot = ins
-        att_all, g_out, g_gu, g_down, cot_all = outs
+        att, cot = ins[:2]
+        g_gate, g_up, g_down, cot_all, att_all = outs
         (hold,) = scratch
         load = pltpu.make_async_copy(cot, hold, link.sems[2].at[15])
         load.start()
-        link.keep(gu.at[link.c], g_gu.at[link.d, link.c])
-        link.keep(wo, g_out.at[link.d, link.y, link.k])
-        link.keep(wd, g_down.at[link.d])
         link.keep(att.at[link.c], att_all.at[link.c])
         exchange_ctx(link, att, lambda s: att_all.at[s])
-        a2a = exchange_ctx(link, gu, lambda s: g_gu.at[link.d, s])
-        for p in link.y_peers():
-            a2a.append(link.put(wo, g_out.at[link.d, link.y, link.k], link.ctx_dev(p, link.k)))
-        ways_c = gather_ctx_start(link, cot, cot_all)
+        own_outer(link, g_down, near)
+        for buf in (g_gate, g_up):
+            pass_inner(link, buf, near[1:])
+        pass_core(link, cot_all, late)
         load.wait()
         store = pltpu.make_async_copy(hold, cot_all.at[link.c], link.sems[2].at[14])
         store.start()
-        for copy in link.local:
-            copy.wait()
-        link.local = []
-        slots = [
-            lambda s: g_down.at[s],
-            lambda s: g_gu.at[s],
-            lambda s: g_out.at[s, :, link.k],
-        ]
-        ways = [gather_dp_start(link, slots[0])]
-        for copy in a2a:
-            link.arrived(copy)
-        ways += [gather_dp_start(link, slot) for slot in slots[1:]]
-        gather_ctx_forward(link, cot_all, ways_c)
-        done = 0
-        for slot, way in zip(slots, ways):
-            gather_dp_forward(link, slot, way)
-        for copy in list(link.inflight):
-            link.arrived(copy)
-        mine = g_out.at[:, :, link.k]
-        link.put(mine, mine, link.ctx_dev(link.y, 1 - link.k))
         store.wait()
 
-    att_all, g_out, g_gu, g_down, cot_all = communicate(
+    g_gate, g_up, g_down, cot_all, att_all = communicate(
         z,
-        "gather_second",
+        "exchange_heads",
         2,
         second_script,
-        (att, w_out, pack_gu, w_down, cotangent),
-        (
-            sds(att.shape),
-            sds((dp, ys, 2, rows, d)),
-            sds((dp, ctx, rows, 2 * f)),
-            sds((dp, frows, d)),
-            sds((ctx, m, r, d)),
-        ),
+        (att, cotangent),
+        (sds(att.shape),),
         [pltpu.VMEM((m, r, d), BF)],
-    )
-    wo = g_out.reshape(d, d)
-    wgu = g_gu.reshape(d, 2 * f)
-    wd = g_down.reshape(f, d)
+        (g_gate, g_up, g_down, cot_all),
+    )
 
     att_rows = att_all.transpose(1, 2, 0, 3).reshape(m * r, H * HD)
     residual = inputs.astype(F32)
@@ -640,52 +789,98 @@
     normed = (mid * scale_f * gain_f).astype(BF)
 
     def third_script(link, ins, outs, scratch):
-        (x,), (x_all,), (hold,) = ins, outs, scratch
+        x, (g_gate, g_up, g_down, x_all), (hold,) = ins[0], outs, scratch
         load = pltpu.make_async_copy(x, hold, link.sems[2].at[15])
         load.start()
         ways = gather_ctx_start(link, x, x_all)
+        bufs = (g_gate, g_up, g_down)
+        coming = []
+        for buf in bufs:
+            for j in mid_way:
+                start = link.put(buf.at[link.d], buf.at[link.d], link.dp_dev(link.outer_to(j), link.i))
+                coming.append((buf, j, start))
+        own_inner(link, g_down)
+        pass_inner(link, g_down, near)
         load.wait()
         store = pltpu.make_async_copy(hold, x_all.at[link.c], link.sems[2].at[14])
         store.start()
-        gather_ctx_forward(link, x_all, ways)
+        for n, (buf, j, copy) in enumerate(coming):
+            if n == len(coming) - 1:
+                gather_ctx_forward(link, x_all, ways)
+            link.arrived(copy)
+            pass_inner(link, buf, [j])
         store.wait()
 
-    (normed_all,) = communicate(
-        z, "gather_third", 3, third_script, (normed,), (sds((ctx, m, r, d)),), [pltpu.VMEM((m, r, d), BF)]
-    )
-
-    hidden, dgu, out_part, dn_part = mlp_call(z, normed_all, cot_all, wgu, wd)
-
+    g_gate, g_up, g_down, normed_all = communicate(
+        z,
+        "gather_third",
+        3,
+        third_script,
+        (normed,),
+        (sds((ctx, m, r, d)),),
+        [pltpu.VMEM((m, r, d), BF)],
+        (g_gate, g_up, g_down),
+    )
+    w_gate_c, w_up_c, w_down_c = g_gate.reshape(d, f), g_up.reshape(d, f), g_down.reshape(f, d)
+
+    core = ki.astype(jnp.int32).reshape(1)
+    hidden, d_gate, d_up, dn_other, dn_mine, out_other, out_mine = mlp_call(
+        z, core, normed_all, cot_all, w_gate_c, w_up_c, w_down_c
+    )
+
+    dp_perm = lambda fn: [(o * inner + i, fn(o, i)) for o in range(outer) for i in range(inner)]
+    ctx_perm = lambda fn: [(y * 2 + k, fn(y, k)) for y in range(ys) for k in range(2)]
+    wide = lambda a: a.astype(F32)
     flat = lambda a: a.reshape(ctx * m * r, a.shape[-1])
+
+    def after(a, dep):
+        return lax.optimization_barrier((a, dep))[0]
+
+    def to_core(a):
+        return lax.ppermute(a, "ctx", ctx_perm(lambda y, k: y * 2 + 1 - k))
+
+    def to_y(mine, got, dim=0):
+        both = lambda at: wide(dyn(mine, at, dim)) + wide(dyn(got, at, dim))
+        came = [
+            lax.ppermute(
+                both((yi + j) % ys).astype(BF), "ctx", ctx_perm(lambda y, k: (y + j) % ys * 2 + k)
+            )
+            for j in range(1, ys)
+        ]
+        return both(yi), came
+
+    def to_inner(part):
+        return [
+            lax.ppermute(
+                dyn(part, (ii + j) % inner, 1), "dp", dp_perm(lambda o, i: o * inner + (i + j) % inner)
+            )
+            for j in range(1, inner)
+        ]
+
+    def to_outer(part, came):
+        both = lambda at: wide(part[at, ii]) + sum(wide(dyn(a, at, 0)) for a in came)
+        got = [
+            lax.ppermute(
+                both((oi + j) % outer).astype(BF), "dp", dp_perm(lambda o, i: (o + j) % outer * inner + i)
+            )
+            for j in range(1, outer)
+        ]
+        return both(oi), got
+
+    close = lambda own, came: own + sum(wide(a) for a in came)
+
+    dn_got = to_core(dn_other)
     part_down = dot_tn(flat(hidden), flat(cot_all)).astype(BF).reshape(outer, inner, frows, d)
-    part_gu = dot_tn(flat(normed_all), flat(dgu)).astype(BF).reshape(outer, inner, ctx, rows, 2 * f)
-
-    halves = lambda a: a.reshape((ys, 2) + a.shape[1:])
-    out_part, dn_part = halves(out_part), halves(dn_part)
-    shape_y = (ys, m, r, d)
-
-    def core_script(link, ins, outs, scratch):
-        for src, dst in zip(ins, outs):
-            scatter_core(link, src, dst)
-
-    def y_script(link, ins, outs, scratch):
-        for src, dst in zip(ins, outs):
-            scatter_y(link, src, dst)
-
-    dn_in, out_in = communicate(
-        z, "reduce_core", 4, core_script, (dn_part, out_part), (sds(shape_y), sds(shape_y))
-    )
-    pair = lambda part, got: (dyn(part, ki, 1).astype(F32) + got.astype(F32)).astype(BF)
-    dn_pair, out_pair = pair(dn_part, dn_in), pair(out_part, out_in)
-    shape_y = (ys - 1, m, r, d)
-    dn_in, out_in = communicate(
-        z, "reduce_y", 5, y_script, (dn_pair, out_pair), (sds(shape_y), sds(shape_y))
-    )
-    total = lambda part, got, at: dyn(part, at, 0).astype(F32) + jnp.sum(got.astype(F32), axis=0)
-    d_normed = total(dn_pair, dn_in, yi)
-    outputs = mid + total(out_pair, out_in, yi)
-
-    grad_gain_f = jnp.sum(d_normed * mid * scale_f, axis=(0, 1))
+    down_x = to_inner(part_down)
+    dn_own, dn_came = to_y(dn_mine, dn_got)
+    shape_g = (outer, inner, ctx, rows, f)
+    part_gate = dot_tn(flat(normed_all), flat(d_gate)).astype(BF).reshape(shape_g)
+    gate_x = to_inner(part_gate)
+    part_up = dot_tn(flat(normed_all), flat(d_up)).astype(BF).reshape(shape_g)
+    up_x = to_inner(part_up)
+    out_got = to_core(out_other)
+
+    d_normed = close(dn_own, dn_came)
     cot32 = cotangent.astype(F32)
     e = d_normed * gain_f
     d_mid = cot32 + (
@@ -694,111 +889,68 @@
     d_mid_low = d_mid.astype(BF).reshape(m * r, d)
     d_att = dot_nt(d_mid_low, wo).astype(BF)
     d_att = d_att.reshape(m, r, ctx, hc * HD).transpose(2, 0, 1, 3)
-    part_out = dot_tn(att_rows, d_mid_low).astype(BF).reshape(dp, ys, 2, rows, d)
 
     def fourth_script(link, ins, outs, scratch):
         link.keep(ins[0].at[link.c], outs[0].at[link.c])
         exchange_ctx(link, ins[0], lambda s: outs[0].at[s])
-        link.put(ins[1].at[:, :, 1 - link.k], outs[1], link.ctx_dev(link.y, 1 - link.k))
-
-    d_att_all, po_in = communicate(
-        z,
-        "exchange_back",
-        6,
-        fourth_script,
-        (d_att, part_out),
-        (sds(d_att.shape), sds((dp, ys, rows, d))),
-    )
-    po_pair = (dyn(part_out, ki, 2).astype(F32) + po_in.astype(F32)).astype(BF)
-    po_pair = po_pair.transpose(1, 0, 2, 3)
-
-    dqkv = attend_back_call(z, q, k, v, qdoc, kdoc, att, d_att_all, lse, cos, sin, hc, kvc)
-    part_qkv = dot_tn(flat(normed_a), flat(dqkv)).astype(BF).reshape(outer, inner, ctx, rows, width)
-    da_part = halves(dot_nt(flat(dqkv), wqkv).astype(BF).reshape(ctx, m, r, d))
-
-    def fifth_script(link, ins, outs, scratch):
-        scatter_core(link, ins[0], outs[0])
-        scatter_y(link, ins[1], outs[1])
-        for n in (2, 3, 4):
-            scatter_inner(link, ins[n], outs[n])
-
-    da_in, po_y, down_in, gu_in, qkv_in = communicate(
-        z,
-        "reduce_inner",
-        7,
-        fifth_script,
-        (da_part, po_pair, part_down, part_gu, part_qkv),
-        (
-            sds((ys, m, r, d)),
-            sds((ys - 1, dp, rows, d)),
-            sds((inner - 1, outer, frows, d)),
-            sds((inner - 1, outer, ctx, rows, 2 * f)),
-            sds((inner - 1, outer, ctx, rows, width)),
-        ),
-    )
-    da_pair = pair(da_part, da_in)
-    po_quarter = total(po_pair, po_y, yi).astype(BF).reshape(outer, inner, rows, d)
-    column = lambda part, got: (dyn(part, ii, 1).astype(F32) + jnp.sum(got.astype(F32), axis=0)).astype(BF)
-    down_col, gu_col, qkv_col = column(part_down, down_in), column(part_gu, gu_in), column(part_qkv, qkv_in)
-
-    def sixth_script(link, ins, outs, scratch):
-        scatter_y(link, ins[0], outs[0])
-        scatter_inner(link, ins[1], outs[1])
-        for n in (2, 3, 4):
-            scatter_outer(link, ins[n], outs[n])
-
-    da_in, po_in, down_in, gu_in, qkv_in = communicate(
-        z,
-        "reduce_outer",
-        8,
-        sixth_script,
-        (da_pair, po_quarter, down_col, gu_col, qkv_col),
-        (
-            sds((ys - 1, m, r, d)),
-            sds((inner - 1, outer, rows, d)),
-            sds((outer - 1, frows, d)),
-            sds((outer - 1, ctx, rows, 2 * f)),
-            sds((outer - 1, ctx, rows, width)),
-        ),
-    )
-    d_normed_a = total(da_pair, da_in, yi)
+
+    (d_att_all,) = communicate(z, "exchange_back", 6, fourth_script, (d_att,), (sds(d_att.shape),))
+
+    part_out = dot_tn(att_rows, d_mid_low).astype(BF).reshape(dp, ys, 2, rows, d)
+    po_got = to_core(dyn(part_out, 1 - ki, 2))
+    down_own, down_z = to_outer(part_down, after(down_x, d_att))
+    gate_own, gate_z = to_outer(part_gate, after(gate_x, d_att_all))
+    out_own, out_came = to_y(after(out_mine, d_att_all), out_got)
+    dq, dkv = attend_back_call(z, q, k, v, qdoc, kdoc, att, d_att_all, lse, cos, sin, hc, kvc)
+
+    part_q = dot_tn(flat(normed_a), flat(dq)).astype(BF).reshape(outer, inner, ctx, rows, hc * LANES)
+    q_x = to_inner(part_q)
+    part_kv = dot_tn(flat(normed_a), flat(dkv)).astype(BF).reshape(outer, inner, ctx, rows, 2 * kvc * LANES)
+    kv_x = to_inner(part_kv)
+    da = dot_nt(flat(dq), wqkv[:, : hc * LANES]) + dot_nt(flat(dkv), wqkv[:, hc * LANES :])
+    da = da.astype(BF).reshape(ys, 2, m, r, d)
+    da_own, da_came = to_y(dyn(da, ki, 1), to_core(dyn(da, 1 - ki, 1)))
+    up_own, up_z = to_outer(part_up, after(up_x, dq))
+    po_own, po_came = to_y(dyn(after(part_out, dq), ki, 2), po_got, 1)
+    q_own, q_z = to_outer(part_q, q_x)
+    kv_own, kv_z = to_outer(part_kv, kv_x)
+    po = close(po_own, po_came).astype(BF).reshape(outer, inner, rows, d)
+    po_own, po_z = to_outer(po, to_inner(po))
+    outputs = mid + close(out_own, after(out_came, dq))
+    grad_down = close(down_own, after(down_z, part_kv))
+    gate_mine = close(gate_own, after(gate_z, part_kv)).astype(BF)
+    up_mine = close(up_own, after(up_z, da_own)).astype(BF)
+    d_normed_a = close(da_own, da_came)
     scale_a = lax.rsqrt(jnp.mean(residual * residual, axis=-1, keepdims=True) + EPS)
-    grad_gain_a = jnp.sum(d_normed_a * residual * scale_a, axis=(0, 1))
     e = d_normed_a * gain_a
     input_grad = d_mid + (
         scale_a * e - residual * (scale_a * scale_a * scale_a) * jnp.mean(e * residual, axis=-1, keepdims=True)
     )
-    grad_down = total(down_col, down_in, oi)
-    gu_mine = total(gu_col, gu_in, oi).astype(BF)
-    qkv_mine = total(qkv_col, qkv_in, oi).astype(BF)
-    po_col = column(po_quarter, po_in)
+    q_mine = close(q_own, q_z).astype(BF)
+    kv_mine = close(kv_own, kv_z).astype(BF)
+    grad_out = close(po_own, po_z)
 
     def seventh_script(link, ins, outs, scratch):
-        for n in (0, 1):
-            link.keep(ins[n].at[link.c], outs[n].at[link.c])
-            exchange_ctx(link, ins[n], lambda s: outs[n].at[s])
-        scatter_outer(link, ins[2], outs[2])
-
-    gu_all, qkv_all, po_in = communicate(
-        z,
-        "reduce_last",
-        9,
-        seventh_script,
-        (gu_mine, qkv_mine, po_col),
-        (sds((ctx, rows, 2 * f)), sds((ctx, rows, width)), sds((outer - 1, rows, d))),
-    )
-    grad_out = total(po_col, po_in, oi)
-    gu_all = gu_all.astype(F32)
-    spread = lambda a: a.reshape(ctx, rows, dp, frows).transpose(1, 2, 0, 3).reshape(rows, ff)
-    grad_gate, grad_up = spread(gu_all[:, :, :f]), spread(gu_all[:, :, f:])
-    qkv_all = qkv_all.astype(F32)
-    cols = lambda a, heads, split: unpad_heads(a, heads, split).transpose(1, 0, 2).reshape(rows, ctx * heads * HD)
-    grad_query = cols(qkv_all[:, :, : hc * LANES], hc, True)
-    grad_key = cols(qkv_all[:, :, hc * LANES : (hc + kvc) * LANES], kvc, True)
-    grad_value = cols(qkv_all[:, :, (hc + kvc) * LANES :], kvc, False)
-    both = lax.psum_scatter(
-        jnp.stack([grad_gain_a, grad_gain_f], axis=1), ("dp", "ctx"), scatter_dimension=0, tiled=True
-    )
+        for src, dst in zip(ins, outs):
+            link.keep(src.at[link.c], dst.at[link.c])
+            exchange_ctx(link, src, lambda s: dst.at[s])
+
+    last = (gate_mine, up_mine, q_mine, kv_mine)
+    gate_all, up_all, q_all, kv_all = communicate(
+        z, "reduce_last", 9, seventh_script, last, [sds(a.shape) for a in last]
+    )
+    spread = lambda a: wide(a).reshape(ctx, rows, dp, frows).transpose(1, 2, 0, 3).reshape(rows, ff)
+    grad_gate, grad_up = spread(gate_all), spread(up_all)
+    cols = lambda a, heads, split: (
+        unpad_heads(wide(a), heads, split).transpose(1, 0, 2).reshape(rows, ctx * heads * HD)
+    )
+    grad_query = cols(q_all, hc, True)
+    grad_key = cols(kv_all[:, :, : kvc * LANES], kvc, True)
+    grad_value = cols(kv_all[:, :, kvc * LANES :], kvc, False)
+
+    along = lambda pairs, gain: sum(jnp.sum(wide(w) * g, axis=1) for w, g in pairs) / wide(gain)
+    grad_gain_a = along(((w_query, grad_query), (w_key, grad_key), (w_value, grad_value)), gain_attn)
+    grad_gain_f = along(((w_gate, grad_gate), (w_up, grad_up)), gain_ffn)
     return (
         outputs,
         input_grad,
@@ -809,8 +961,8 @@
         grad_gate,
         grad_up,
         grad_down,
-        both[:, 0],
-        both[:, 1],
+        grad_gain_a,
+        grad_gain_f,
     )
 
 

time: 1080 us -> 705 us (0.65)
  Pallas kernels: 843 us -> 357 us
  waiting for transfers between devices: 41.3 us -> 109 us
  starting transfers between devices: 0.04 us -> 42.2 us
  between operations: 15.3 us -> 2 us
    pallas_call x9 -> x5, Pallas kernels: 726 us -> 216 us  [communicate(): pl.pallas_call(kernel, name=name, out_shape=list(outs), in_specs=[hbm] *...]
    ppermute x0 -> x32, waiting for transfers between devices: none -> 109 us  [the longest x18 85 us: to_outer(): lax.ppermute(both((oi + j) % outer).astype(BF), 'dp', dp_perm(lambda o, i...]
    ppermute x0 -> x32, starting transfers between devices: none -> 42.2 us  [the longest x18 31.2 us: to_outer(): lax.ppermute(both((oi + j) % outer).astype(BF), 'dp', dp_perm(lambda o, i...]
    unnamed x2 -> x0, waiting for transfers between devices: 41.3 us -> none
    pallas_call x3, Pallas kernels: 84.8 us -> 110 us  [the longest x2 57.8 us: fused_call(): pl.pallas_call(kernel, name=name, grid=grid, in_specs=list(in_specs) + [h...]
    convert_element_type x10 -> x15, other arithmetic: 34.2 us -> 21.8 us  [the longest x4 7.43 us: to_y(): both((yi + j) % ys).astype(BF)]
    dot_general x4 -> x6, matrix products: 45.5 us -> 46.7 us  [dot_tn(): lax.dot_general(a, b, (((0,), (0,)), ((), ())), preferred_element_type=F32)]
  transfers between devices with their start and end apart: 1 -> 32, of which waited for: 1 -> 11; matrix products, arithmetic and copies ran while one was open for 3% -> 18% of each run, Pallas kernels for 2% -> 7%
where the time goes in v2:
time: 705 us; the launch traced here: 698 us
  Pallas kernels  357 us (51%)
  waiting for transfers between devices  109 us (15%)
  matrix products  73.7 us (10%)
  other arithmetic  59.2 us (8%)
  local copies, waits for them, and re-layouts  55.2 us (8%)
  starting transfers between devices  42.2 us (6%)
    pallas_call x5, Pallas kernels, communicate(): pl.pallas_call(kernel, name=name, out_shape=list(outs), in_specs=[hbm] *...  216 us
    ppermute x18, waiting for transfers between devices, to_outer(): lax.ppermute(both((oi + j) % outer).astype(BF), 'dp', dp_perm(lambda o, i...  85 us
    pallas_call x2, Pallas kernels, fused_call(): pl.pallas_call(kernel, name=name, grid=grid, in_specs=list(in_specs) + [h...  57.8 us
    pallas_call x1, Pallas kernels, mlp_call(): pl.pallas_call(mlp_kernel, name='mlp', grid_spec=pltpu.PrefetchScalarGrid...  51.7 us
    dot_general x6, matrix products, dot_tn(): lax.dot_general(a, b, (((0,), (0,)), ((), ())), preferred_element_type=F32)  46.7 us
    pallas_call x1, Pallas kernels, attend_back_call(): pl.pallas_call(functools.partial(attend_back_kernel, hc, kvc, ctx), name=...  31.5 us
    ppermute x18, starting transfers between devices, to_outer(): lax.ppermute(both((oi + j) % outer).astype(BF), 'dp', dp_perm(lambda o, i...  31.2 us
    dot_general x3, matrix products, dot_nt(): lax.dot_general(a, b, (((1,), (1,)), ((), ())), preferred_element_type=F32)  20.8 us
  transfers between devices with their start and end apart: 32, of which 11 were waited for; matrix products, arithmetic and copies ran while one was open for 18% of the time, Pallas kernels for 7%

profile of v2, /device:TPU:0, one launch (start us, length us, event | category | flops | bytes accessed | tf_op | source)
XLA Modules:
  0.0 698.2 jit_solution(17147036963818555597)
XLA Ops:
  8.0 1.9 multiply_sine_fusion
  12.4 90.4 %gather_first.1 = (bf16[4,2,256,1536]{3,2,1,0:T(8,128)(2,1)}, s32[4,2,256]{2,1,0:T(2,128)}, bf16[8,4,48,1024]{3,2,1,0:T(8,128)(2,1)}, f32[8,4,8,128]{3,2,1,0:T(8...) custom-call(bf16[2,256,1536]{2,1,0:T(8,128)(2,1)} %refs_0_.1, ...), custom_call_target="tpu_custom_call" | custom-call | tf_op jit(solution)/shard_map/gather_first/pallas_call | solution.py:147
  106.5 2.1 copy.54.refs_3_.qdoc_ref
  109.6 34.4 %qkv.1 = (bf16[8,4,48,1024]{3,2,1,0:T(8,128)(2,1)}, bf16[8,4,48,1024]{3,2,1,0:T(8,128)(2,1)}, bf16[4,2,256,1536]{3,2,1,0:T(8,128)(2,1)}, bf16[4,2,256,1536]{3,2,...) custom-call(bf16[4,2,256,1536]{3,2,1,0:T(8,128)(2,1)} %get-tuple-ele, ...), custom_call_target="tpu_custom_call", output_to_operand_aliasing={{0}: (6, {}), {1}: (7, {})} | custom-call | tf_op jit(solution)/shard_map/qkv/pallas_call | solution.py:282
  144.0 23.5 %attend.1 = (bf16[8,4,48,1024]{3,2,1,0:T(8,128)(2,1)}, bf16[8,4,48,1024]{3,2,1,0:T(8,128)(2,1)}, bf16[4,2,256,1536]{3,2,1,0:T(8,128)(2,1)}, bf16[4,2,256,384]{3,2,1,0:T(8,128)(2,1)}, f32[4,2,256,128]{3,2,1,0:T(8,128)}) custom-call(bf16[4,2,256,512]{3,2,1,0:T(8,128)(2,1)} %get-tuple-element.73.refs_0_.q_ref, ...), custom_call_target="tpu_custom_call", output_to_operand_aliasing={{0}: (6, {}), {1}: (7, {}), {2}: (8, {})} | custom-call | tf_op jit(solution)/shard_map/attend/pallas_call | solution.py:282
  167.4 22.1 %exchange_heads.1 = (bf16[8,4,48,1024]{3,2,1,0:T(8,128)(2,1)}, bf16[8,4,48,1024]{3,2,1,0:T(8,128)(2,1)}, bf16[8,128,1536]{2,1,0:T(8,128)(2,1)}, bf16[4,2,256,153...) custom-call(bf16[4,2,256,384]{3,2,1,0:T(8,128)(2,1)} %get-tuple-elem, ...), custom_call_target="tpu_custom_call", output_to_operand_aliasing={{0}: (2, {}), {1}: (3, {}), {2}: (4, {}), {3}: (5, {})} | custom-call | tf_op jit(solution)/shard_map/exchange_heads/pallas_call | solution.py:147
  189.6 2.6 copy.55
  192.2 6.1 multiply_reduce_fusion.1
  200.4 66.1 %gather_third.1 = (bf16[8,4,48,1024]{3,2,1,0:T(8,128)(2,1)}, bf16[8,4,48,1024]{3,2,1,0:T(8,128)(2,1)}, bf16[8,128,1536]{2,1,0:T(8,128)(2,1)}, bf16[4,2,256,1536]{3,2,1,0:T(8,128)(2,1)}) custom-call(bf16[2,256,1536]{2,1,0:T(8,128)(2,1)} %multiply_convert_fusion.refs_0_, ...), custom_call_target="tpu_custom_call", output_to_operand_aliasing={{0}: (1, {}), {1}: (2, {}), {2}: (3, {})} | custom-call | tf_op jit(solution)/shard_map/gather_third/pallas_call | solution.py:147
  266.5 51.7 %mlp.1 = (bf16[4,2,256,1024]{3,2,1,0:T(8,128)(2,1)}, bf16[4,2,256,1024]{3,2,1,0:T(8,128)(2,1)}, bf16[4,2,256,1024]{3,2,1,0:T(8,128)(2,1)}, bf16[2,2,256,1536]{3,...) custom-call(s32[1]{0:T(128)} %bitcast.13.k_ref, ...), custom_call_target="tpu_custom_call" | custom-call | tf_op jit(solution)/shard_map/mlp/pallas_call | solution.py:575
  318.2 11.4 %bitcast_convert_fusion = bf16[1024,1536]{1,0:T(8,128)(2,1)} fusion(bf16[4,2,256,1024]{3,2,1,0:T(8,128)(2,1)} %get-tuple-element.120, bf16[4,2,256,1536]{3,2,1,0:T(8,128)(2,1)} %get-tuple-element.91.cot_ref), kind=kOutput, calls=%fused_computation.2 | convolution fusion | flops 6444023808 | bytes 13631488 | tf_op jit(solution)/shard_map/dot_general | solution.py:40
  329.6 2.6 dynamic-slice_bitcast_fusion.1
  333.3 10.6 %bitcast_convert_fusion.1 = bf16[1536,1024]{1,0:T(8,128)(2,1)S(1)} fusion(bf16[4,2,256,1536]{3,2,1,0:T(8,128)(2,1)} %get-tuple-element.90.x_ref, bf16[4,2,256,1024]{3,2,1,0:T(8,128)(2,1)} %get-tuple-element.110), kind=kOutput, calls=%fused_computation.3 | convolution fusion | flops 6444023808 | bytes 13631488 | tf_op jit(solution)/shard_map/dot_general | solution.py:40
  343.8 1.7 copy-done.7
  347.9 3.6 fusion.13
  352.7 8.8 %bitcast_convert_fusion.2 = bf16[1536,1024]{1,0:T(8,128)(2,1)S(1)} fusion(bf16[4,2,256,1536]{3,2,1,0:T(8,128)(2,1)} %get-tuple-element.90.x_ref, bf16[4,2,256,1024]{3,2,1,0:T(8,128)(2,1)S(1)} %copy-done.27), kind=kOutput, calls=%fused_computation.4 | convolution fusion | flops 6444023808 | bytes 13631488 | tf_op jit(solution)/shard_map/dot_general | solution.py:40
  365.2 3.8 copy.66
  369.7 2.9 copy.84
  372.6 15.4 %collective-permute-done.1 = bf16[2,256,1536]{2,1,0:T(8,128)(2,1)} collective-permute-done((bf16[2,256,1536]{2,1,0:T(8,128)(2,1)}, bf16[2,256,1536]{2,1,0:T(8,128)(2,1)}, u32[]{:S(2)}, u32[]{:S(2)}) %collective-permute-start.1) | collective-permute-done | bytes 1572896 | tf_op jit(solution)/shard_map/ppermute | solution.py:845
  388.0 3.4 multiply_reduce_fusion
  391.5 4.1 fusion.53
  396.7 3.7 convolution_convert_fusion.1
  400.4 4.0 reshape.387
  404.4 2.8 copy.95
  407.2 20.2 %exchange_back.1.do_ref = bf16[4,2,256,384]{3,2,1,0:T(8,128)(2,1)} custom-call(bf16[4,2,256,384]{3,2,1,0:T(8,128)(2,1)} %bitcast.323), custom_call_target="tpu_custom_call" | custom-call | tf_op jit(solution)/shard_map/exchange_back/pallas_call | solution.py:147
  427.4 2.9 fusion.18
  430.3 1.8 collective-permute-start.31
  432.1 3.0 convolution_convert_fusion
  435.1 2.1 copy-done.6
  439.9 31.5 %attend_back.1 = (bf16[4,2,256,512]{3,2,1,0:T(8,128)(2,1)}, bf16[4,2,256,512]{3,2,1,0:T(8,128)(2,1)}) custom-call(bf16[4,2,256,512]{3,2,1,0:T(8,128)(2,1)} %get-tuple-element.73.refs_0_.q_ref, bf16[4,2,256,256]{3,2,1,0:T(8,128)(2,1)} %get-tuple-element.74.refs_1_.k_ref, bf16[4,2,256,256]{3,2,1,0:T(8,128)(2,1)} %get-tuple-element.75.refs_2_.v_ref, ...), custom_call_target="tpu_custom_call" | custom-call | tf_op jit(solution)/shard_map/attend_back/pallas_call | solution.py:508
  471.5 10.2 %fusion.16 = f32[2048,1536]{1,0:T(8,128)} fusion(bf16[2048,512]{1,0:T(8,128)(2,1)} %bitcast.380, bf16[1536,1024]{1,0:T(8,128)(2,1)} %bitcast.356), kind=kOutput, calls=%fused_computation.43 | convolution fusion | flops 3221225472 | bytes 16252928 | tf_op jit(solution)/shard_map/dot_general | solution.py:36
  481.7 6.9 add_convert_fusion
  489.0 6.4 fusion.8
  495.4 6.4 fusion.9
  501.9 1.9 fusion.27
  504.7 1.9 fusion.14
  506.6 1.7 fusion.22
  508.3 2.9 collective-permute-start.9
  511.2 6.3 collective-permute-done.30
  520.5 5.5 collective-permute-done.9
  527.1 24.2 %collective-permute-done.8 = bf16[4,48,1024]{2,1,0:T(8,128)(2,1)S(1)} collective-permute-done((bf16[4,48,1024]{2,1,0:T(8,128)(2,1)S(1)}, bf16[4,48,1024]{2,1,0:T(8,128)(2,1)S(1)}, u32[]{:S(2)}, u32[]{:S(2)}) %collective-permute-start.8) | collective-permute-done | bytes 393248 | tf_op jit(solution)/shard_map/ppermute | solution.py:863
  553.3 2.1 fusion.31.refs_0_
  555.3 2.3 fusion.21
  557.9 4.2 collective-permute-start.19
  562.0 8.8 %collective-permute-done.14 = bf16[4,4,48,512]{3,2,1,0:T(8,128)(2,1)S(1)} collective-permute-done((bf16[4,4,48,512]{3,2,1,0:T(8,128)(2,1)S(1)}, bf16[4,4,48,512]{3,2,1,0:T(8,128)(2,1)S(1)}, u32[]{:S(2)}, u32[]{:S(2)}) %collective-permute-start.14) | collective-permute-done | bytes 786464 | tf_op jit(solution)/shard_map/ppermute | solution.py:854
  572.6 1.7 fusion.12
  574.4 2.1 collective-permute-start.15
  576.5 1.7 collective-permute-done.21
  578.2 2.3 collective-permute-start.17
  580.5 10.3 %collective-permute-done.20 = bf16[4,48,512]{2,1,0:T(8,128)(2,1)S(1)} collective-permute-done((bf16[4,48,512]{2,1,0:T(8,128)(2,1)S(1)}, bf16[4,48,512]{2,1,0:T(8,128)(2,1)S(1)}, u32[]{:S(2)}, u32[]{:S(2)}) %collective-permute-start.20) | collective-permute-done | bytes 196640 | tf_op jit(solution)/shard_map/ppermute | solution.py:863
  593.9 7.2 %collective-permute-done.16 = bf16[4,48,512]{2,1,0:T(8,128)(2,1)S(1)} collective-permute-done((bf16[4,48,512]{2,1,0:T(8,128)(2,1)S(1)}, bf16[4,48,512]{2,1,0:T(8,128)(2,1)S(1)}, u32[]{:S(2)}, u32[]{:S(2)}) %collective-permute-start.16) | collective-permute-done | bytes 196640 | tf_op jit(solution)/shard_map/ppermute | solution.py:863
  602.1 8.7 %collective-permute-start.25 = (bf16[48,1536]{1,0:T(8,128)(2,1)S(1)}, bf16[48,1536]{1,0:T(8,128)(2,1)S(1)}, u32[]{:S(2)}, u32[]{:S(2)}) collective-permute-start(bf16[48,1536]{1,0:T(8,128)(2,1)S(1)} %get-tuple-element.147), channel_id=1, source_target_pairs={{0,8},{4,12},{8,16},{12,20},{16,24},{20,28},{24,0},{28,4},{1,9},{5... | collective-permute-start | bytes 442376 | tf_op jit(solution)/shard_map/ppermute | solution.py:863
  610.8 3.1 collective-permute-start.27
  614.5 4.0 fusion.6
  618.5 3.8 collective-permute-done.25
  622.2 2.8 collective-permute-start.11
  625.0 22.0 %collective-permute-done.26 = bf16[48,1536]{1,0:T(8,128)(2,1)S(1)} collective-permute-done((bf16[48,1536]{1,0:T(8,128)(2,1)S(1)}, bf16[48,1536]{1,0:T(8,128)(2,1)S(1)}, u32[]{:S(2)}, u32[]{:S(2)}) %collective-permute-start.26) | collective-permute-done | bytes 147488 | tf_op jit(solution)/shard_map/ppermute | solution.py:863
  647.9 2.8 fusion
  650.7 4.0 collective-permute-done.12
  655.3 2.1 fusion.26.refs_1_
  657.4 16.7 %reduce_last.1 = (bf16[4,48,1024]{2,1,0:T(8,128)(2,1)}, bf16[4,48,1024]{2,1,0:T(8,128)(2,1)}, bf16[4,48,512]{2,1,0:T(8,128)(2,1)}, bf16[4,48,512]{2,1,0:T(8,128)(2,1)}) custom-call(bf16[4,48,1024]{2,1,0:T(8,128)(2,1)} %fusion.31.refs_0_, bf16[4,48,1024]{2,1,0:T(8,128)(2,1)} %fusion.26.refs_1_, bf16[4,48,512]{2,1,0:T(8,128)(2,1)} %fusion.41.refs_2_, ...), custom_call_target="tpu_custom_call" | custom-call | tf_op jit(solution)/shard_map/reduce_last/pallas_call | solution.py:147
  684.6 2.3 reshape.474
  688.1 1.8 multiply_reduce_fusion.2
  692.3 5.5 fusion.3
  (191 shorter events, 58.5 us)
Async XLA Ops:
  0.6 4.8 copy-start.16
  1.8 4.9 copy-start.17
  7.0 4.0 copy-start.25
  7.0 4.0 copy-start.26
  198.9 67.5 %copy-start.22 = (f32[2,256]{1,0:T(2,128)}, f32[2,256]{1,0:T(2,128)S(1)}, u32[]{:S(2)}) copy-start(f32[2,256]{1,0:T(2,128)S(1)} %get-tuple-element.160) | copy-start | bytes 6148
  318.2 29.8 %collective-permute-start = (bf16[2,2,256,1536]{3,2,1,0:T(8,128)(2,1)}, bf16[2,2,256,1536]{3,2,1,0:T(8,128)(2,1)}, u32[]{:S(2)}, u32[]{:S(2)}) collective-permute-start(bf16[2,2,256,1536]{3,2,1,0:T(8,128)(2,1)} %get-tuple-element.97), channel_id=1, source_target_pairs={{0,1},{1,0},{2,3},{3,2},{4,5},{5,4},{6,7},{7,6},{8,9},{9,8},{10,11... | collective-permute-start | bytes 9437192 | tf_op jit(solution)/shard_map/ppermute | solution.py:840
  332.3 95.1 %collective-permute-start.28 = (bf16[4,128,1536]{2,1,0:T(8,128)(2,1)}, bf16[4,128,1536]{2,1,0:T(8,128)(2,1)}, u32[]{:S(2)}, u32[]{:S(2)}) collective-permute-start(bf16[4,128,1536]{2,1,0:T(8,128)(2,1)} %dynamic-slice_bitcast_fusion.1), channel_id=1, source_target_pairs={{0,4},{4,0},{8,12},{12,8},{16,20},{20,16},{24,28},{28,24},{1,5},{5... | collective-permute-start | bytes 4718600 | tf_op jit(solution)/shard_map/ppermute | solution.py:854
  343.8 1.7 copy-start.7
  346.9 141.9 %collective-permute-start.10 = (bf16[4,4,48,1024]{3,2,1,0:T(8,128)(2,1)}, bf16[4,4,48,1024]{3,2,1,0:T(8,128)(2,1)}, u32[]{:S(2)}, u32[]{:S(2)}) collective-permute-start(bf16[4,4,48,1024]{3,2,1,0:T(8,128)(2,1)} %dynamic-slice_bitcast_fusion.2), channel_id=1, source_target_pairs={{0,4},{4,0},{8,12},{12,8},{16,20},{20,16},{24,28},{28,24},{1,5},{5... | collective-permute-start | bytes 4718600 | tf_op jit(solution)/shard_map/ppermute | solution.py:854
  347.9 4.8 copy-start.27
  351.5 36.5 %collective-permute-start.1 = (bf16[2,256,1536]{2,1,0:T(8,128)(2,1)}, bf16[2,256,1536]{2,1,0:T(8,128)(2,1)}, u32[]{:S(2)}, u32[]{:S(2)}) collective-permute-start(bf16[2,256,1536]{2,1,0:T(8,128)(2,1)} %fusion.13), channel_id=1, source_target_pairs={{0,2},{1,3},{2,0},{3,1},{4,6},{5,7},{6,4},{7,5},{8,10},{9,11},{10,... | collective-permute-start | bytes 4718600 | tf_op jit(solution)/shard_map/ppermute | solution.py:845
  361.6 1.6 copy-start.9
  364.5 124.4 %collective-permute-start.6 = (bf16[4,4,48,1024]{3,2,1,0:T(8,128)(2,1)}, bf16[4,4,48,1024]{3,2,1,0:T(8,128)(2,1)}, u32[]{:S(2)}, u32[]{:S(2)}) collective-permute-start(bf16[4,4,48,1024]{3,2,1,0:T(8,128)(2,1)} %dynamic-slice_bitcast_fusion.3), channel_id=1, source_target_pairs={{0,4},{4,0},{8,12},{12,8},{16,20},{20,16},{24,28},{28,24},{1,5},{5... | collective-permute-start | bytes 4718600 | tf_op jit(solution)/shard_map/ppermute | solution.py:854
  365.2 138.6 %collective-permute-start.2 = (bf16[2,2,256,1536]{3,2,1,0:T(8,128)(2,1)}, bf16[2,2,256,1536]{3,2,1,0:T(8,128)(2,1)}, u32[]{:S(2)}, u32[]{:S(2)}) collective-permute-start(bf16[2,2,256,1536]{3,2,1,0:T(8,128)(2,1)} %get-tuple-element.99), channel_id=1, source_target_pairs={{0,1},{1,0},{2,3},{3,2},{4,5},{5,4},{6,7},{7,6},{8,9},{9,8},{10,11... | collective-permute-start | bytes 9437192 | tf_op jit(solution)/shard_map/ppermute | solution.py:840
  372.6 18.8 %copy-start = (bf16[2,256,1536]{2,1,0:T(8,128)(2,1)S(1)}, bf16[2,256,1536]{2,1,0:T(8,128)(2,1)}, u32[]{:S(2)}) copy-start(bf16[2,256,1536]{2,1,0:T(8,128)(2,1)} %refs_1_.3) | copy-start | bytes 4718596
  372.6 18.9 %copy-start.3 = (bf16[2,2,256,1536]{3,2,1,0:T(8,128)(2,1)S(1)}, bf16[2,2,256,1536]{3,2,1,0:T(8,128)(2,1)}, u32[]{:S(2)}) copy-start(bf16[2,2,256,1536]{3,2,1,0:T(8,128)(2,1)} %get-tuple-element.96) | copy-start | bytes 9437188
  372.6 18.9 %copy-start.23 = (f32[2,256]{1,0:T(2,128)S(1)}, f32[2,256]{1,0:T(2,128)}, u32[]{:S(2)}) copy-start(f32[2,256]{1,0:T(2,128)} %copy-done.22) | copy-start | bytes 6148
  372.6 18.9 %copy-start.24 = (f32[2,256]{1,0:T(2,128)S(1)}, f32[2,256]{1,0:T(2,128)}, u32[]{:S(2)}) copy-start(f32[2,256]{1,0:T(2,128)} %get-tuple-element.159) | copy-start | bytes 6148
  388.0 8.7 %slice-start = ((s8[4718592]{0:T(1024)(128)(4,1)}), s8[4194304]{0:T(1024)(128)(4,1)S(1)}, s32[]{:S(2)}) async-start(s8[4718592]{0:T(1024)(128)(4,1)} %bitcast.333), calls=%async_computation | async-start | bytes 8388608
  391.5 5.3 slice-start.1
  427.4 4.7 copy-start.14
  427.4 4.7 copy-start.15
  430.3 78.0 %collective-permute-start.31 = (bf16[128,1536]{1,0:T(8,128)(2,1)}, bf16[128,1536]{1,0:T(8,128)(2,1)}, u32[]{:S(2)}, u32[]{:S(2)}) collective-permute-start(bf16[128,1536]{1,0:T(8,128)(2,1)} %get-tuple-element.132), channel_id=1, source_target_pairs={{0,24},{4,28},{8,0},{12,4},{16,8},{20,12},{24,16},{28,20},{1,25},{... | collective-permute-start | bytes 1179656 | tf_op jit(solution)/shard_map/ppermute | solution.py:863
  435.1 2.1 copy-start.6
  438.9 78.7 %collective-permute-start.22 = (bf16[8,2,48,1536]{3,2,0,1:T(8,128)(2,1)}, bf16[8,2,48,1536]{3,2,0,1:T(8,128)(2,1)}, u32[]{:S(2)}, u32[]{:S(2)}) collective-permute-start(bf16[8,2,48,1536]{3,2,0,1:T(8,128)(2,1)} %copy_bitcast_fusion), channel_id=1, source_target_pairs={{0,1},{1,0},{2,3},{3,2},{4,5},{5,4},{6,7},{7,6},{8,9},{9,8},{10,11... | collective-permute-start | bytes 7077896 | tf_op jit(solution)/shard_map/ppermute | solution.py:840
  471.4 10.2 %copy-start.12 = (bf16[8,4,48,1024]{3,2,1,0:T(8,128)(2,1)S(1)}, bf16[8,4,48,1024]{3,2,1,0:T(8,128)(2,1)}, u32[]{:S(2)}) copy-start(bf16[8,4,48,1024]{3,2,1,0:T(8,128)(2,1)} %get-tuple-element.70) | copy-start | bytes 9437188
  471.5 10.2 %copy-start.29 = (bf16[4,2,256,512]{3,2,1,0:T(8,128)(2,1)S(1)}, bf16[4,2,256,512]{3,2,1,0:T(8,128)(2,1)}, u32[]{:S(2)}) copy-start(bf16[4,2,256,512]{3,2,1,0:T(8,128)(2,1)} %get-tuple-element.103) | copy-start | bytes 6291460
  488.8 28.7 %collective-permute-start.30 = (bf16[128,1536]{1,0:T(8,128)(2,1)}, bf16[128,1536]{1,0:T(8,128)(2,1)S(1)}, u32[]{:S(2)}, u32[]{:S(2)}) collective-permute-start(bf16[128,1536]{1,0:T(8,128)(2,1)} %get-tuple-element.133), channel_id=1, source_target_pairs={{0,16},{4,20},{8,24},{12,28},{16,0},{20,4},{24,8},{28,12},{1,17},{... | collective-permute-start | bytes 1179656 | tf_op jit(solution)/shard_map/ppermute | solution.py:863
  488.9 103.2 %collective-permute-start.4 = (bf16[2,2,256,1536]{3,2,1,0:T(8,128)(2,1)S(1)}, bf16[2,2,256,1536]{3,2,1,0:T(8,128)(2,1)S(1)}, u32[]{:S(2)}, u32[]{:S(2)}) collective-permute-start(bf16[2,2,256,1536]{3,2,1,0:T(8,128)(2,1)S(1)} %dynamic-slice_bitcast_fusion), channel_id=1, source_target_pairs={{0,1},{1,0},{2,3},{3,2},{4,5},{5,4},{6,7},{7,6},{8,9},{9,8},{10,11... | collective-permute-start | bytes 9437192 | tf_op jit(solution)/shard_map/ppermute | solution.py:840
  489.0 6.4 copy-start.28
  495.4 6.5 copy-start.10
  495.4 9.3 %copy-start.11 = (bf16[2,2,256,1536]{3,2,1,0:T(8,128)(2,1)S(1)}, bf16[2,2,256,1536]{3,2,1,0:T(8,128)(2,1)}, u32[]{:S(2)}) copy-start(bf16[2,2,256,1536]{3,2,1,0:T(8,128)(2,1)} %get-tuple-element.98) | copy-start | bytes 9437188
  501.9 15.7 %slice-start.2 = ((s8[4718592]{0:T(1024)(128)(4,1)}), s8[4194304]{0:T(1024)(128)(4,1)S(1)}, s32[]{:S(2)}) async-start(s8[4718592]{0:T(1024)(128)(4,1)} %bitcast.337), calls=%async_computation.2 | async-start | bytes 8388608
  503.8 2.8 copy-start.8
  503.8 13.8 %slice-start.3 = ((s8[4718592]{0:T(1024)(128)(4,1)}), s8[524288]{0:T(1024)(128)(4,1)S(1)}, s32[]{:S(2)}) async-start(s8[4718592]{0:T(1024)(128)(4,1)} %bitcast.337), calls=%async_computation.3 | async-start | bytes 1048576
  503.8 15.4 %collective-permute-start.29 = (bf16[128,1536]{1,0:T(8,128)(2,1)}, bf16[128,1536]{1,0:T(8,128)(2,1)S(1)}, u32[]{:S(2)}, u32[]{:S(2)}) collective-permute-start(bf16[128,1536]{1,0:T(8,128)(2,1)} %get-tuple-element.134), channel_id=1, source_target_pairs={{0,8},{4,12},{8,16},{12,20},{16,24},{20,28},{24,0},{28,4},{1,9},{5... | collective-permute-start | bytes 1179656 | tf_op jit(solution)/shard_map/ppermute | solution.py:863
  508.3 17.7 %collective-permute-start.9 = (bf16[4,48,1024]{2,1,0:T(8,128)(2,1)S(1)}, bf16[4,48,1024]{2,1,0:T(8,128)(2,1)S(1)}, u32[]{:S(2)}, u32[]{:S(2)}) collective-permute-start(bf16[4,48,1024]{2,1,0:T(8,128)(2,1)S(1)} %get-tuple-element.138), channel_id=1, source_target_pairs={{0,24},{4,28},{8,0},{12,4},{16,8},{20,12},{24,16},{28,20},{1,25},{... | collective-permute-start | bytes 1179656 | tf_op jit(solution)/shard_map/ppermute | solution.py:863
  517.5 33.8 %collective-permute-start.8 = (bf16[4,48,1024]{2,1,0:T(8,128)(2,1)S(1)}, bf16[4,48,1024]{2,1,0:T(8,128)(2,1)S(1)}, u32[]{:S(2)}, u32[]{:S(2)}) collective-permute-start(bf16[4,48,1024]{2,1,0:T(8,128)(2,1)S(1)} %get-tuple-element.139), channel_id=1, source_target_pairs={{0,16},{4,20},{8,24},{12,28},{16,0},{20,4},{24,8},{28,12},{1,17},{... | collective-permute-start | bytes 1179656 | tf_op jit(solution)/shard_map/ppermute | solution.py:863
  517.5 34.8 %collective-permute-start.7 = (bf16[4,48,1024]{2,1,0:T(8,128)(2,1)S(1)}, bf16[4,48,1024]{2,1,0:T(8,128)(2,1)S(1)}, u32[]{:S(2)}, u32[]{:S(2)}) collective-permute-start(bf16[4,48,1024]{2,1,0:T(8,128)(2,1)S(1)} %get-tuple-element.140), channel_id=1, source_target_pairs={{0,8},{4,12},{8,16},{12,20},{16,24},{20,28},{24,0},{28,4},{1,9},{5... | collective-permute-start | bytes 1179656 | tf_op jit(solution)/shard_map/ppermute | solution.py:863
  519.2 51.8 %collective-permute-start.23 = (bf16[8,48,1536]{2,1,0:T(8,128)(2,1)S(1)}, bf16[8,48,1536]{2,1,0:T(8,128)(2,1)S(1)}, u32[]{:S(2)}, u32[]{:S(2)}) collective-permute-start(bf16[8,48,1536]{2,1,0:T(8,128)(2,1)S(1)} %fusion.10), channel_id=1, source_target_pairs={{0,2},{1,3},{2,0},{3,1},{4,6},{5,7},{6,4},{7,5},{8,10},{9,11},{10,... | collective-permute-start | bytes 3538952 | tf_op jit(solution)/shard_map/ppermute | solution.py:845
  526.0 31.6 %collective-permute-start.18 = (bf16[4,4,48,512]{3,2,1,0:T(8,128)(2,1)S(1)}, bf16[4,4,48,512]{3,2,1,0:T(8,128)(2,1)S(1)}, u32[]{:S(2)}, u32[]{:S(2)}) collective-permute-start(bf16[4,4,48,512]{3,2,1,0:T(8,128)(2,1)S(1)} %dynamic-slice_bitcast_fusion.4), channel_id=1, source_target_pairs={{0,4},{4,0},{8,12},{12,8},{16,20},{20,16},{24,28},{28,24},{1,5},{5... | collective-permute-start | bytes 2359304 | tf_op jit(solution)/shard_map/ppermute | solution.py:854
  551.3 19.5 %collective-permute-start.14 = (bf16[4,4,48,512]{3,2,1,0:T(8,128)(2,1)S(1)}, bf16[4,4,48,512]{3,2,1,0:T(8,128)(2,1)S(1)}, u32[]{:S(2)}, u32[]{:S(2)}) collective-permute-start(bf16[4,4,48,512]{3,2,1,0:T(8,128)(2,1)S(1)} %dynamic-slice_bitcast_fusion.5), channel_id=1, source_target_pairs={{0,4},{4,0},{8,12},{12,8},{16,20},{20,16},{24,28},{28,24},{1,5},{5... | collective-permute-start | bytes 2359304 | tf_op jit(solution)/shard_map/ppermute | solution.py:854
  552.3 49.6 %collective-permute-start.3 = (bf16[2,256,1536]{2,1,0:T(8,128)(2,1)S(1)}, bf16[2,256,1536]{2,1,0:T(8,128)(2,1)S(1)}, u32[]{:S(2)}, u32[]{:S(2)}) collective-permute-start(bf16[2,256,1536]{2,1,0:T(8,128)(2,1)S(1)} %fusion.14), channel_id=1, source_target_pairs={{0,2},{1,3},{2,0},{3,1},{4,6},{5,7},{6,4},{7,5},{8,10},{9,11},{10,... | collective-permute-start | bytes 4718600 | tf_op jit(solution)/shard_map/ppermute | solution.py:845
  557.9 16.6 %collective-permute-start.19 = (bf16[4,48,512]{2,1,0:T(8,128)(2,1)S(1)}, bf16[4,48,512]{2,1,0:T(8,128)(2,1)S(1)}, u32[]{:S(2)}, u32[]{:S(2)}) collective-permute-start(bf16[4,48,512]{2,1,0:T(8,128)(2,1)S(1)} %get-tuple-element.141), channel_id=1, source_target_pairs={{0,8},{4,12},{8,16},{12,20},{16,24},{20,28},{24,0},{28,4},{1,9},{5... | collective-permute-start | bytes 589832 | tf_op jit(solution)/shard_map/ppermute | solution.py:863
  570.8 7.3 %collective-permute-start.21 = (bf16[4,48,512]{2,1,0:T(8,128)(2,1)S(1)}, bf16[4,48,512]{2,1,0:T(8,128)(2,1)S(1)}, u32[]{:S(2)}, u32[]{:S(2)}) collective-permute-start(bf16[4,48,512]{2,1,0:T(8,128)(2,1)S(1)} %get-tuple-element.142), channel_id=1, source_target_pairs={{0,24},{4,28},{8,0},{12,4},{16,8},{20,12},{24,16},{28,20},{1,25},{... | collective-permute-start | bytes 589832 | tf_op jit(solution)/shard_map/ppermute | solution.py:863
  571.0 19.7 %collective-permute-start.20 = (bf16[4,48,512]{2,1,0:T(8,128)(2,1)S(1)}, bf16[4,48,512]{2,1,0:T(8,128)(2,1)S(1)}, u32[]{:S(2)}, u32[]{:S(2)}) collective-permute-start(bf16[4,48,512]{2,1,0:T(8,128)(2,1)S(1)} %get-tuple-element.143), channel_id=1, source_target_pairs={{0,16},{4,20},{8,24},{12,28},{16,0},{20,4},{24,8},{28,12},{1,17},{... | collective-permute-start | bytes 589832 | tf_op jit(solution)/shard_map/ppermute | solution.py:863
  574.4 18.1 %collective-permute-start.15 = (bf16[4,48,512]{2,1,0:T(8,128)(2,1)S(1)}, bf16[4,48,512]{2,1,0:T(8,128)(2,1)S(1)}, u32[]{:S(2)}, u32[]{:S(2)}) collective-permute-start(bf16[4,48,512]{2,1,0:T(8,128)(2,1)S(1)} %get-tuple-element.144), channel_id=1, source_target_pairs={{0,8},{4,12},{8,16},{12,20},{16,24},{20,28},{24,0},{28,4},{1,9},{5... | collective-permute-start | bytes 589832 | tf_op jit(solution)/shard_map/ppermute | solution.py:863
  578.2 14.4 %collective-permute-start.17 = (bf16[4,48,512]{2,1,0:T(8,128)(2,1)S(1)}, bf16[4,48,512]{2,1,0:T(8,128)(2,1)S(1)}, u32[]{:S(2)}, u32[]{:S(2)}) collective-permute-start(bf16[4,48,512]{2,1,0:T(8,128)(2,1)S(1)} %get-tuple-element.145), channel_id=1, source_target_pairs={{0,24},{4,28},{8,0},{12,4},{16,8},{20,12},{24,16},{28,20},{1,25},{... | collective-permute-start | bytes 589832 | tf_op jit(solution)/shard_map/ppermute | solution.py:863
  590.8 11.2 %collective-permute-start.24 = (bf16[4,48,1536]{2,1,0:T(8,128)(2,1)S(1)}, bf16[4,48,1536]{2,1,0:T(8,128)(2,1)S(1)}, u32[]{:S(2)}, u32[]{:S(2)}) collective-permute-start(bf16[4,48,1536]{2,1,0:T(8,128)(2,1)S(1)} %dynamic-slice_bitcast_fusion.6), channel_id=1, source_target_pairs={{0,4},{4,0},{8,12},{12,8},{16,20},{20,16},{24,28},{28,24},{1,5},{5... | collective-permute-start | bytes 1769480 | tf_op jit(solution)/shard_map/ppermute | solution.py:854
  592.1 9.0 %collective-permute-start.16 = (bf16[4,48,512]{2,1,0:T(8,128)(2,1)S(1)}, bf16[4,48,512]{2,1,0:T(8,128)(2,1)S(1)}, u32[]{:S(2)}, u32[]{:S(2)}) collective-permute-start(bf16[4,48,512]{2,1,0:T(8,128)(2,1)S(1)} %get-tuple-element.146), channel_id=1, source_target_pairs={{0,16},{4,20},{8,24},{12,28},{16,0},{20,4},{24,8},{28,12},{1,17},{... | collective-permute-start | bytes 589832 | tf_op jit(solution)/shard_map/ppermute | solution.py:863
  592.5 58.2 %collective-permute-start.13 = (bf16[4,48,1024]{2,1,0:T(8,128)(2,1)S(1)}, bf16[4,48,1024]{2,1,0:T(8,128)(2,1)S(1)}, u32[]{:S(2)}, u32[]{:S(2)}) collective-permute-start(bf16[4,48,1024]{2,1,0:T(8,128)(2,1)S(1)} %get-tuple-element.135), channel_id=1, source_target_pairs={{0,24},{4,28},{8,0},{12,4},{16,8},{20,12},{24,16},{28,20},{1,25},{... | collective-permute-start | bytes 1179656 | tf_op jit(solution)/shard_map/ppermute | solution.py:863
  592.6 55.3 %collective-permute-start.5 = (bf16[2,256,1536]{2,1,0:T(8,128)(2,1)S(1)}, bf16[2,256,1536]{2,1,0:T(8,128)(2,1)S(1)}, u32[]{:S(2)}, u32[]{:S(2)}) collective-permute-start(bf16[2,256,1536]{2,1,0:T(8,128)(2,1)S(1)} %fusion.5), channel_id=1, source_target_pairs={{0,2},{1,3},{2,0},{3,1},{4,6},{5,7},{6,4},{7,5},{8,10},{9,11},{10,... | collective-permute-start | bytes 4718600 | tf_op jit(solution)/shard_map/ppermute | solution.py:845
  602.1 20.2 %collective-permute-start.25 = (bf16[48,1536]{1,0:T(8,128)(2,1)S(1)}, bf16[48,1536]{1,0:T(8,128)(2,1)S(1)}, u32[]{:S(2)}, u32[]{:S(2)}) collective-permute-start(bf16[48,1536]{1,0:T(8,128)(2,1)S(1)} %get-tuple-element.147), channel_id=1, source_target_pairs={{0,8},{4,12},{8,16},{12,20},{16,24},{20,28},{24,0},{28,4},{1,9},{5... | collective-permute-start | bytes 442376 | tf_op jit(solution)/shard_map/ppermute | solution.py:863
  610.8 11.4 %collective-permute-start.27 = (bf16[48,1536]{1,0:T(8,128)(2,1)S(1)}, bf16[48,1536]{1,0:T(8,128)(2,1)S(1)}, u32[]{:S(2)}, u32[]{:S(2)}) collective-permute-start(bf16[48,1536]{1,0:T(8,128)(2,1)S(1)} %get-tuple-element.148), channel_id=1, source_target_pairs={{0,24},{4,28},{8,0},{12,4},{16,8},{20,12},{24,16},{28,20},{1,25},{... | collective-permute-start | bytes 442376 | tf_op jit(solution)/shard_map/ppermute | solution.py:863
  613.9 33.9 %copy-start.1 = (bf16[2,256,1536]{2,1,0:T(8,128)(2,1)S(1)}, bf16[2,256,1536]{2,1,0:T(8,128)(2,1)}, u32[]{:S(2)}) copy-start(bf16[2,256,1536]{2,1,0:T(8,128)(2,1)} %refs_0_.1) | copy-start | bytes 4718596
  613.9 33.1 %collective-permute-start.26 = (bf16[48,1536]{1,0:T(8,128)(2,1)S(1)}, bf16[48,1536]{1,0:T(8,128)(2,1)S(1)}, u32[]{:S(2)}, u32[]{:S(2)}) collective-permute-start(bf16[48,1536]{1,0:T(8,128)(2,1)S(1)} %get-tuple-element.149), channel_id=1, source_target_pairs={{0,16},{4,20},{8,24},{12,28},{16,0},{20,4},{24,8},{28,12},{1,17},{... | collective-permute-start | bytes 442376 | tf_op jit(solution)/shard_map/ppermute | solution.py:863
  622.2 32.5 %collective-permute-start.12 = (bf16[4,48,1024]{2,1,0:T(8,128)(2,1)S(1)}, bf16[4,48,1024]{2,1,0:T(8,128)(2,1)S(1)}, u32[]{:S(2)}, u32[]{:S(2)}) collective-permute-start(bf16[4,48,1024]{2,1,0:T(8,128)(2,1)S(1)} %get-tuple-element.136), channel_id=1, source_target_pairs={{0,16},{4,20},{8,24},{12,28},{16,0},{20,4},{24,8},{28,12},{1,17},{... | collective-permute-start | bytes 1179656 | tf_op jit(solution)/shard_map/ppermute | solution.py:863
  622.2 32.5 %collective-permute-start.11 = (bf16[4,48,1024]{2,1,0:T(8,128)(2,1)S(1)}, bf16[4,48,1024]{2,1,0:T(8,128)(2,1)S(1)}, u32[]{:S(2)}, u32[]{:S(2)}) collective-permute-start(bf16[4,48,1024]{2,1,0:T(8,128)(2,1)S(1)} %get-tuple-element.137), channel_id=1, source_target_pairs={{0,8},{4,12},{8,16},{12,20},{16,24},{20,28},{24,0},{28,4},{1,9},{5... | collective-permute-start | bytes 1179656 | tf_op jit(solution)/shard_map/ppermute | solution.py:863
  647.9 2.8 copy-start.4
  676.6 3.9 copy-start.19
  676.7 4.5 copy-start.21
  680.5 2.6 copy-start.20
  683.2 9.1 %copy-start.2 = (bf16[2,256,1536]{2,1,0:T(8,128)(2,1)S(1)}, bf16[2,256,1536]{2,1,0:T(8,128)(2,1)}, u32[]{:S(2)}) copy-start(bf16[2,256,1536]{2,1,0:T(8,128)(2,1)} %refs_0_.1) | copy-start | bytes 4718596
  683.2 9.1 %copy-start.5 = (bf16[2,256,1536]{2,1,0:T(8,128)(2,1)S(1)}, bf16[2,256,1536]{2,1,0:T(8,128)(2,1)}, u32[]{:S(2)}) copy-start(bf16[2,256,1536]{2,1,0:T(8,128)(2,1)} %copy-done.4) | copy-start | bytes 4718596
  (2 other events, 1.9 us)

commit v3 on v2

--- a/solution.py
+++ b/solution.py
@@ -61,6 +61,12 @@
     def ctx_dev(self, y, k):
         return (self.d, y * 2 + k)
 
+    def slot(self, y, rel):
+        return y + self.z.ys if rel else y * 2 + self.k
+
+    def slot_across(self, y, rel):
+        return y if rel else y * 2 + self.k
+
     def ctx_peers(self):
         n = self.z.ctx
         return [lax.rem(self.c + j, n) for j in range(1, n)]
@@ -81,10 +87,17 @@
     def dp_dev(self, o, i):
         return (o * self.z.inner + i, self.c)
 
-    def barrier(self):
+    def barrier(self, core_only=False):
         devices = [(self.d, c) for c in self.ctx_peers()]
+        if core_only:
+            devices = [self.ctx_dev(self.y, 1 - self.k)]
+            self.signal_all(devices)
+            return
         devices += [self.dp_dev(self.outer_to(j), self.i) for j in range(1, self.z.outer)]
         devices += [self.dp_dev(self.o, self.inner_to(j)) for j in range(1, self.z.inner)]
+        self.signal_all(devices)
+
+    def signal_all(self, devices):
         barrier = pltpu.get_barrier_semaphore()
         for device in devices:
             pl.semaphore_signal(barrier, inc=1, device_id=device, device_id_type=MESH)
@@ -163,22 +176,23 @@
     )(*ins)
 
 
-def gather_ctx_start(link, src, buf, wait_src=None):
-    slot = buf.at[link.c]
+def gather_ctx_start(link, src, buf, rel=False):
     ways = []
+    slot = buf.at[link.slot(link.y, rel)]
     for j in range(1, link.z.ys):
         to = lax.rem(link.y + j, link.z.ys)
         frm = lax.rem(link.y + link.z.ys - j, link.z.ys)
         ways.append((frm, link.put(src, slot, link.ctx_dev(to, link.k))))
-    link.put(src, slot, link.ctx_dev(link.y, 1 - link.k))
+    link.put(src, buf.at[link.slot_across(link.y, rel)], link.ctx_dev(link.y, 1 - link.k))
     return ways
 
 
-def gather_ctx_forward(link, buf, ways):
+def gather_ctx_forward(link, buf, ways, rel=False):
     for frm, copy in ways:
         link.arrived(copy)
-        slot = buf.at[frm * 2 + link.k]
-        link.put(slot, slot, link.ctx_dev(link.y, 1 - link.k))
+        link.put(
+            buf.at[link.slot(frm, rel)], buf.at[link.slot_across(frm, rel)], link.ctx_dev(link.y, 1 - link.k)
+        )
 
 
 def exchange_ctx(link, pack, slot_of):
@@ -210,8 +224,8 @@
         link.put(src.at[:, to], dst.at[j - 1], link.dp_dev(link.o, to))
 
 
-def scatter_outer(link, src, dst):
-    for j in range(1, link.z.outer):
+def scatter_outer(link, src, dst, js):
+    for j in js:
         to = link.outer_to(j)
         link.put(src.at[to], dst.at[j - 1], link.dp_dev(to, link.i))
 
@@ -294,36 +308,33 @@
     )(*args, *moved, *filled)
 
 
-def own_outer(link, buf, js):
-    for j in js:
-        link.put(buf.at[link.d], buf.at[link.d], link.dp_dev(link.outer_to(j), link.i))
-
-
-def own_inner(link, buf):
+def ring_outer(link, slot_of, step):
+    slot = slot_of(link.outer_from(step - 1) * link.z.inner + link.i)
+    return link.put(slot, slot, link.dp_dev(link.outer_to(1), link.i))
+
+
+def pass_inner(link, slot_of, step):
+    slot = slot_of(link.outer_from(step) * link.z.inner + link.i)
     for j in range(1, link.z.inner):
-        link.put(buf.at[link.d], buf.at[link.d], link.dp_dev(link.o, link.inner_to(j)))
-
-
-def pass_inner(link, buf, js):
-    for from_j in js:
-        slot = buf.at[link.outer_from(from_j) * link.z.inner + link.i]
-        for j in range(1, link.z.inner):
-            link.put(slot, slot, link.dp_dev(link.o, link.inner_to(j)))
+        link.put(slot, slot, link.dp_dev(link.o, link.inner_to(j)))
 
 
 def pass_core(link, buf, parts):
     for j in range(1, link.z.ys):
-        at = lax.rem(link.y + link.z.ys - j, link.z.ys) * 2 + link.k
+        at = lax.rem(link.y + link.z.ys - j, link.z.ys)
         for part in parts:
-            link.put(buf.at[at, part], buf.at[at, part], link.ctx_dev(link.y, 1 - link.k))
+            src, dst = buf.at[link.slot(at, True), part], buf.at[link.slot_across(at, True), part]
+            link.put(src, dst, link.ctx_dev(link.y, 1 - link.k))
 
 
 def own_y(link, src, buf, parts):
     for part in parts:
+        slot = buf.at[link.slot(link.y, True), part]
         for j in range(1, link.z.ys):
             to = lax.rem(link.y + j, link.z.ys)
-            link.put(src.at[part], buf.at[link.c, part], link.ctx_dev(to, link.k))
-        link.put(src.at[part], buf.at[link.c, part], link.ctx_dev(link.y, 1 - link.k))
+            link.put(src.at[part], slot, link.ctx_dev(to, link.k))
+        slot = buf.at[link.slot_across(link.y, True), part]
+        link.put(src.at[part], slot, link.ctx_dev(link.y, 1 - link.k))
 
 
 def rotated(u, cos, sin):
@@ -500,16 +511,18 @@
                 dkv_ref[b, 0, :, at : at + LANES] = dv_acc[b, :, here].astype(BF)
 
 
-def attend_back_call(z, q, k, v, qdoc, kdoc, o, do, lse, cos, sin, hc, kvc):
+def attend_back_call(z, q, k, v, qdoc, kdoc, o, do, lse, cos, sin, hc, kvc, script, moved, new, filled):
     ctx, m, r, _ = q.shape
     row = lambda b, s: (s, b, 0, 0)
     seq = lambda b, s: (0, b, 0, 0)
     table = pl.BlockSpec((ctx, r, LANES), lambda b, s: (0, 0, 0))
-    return pl.pallas_call(
+    return fused_call(
+        z,
+        "attend_back",
+        14,
         functools.partial(attend_back_kernel, hc, kvc, ctx),
-        name="attend_back",
-        grid=(m, ctx),
-        in_specs=[
+        (m, ctx),
+        [
             pl.BlockSpec((1, 1, r, hc * LANES), row),
             pl.BlockSpec((ctx, 1, r, kvc * LANES), seq),
             pl.BlockSpec((ctx, 1, r, kvc * LANES), seq),
@@ -521,23 +534,164 @@
             table,
             table,
         ],
-        out_specs=[
+        [
             pl.BlockSpec((1, 1, r, hc * LANES), row),
             pl.BlockSpec((ctx, 1, r, 2 * kvc * LANES), seq),
         ],
-        out_shape=[sds((ctx, m, r, hc * LANES)), sds((ctx, m, r, 2 * kvc * LANES))],
-        scratch_shapes=[
-            pltpu.VMEM((ctx, r, kvc * LANES), F32),
-            pltpu.VMEM((ctx, r, kvc * LANES), F32),
+        [sds((ctx, m, r, hc * LANES)), sds((ctx, m, r, 2 * kvc * LANES))],
+        (q, k, v, qdoc, kdoc, o, do, lse, cos, sin),
+        script,
+        moved,
+        new,
+        filled,
+        [pltpu.VMEM((ctx, r, kvc * LANES), F32), pltpu.VMEM((ctx, r, kvc * LANES), F32)],
+    )
+
+
+def mix_kernel(ctx, att_ref, x_ref, gain_ref, w_ref, mid_ref, normed_ref, rows_ref):
+    rows = jnp.concatenate([att_ref[c, 0] for c in range(ctx)], axis=1)
+    rows_ref[0] = rows
+    mid = x_ref[0].astype(F32) + dot_nn(rows, w_ref[...])
+    mid_ref[0] = mid
+    scale = lax.rsqrt(jnp.mean(mid * mid, axis=-1, keepdims=True) + EPS)
+    normed_ref[0] = (mid * scale * gain_ref[...]).astype(BF)
+
+
+def mix_call(z, att, x, gain, w, script, moved, new, filled):
+    ctx, m, r, cols = att.shape
+    d = x.shape[-1]
+    seq = pl.BlockSpec((1, r, d), lambda b: (b, 0, 0))
+    whole = lambda b: (0, 0)
+    return fused_call(
+        z,
+        "mix",
+        16,
+        functools.partial(mix_kernel, ctx),
+        (m,),
+        [
+            pl.BlockSpec((ctx, 1, r, cols), lambda b: (0, b, 0, 0)),
+            seq,
+            pl.BlockSpec((1, d), whole),
+            pl.BlockSpec(w.shape, whole, pipeline_mode=pl.Buffered(1)),
         ],
-        compiler_params=pltpu.CompilerParams(vmem_limit_bytes=VMEM_LIMIT),
-    )(q, k, v, qdoc, kdoc, o, do, lse, cos, sin)
+        [seq, seq, seq],
+        [sds((m, r, d), F32), sds((m, r, d)), sds((m, r, d))],
+        (att, x, gain, w),
+        script,
+        moved,
+        new,
+        filled,
+    )
+
+
+def turn_kernel(z, dn_ref, *refs):
+    came_refs = refs[: z.ys - 1]
+    mid_ref, cot_ref, gain_ref, w_ref = refs[z.ys - 1 : z.ys + 3]
+    d_mid_ref, low_ref, all_ref, hold, send_sems, recv_sems, own_sems = refs[z.ys + 3 :]
+    b, last = pl.program_id(0), pl.num_programs(0) - 1
+    link = Link(z, send_sems, recv_sems, own_sems)
+    cols = hold.shape[-1]
+
+    def copies(n):
+        remote = [
+            pltpu.make_async_remote_copy(
+                src_ref=hold.at[p, n],
+                dst_ref=all_ref.at[link.c, n],
+                send_sem=send_sems.at[n, j],
+                recv_sem=recv_sems.at[n, j],
+                device_id=(link.d, p),
+                device_id_type=MESH,
+            )
+            for j, p in enumerate(link.ctx_peers())
+        ]
+        return remote, pltpu.make_async_copy(hold.at[link.c, n], all_ref.at[link.c, n], own_sems.at[n])
+
+    d_normed = dn_ref[link.y, 0].astype(F32)
+    for ref in came_refs:
+        d_normed += ref[0].astype(F32)
+    mid = mid_ref[0]
+    scale = lax.rsqrt(jnp.mean(mid * mid, axis=-1, keepdims=True) + EPS)
+    e = d_normed * gain_ref[...]
+    d_mid = cot_ref[0].astype(F32) + (
+        scale * e - mid * (scale * scale * scale) * jnp.mean(e * mid, axis=-1, keepdims=True)
+    )
+    d_mid_ref[0] = d_mid
+    low = d_mid.astype(BF)
+    low_ref[0] = low
+    d_att = dot_nt(low, w_ref[...]).astype(BF)
+    for c in range(z.ctx):
+        hold[c, b] = d_att[:, c * cols : (c + 1) * cols]
+    remote, own = copies(b)
+    for copy in remote:
+        copy.start()
+    own.start()
+
+    @pl.when(b == last)
+    def _():
+        for n in range(hold.shape[1]):
+            remote, own = copies(n)
+            for copy in remote:
+                copy.wait_recv()
+            for copy in remote:
+                copy.wait_send()
+            own.wait()
+
+
+def turn_call(z, dn, came, mid, cot, gain, w, cols, script, moved, new, filled):
+    ys, m, r, d = dn.shape
+    seq = pl.BlockSpec((1, r, d), lambda b: (b, 0, 0))
+    whole = lambda b: (0, 0)
+    return fused_call(
+        z,
+        "turn",
+        6,
+        functools.partial(turn_kernel, z),
+        (m,),
+        [pl.BlockSpec((ys, 1, r, d), lambda b: (0, b, 0, 0))]
+        + [seq] * (ys + 1)
+        + [pl.BlockSpec((1, d), whole), pl.BlockSpec(w.shape, whole, pipeline_mode=pl.Buffered(1))],
+        [seq, seq, pl.BlockSpec(memory_space=pltpu.HBM)],
+        [sds((m, r, d), F32), sds((m, r, d)), sds((z.ctx, m, r, cols))],
+        (dn, *came, mid, cot, gain, w),
+        script,
+        moved,
+        new,
+        filled,
+        [
+            pltpu.VMEM((z.ctx, m, r, cols), BF),
+            pltpu.SemaphoreType.DMA((m, z.ctx)),
+            pltpu.SemaphoreType.DMA((m, z.ctx)),
+            pltpu.SemaphoreType.DMA((m,)),
+        ],
+    )
 
 
 def mlp_kernel(
-    k_ref, x_ref, cot_ref, gate_ref, up_ref, down_ref,
-    hid_ref, dg_ref, du_ref, dn_other, dn_mine, out_other, out_mine,
+    z, x_ref, cot_ref, gate_ref, up_ref, down_ref,
+    hid_ref, dg_ref, du_ref, dn_ref, out_ref,
+    dn_send, dn_got, out_send, out_got, send_sems, recv_sems,
 ):
+    other, y, b = pl.program_id(0) == 0, pl.program_id(1), pl.program_id(2)
+    link = Link(z, send_sems, recv_sems, None)
+    at = y * pl.num_programs(2) + b
+
+    def copies(n):
+        return [
+            pltpu.make_async_remote_copy(
+                src_ref=src.at[n],
+                dst_ref=dst.at[n],
+                send_sem=send_sems.at[which, n],
+                recv_sem=recv_sems.at[which, n],
+                device_id=link.ctx_dev(link.y, 1 - link.k),
+                device_id_type=MESH,
+            )
+            for which, (src, dst) in enumerate(((dn_send, dn_got), (out_send, out_got)))
+        ]
+
+    @pl.when(other & (at == 0))
+    def _():
+        link.barrier(core_only=True)
+
     x, cot = x_ref[0, 0], cot_ref[0, 0]
     gate, up = dot_nn(x, gate_ref[...]), dot_nn(x, up_ref[...])
     d_hidden = dot_nt(cot, down_ref[...])
@@ -549,48 +703,187 @@
     d_up = (d_hidden * act).astype(BF)
     dg_ref[0, 0] = d_gate
     du_ref[0, 0] = d_up
-    out = dot_nn(hidden, down_ref[...]).astype(BF)
-    dn = (dot_nt(d_gate, gate_ref[...]) + dot_nt(d_up, up_ref[...])).astype(BF)
-
-    @pl.when(pl.program_id(0) == 0)
+    out = dot_nn(hidden, down_ref[...])
+    dn = dot_nt(d_gate, gate_ref[...]) + dot_nt(d_up, up_ref[...])
+
+    @pl.when(other)
     def _():
-        out_other[0, 0] = out
-        dn_other[0, 0] = dn
-
-    @pl.when(pl.program_id(0) == 1)
+        dn_send[at] = dn.astype(BF)
+        out_send[at] = out.astype(BF)
+        for copy in copies(at):
+            copy.start()
+
+    @pl.when(jnp.logical_not(other))
     def _():
-        out_mine[0, 0] = out
-        dn_mine[0, 0] = dn
-
-
-def mlp_call(z, core, x, cot, gate, up, down):
+        for copy in copies(at):
+            copy.wait_recv()
+        dn_ref[0, 0] = (dn + dn_got[at].astype(F32)).astype(BF)
+        out_ref[0, 0] = (out + out_got[at].astype(F32)).astype(BF)
+        for copy in copies(at):
+            copy.wait_send()
+
+
+def mlp_call(z, x, cot, gate, up, down):
     ctx, m, r, d = x.shape
     f = down.shape[0]
-    row = lambda a, y, b, k: (y * 2 + a * k[0] + (1 - a) * (1 - k[0]), b, 0, 0)
-    whole = lambda a, y, b, k: (0, 0)
-    other = lambda a, y, b, k: (y + a * (z.ys - 1 - y), b + a * (m - 1 - b), 0, 0)
-    mine = lambda a, y, b, k: (a * y, a * b, 0, 0)
+    row = lambda a, y, b: (a * z.ys + y, b, 0, 0)
+    whole = lambda a, y, b: (0, 0)
+    mine = lambda a, y, b: (a * y, a * b, 0, 0)
     block = lambda width, at: pl.BlockSpec((1, 1, r, width), at)
-    part = sds((z.ys, m, r, d))
+    resident = lambda w: pl.BlockSpec(w.shape, whole, pipeline_mode=pl.Buffered(1))
+    held = pltpu.VMEM((z.ys * m, r, d), BF)
     return pl.pallas_call(
-        mlp_kernel,
+        functools.partial(mlp_kernel, z),
         name="mlp",
-        grid_spec=pltpu.PrefetchScalarGridSpec(
-            num_scalar_prefetch=1,
-            grid=(2, z.ys, m),
-            in_specs=[
-                block(d, row),
-                block(d, row),
-                pl.BlockSpec(gate.shape, whole, pipeline_mode=pl.Buffered(1)),
-                pl.BlockSpec(up.shape, whole, pipeline_mode=pl.Buffered(1)),
-                pl.BlockSpec(down.shape, whole, pipeline_mode=pl.Buffered(1)),
-            ],
-            out_specs=[block(f, row), block(f, row), block(f, row)]
-            + [block(d, other), block(d, mine), block(d, other), block(d, mine)],
+        grid=(2, z.ys, m),
+        in_specs=[block(d, row), block(d, row), resident(gate), resident(up), resident(down)],
+        out_specs=[block(f, row), block(f, row), block(f, row), block(d, mine), block(d, mine)],
+        scratch_shapes=[held] * 4
+        + [pltpu.SemaphoreType.DMA((2, z.ys * m)), pltpu.SemaphoreType.DMA((2, z.ys * m))],
+        out_shape=[sds((ctx, m, r, f))] * 3 + [sds((z.ys, m, r, d))] * 2,
+        compiler_params=pltpu.CompilerParams(
+            collective_id=13, has_side_effects=True, vmem_limit_bytes=VMEM_LIMIT
         ),
-        out_shape=[sds((ctx, m, r, f))] * 3 + [part] * 4,
-        compiler_params=pltpu.CompilerParams(vmem_limit_bytes=VMEM_LIMIT),
-    )(core, x, cot, gate, up, down)
+    )(x, cot, gate, up, down)
+
+
+def tail_kernel(
+    z, da_ref, q_ref, kv_ref, po_ref, up_ref, gate_ref,
+    da_out, q_out, kv_out, po_out, gate_out, up_out,
+    da_mine, da_got, da_send, da_came, q_x, q_col, q_z, kv_x, kv_col, kv_z, po_x, po_col, po_z,
+    up_mine, up_z, mine_q, mine_kv, mine_up, send_sems, recv_sems, local_sems,
+):
+    link = Link(z, send_sems, recv_sems, local_sems)
+    link.landed = []
+    link.barrier()
+    peer = link.ctx_dev(link.y, 1 - link.k)
+    far = list(range(1, z.outer))
+    order = [j for j in far if j in (1, z.outer - 1)] + [j for j in far if j not in (1, z.outer - 1)]
+    wide = lambda a: a.astype(F32)
+
+    core = link.put(da_ref.at[:, 1 - link.k], da_got, peer)
+    scatter = lambda src, dst: [
+        link.put(src.at[:, link.inner_to(j)], dst.at[j - 1], link.dp_dev(link.o, link.inner_to(j)))
+        for j in range(1, z.inner)
+    ]
+    x_ways = [(q_ref, q_x, q_col, q_z, scatter(q_ref, q_x)), (kv_ref, kv_x, kv_col, kv_z, scatter(kv_ref, kv_x))]
+    po_way = (po_ref, po_x, po_col, po_z, scatter(po_ref, po_x))
+    up_ways = []
+    near = [j for j in order if j in (1, z.outer - 1)]
+    rest = [j for j in order if j not in near]
+
+    def outer_put(src, dst, j):
+        to = link.outer_to(j)
+        return link.put(src.at[to], dst.at[j - 1], link.dp_dev(to, link.i))
+
+    up_ways += [outer_put(up_ref, up_z, j) for j in near]
+    load = link.keep(da_ref.at[:, link.k], da_mine)
+    load_up = link.keep(up_ref.at[link.o], up_mine)
+    link.keep(gate_ref.at[link.c], gate_out.at[link.c])
+    exchange_ctx(link, gate_ref, lambda s: gate_out.at[s])
+
+    link.arrived(core)
+    load.wait()
+    load_up.wait()
+    link.local = [copy for copy in link.local if copy is not load and copy is not load_up]
+    rows = 32 if da_mine.shape[2] % 32 == 0 else da_mine.shape[2]
+    count = da_mine.shape[2] // rows
+    seqs = da_mine.shape[1]
+
+    def add_core(step, _):
+        b, at = lax.div(step, count), pl.ds(pl.multiple_of(lax.rem(step, count) * rows, rows), rows)
+        for j in range(z.ys):
+            y = lax.rem(link.y + j, z.ys)
+            total = wide(da_mine[y, b, at]) + wide(da_got[y, b, at])
+            if j == 0:
+                da_out[b, at] = total
+            else:
+                da_send[j - 1, b, at] = total.astype(BF)
+        return 0
+
+    lax.fori_loop(0, seqs * count, add_core, 0)
+    y_ways = []
+    for j in range(1, z.ys):
+        to = lax.rem(link.y + j, z.ys)
+        y_ways.append(link.put(da_send.at[j - 1], da_came.at[j - 1], link.ctx_dev(to, link.k)))
+
+    def columns(way):
+        part, came, col, got, copies = way
+        for copy in copies:
+            link.arrived(copy)
+        for o in range(z.outer):
+            total = wide(part[o, link.i])
+            for j in range(z.inner - 1):
+                total += wide(came[j, o])
+            col[o] = total.astype(BF)
+        return [outer_put(col, got, j) for j in order]
+
+    z_ways = [columns(way) for way in x_ways]
+    z_ways.append(columns(po_way))
+    up_ways += [outer_put(up_ref, up_z, j) for j in rest]
+
+    def close(col, got, copies):
+        for copy in copies:
+            link.arrived(copy)
+        total = wide(col)
+        for j in range(z.outer - 1):
+            total += wide(got[j])
+        return total
+
+    for way, copies, mine, out in zip(x_ways, z_ways, (mine_q, mine_kv), (q_out, kv_out)):
+        mine[...] = close(way[2][link.o], way[3], copies).astype(BF)
+        exchange_ctx(link, mine, lambda s: out.at[s])
+        link.keep(mine.at[link.c], out.at[link.c])
+    for copy in y_ways:
+        link.arrived(copy)
+
+    def add_y(step, _):
+        b, at = lax.div(step, count), pl.ds(pl.multiple_of(lax.rem(step, count) * rows, rows), rows)
+        total = da_out[b, at]
+        for j in range(z.ys - 1):
+            total += wide(da_came[j, b, at])
+        da_out[b, at] = total
+        return 0
+
+    lax.fori_loop(0, seqs * count, add_y, 0)
+    po_out[...] = close(po_col[link.o], po_z, z_ways[2])
+    mine_up[...] = close(up_mine[...], up_z, up_ways).astype(BF)
+    exchange_ctx(link, mine_up, lambda s: up_out.at[s])
+    link.keep(mine_up.at[link.c], up_out.at[link.c])
+    link.finish()
+
+
+def tail_call(z, da, part_q, part_kv, po, up_col, gate_mine):
+    ys, _, m, r, d = da.shape
+    one = lambda a: a.shape[2:]
+    grown = lambda n, a: (n,) + tuple(a)
+    q1, kv1, po1, up1 = one(part_q), one(part_kv), one(po), up_col.shape[1:]
+    vm = lambda shape: pltpu.VMEM(tuple(shape), BF)
+    hbm, vmem = pl.BlockSpec(memory_space=pltpu.HBM), pl.BlockSpec(memory_space=pltpu.VMEM)
+    scratch = [vm((ys, m, r, d)), vm((ys, m, r, d)), vm((ys - 1, m, r, d)), vm((ys - 1, m, r, d))]
+    for shape in (q1, kv1, po1):
+        scratch += [vm((z.inner - 1, z.outer) + shape), vm((z.outer,) + shape), vm((z.outer - 1,) + shape)]
+    scratch += [vm(up1), vm((z.outer - 1,) + up1), vm(q1), vm(kv1), vm(up1)]
+    scratch += [
+        pltpu.SemaphoreType.DMA((64,)),
+        pltpu.SemaphoreType.DMA((64,)),
+        pltpu.SemaphoreType.DMA((16,)),
+    ]
+
+    def body(da, q, kv, po, up, gate, *rest):
+        tail_kernel(z, da, q, kv, po, up, gate, *rest)
+
+    return pl.pallas_call(
+        body,
+        name="tail",
+        in_specs=[hbm, vmem, vmem, vmem, hbm, hbm],
+        out_specs=[vmem, hbm, hbm, vmem, hbm, hbm],
+        out_shape=[sds((m, r, d), F32), sds(q1), sds(kv1), sds(po1, F32), sds(gate_mine.shape), sds(up1)],
+        scratch_shapes=scratch,
+        compiler_params=pltpu.CompilerParams(
+            collective_id=15, has_side_effects=True, vmem_limit_bytes=VMEM_LIMIT
+        ),
+    )(da, part_q, part_kv, po, up_col, gate_mine)
 
 
 def pad_heads(w, heads, split):
@@ -650,9 +943,9 @@
     gains = jnp.stack([gain_attn, gain_ffn]).astype(F32)
     gains = jnp.pad(gains, ((0, 6), (0, LANES - rows)))
 
-    far = list(range(1, outer))
-    near = [j for j in far if j in (1, outer - 1)]
-    mid_way = [j for j in far if j not in near]
+    steps = list(range(1, outer))
+    by_owner = lambda buf: lambda s: buf.at[s]
+    out_slot = lambda link, buf: lambda s: buf.at[s, :, link.k]
 
     def first_script(link, ins, outs, scratch):
         x, seg, qkv, gain, wo, pg, pu, wd = ins
@@ -675,32 +968,33 @@
         ]
         ways_x = gather_ctx_start(link, x, x_all)
         exchange_ctx(link, pg, lambda s: g_gate.at[link.d, s])
-        exchange_ctx(link, pu, lambda s: g_up.at[link.d, s])
         for copy in a2a:
             link.arrived(copy)
         for copy in mine:
             copy.wait()
         link.local = []
-        small = [lambda s: g_qkv.at[s], lambda s: g_gain.at[s]]
-        ways = [gather_dp_start(link, slot) for slot in small]
-        for copy in over_y:
-            link.arrived(copy)
-        out_slot = lambda s: g_out.at[s, :, link.k]
-        ways_out = gather_dp_start(link, out_slot)
+        small = [by_owner(g_qkv), by_owner(g_gain)]
+        ways = [ring_outer(link, slot, 1) for slot in small]
+        for slot in small:
+            pass_inner(link, slot, 0)
+        link.keep(pg.at[link.c], g_gate.at[link.d, link.c])
+        link.keep(pu.at[link.c], g_up.at[link.d, link.c])
+        link.keep(wd, g_down.at[link.d])
         load.wait()
         store = pltpu.make_async_copy(hold, x_all.at[link.c], link.sems[2].at[14])
         store.start()
-        link.keep(pg.at[link.c], g_gate.at[link.d, link.c])
-        link.keep(pu.at[link.c], g_up.at[link.d, link.c])
-        link.keep(wd, g_down.at[link.d])
-        for slot, way in zip(small, ways):
-            gather_dp_forward(link, slot, way)
+        for step in steps:
+            came, ways = ways, []
+            for copy, slot in zip(came, small):
+                link.arrived(copy)
+                if step < steps[-1]:
+                    ways.append(ring_outer(link, slot, step + 1))
+                pass_inner(link, slot, step)
+        for copy in over_y:
+            link.arrived(copy)
+        ring_outer(link, out_slot(link, g_out), 1)
+        pass_inner(link, out_slot(link, g_out), 0)
         gather_ctx_forward(link, x_all, ways_x)
-        gather_dp_forward(link, out_slot, ways_out)
-        for copy in list(link.inflight):
-            link.arrived(copy)
-        both = g_out.at[:, :, link.k]
-        link.put(both, both, link.ctx_dev(link.y, 1 - link.k))
         store.wait()
 
     x_all, seg_all, g_qkv, g_gain, g_out, g_gate, g_up, g_down = communicate(
@@ -724,54 +1018,61 @@
     gain_a = g_gain[:, :, 0, :rows].reshape(1, d)
     gain_f = g_gain[:, :, 1, :rows].reshape(1, d)
     wqkv = g_qkv.reshape(d, width)
-    wo = g_out.reshape(d, d)
     cos, sin = rope_tables(ctx, r)
     qdoc = seg_all.reshape(ctx, m, r, 1)
     kdoc = seg_all.reshape(ctx, m, 1, r)
     early, late = range(m // 2), range(m // 2, m)
 
     def qkv_cargo(cargo, moved, bufs):
-        (cot,), (g_gate, g_up, cot_all) = moved, bufs
+        (cot, pu), (g_out, g_gate, g_up, cot_all) = moved, bufs
+        exchange_ctx(cargo, pu, lambda s: g_up.at[cargo.d, s])
         own_y(cargo, cot, cot_all, early)
-        for buf in (g_gate, g_up):
-            own_outer(cargo, buf, near[:1])
-            own_inner(cargo, buf)
-
-    g_gate, g_up, cot_all, normed_a, q, k, v = qkv_call(
+        for slot, step in ((out_slot(cargo, g_out), 2), (by_owner(g_gate), 1)):
+            ring_outer(cargo, slot, step)
+            pass_inner(cargo, slot, step - 1)
+
+    g_out, g_gate, g_up, cot_all, normed_a, q, k, v = qkv_call(
         z, x_all, gain_a, wqkv, cos, sin, hc, kvc,
-        qkv_cargo, (cotangent,), (sds((ctx, m, r, d)),), (g_gate, g_up),
+        qkv_cargo, (cotangent, pack_up), (sds((ctx, m, r, d)),), (g_out, g_gate, g_up),
     )
 
     def attend_cargo(cargo, moved, bufs):
-        (cot,), (g_gate, g_up, cot_all) = moved, bufs
+        (cot,), (g_out, g_gate, g_up, cot_all) = moved, bufs
         own_y(cargo, cot, cot_all, late)
         pass_core(cargo, cot_all, early)
-        for buf in (g_gate, g_up):
-            own_outer(cargo, buf, near[1:])
-            pass_inner(cargo, buf, near[:1])
-
-    g_gate, g_up, cot_all, att, lse = attend_call(
-        z, q, k, v, qdoc, kdoc, hc, kvc, attend_cargo, (cotangent,), (), (g_gate, g_up, cot_all)
+        for slot, step in ((out_slot(cargo, g_out), 3), (by_owner(g_gate), 2), (by_owner(g_up), 1)):
+            ring_outer(cargo, slot, step)
+            pass_inner(cargo, slot, step - 1)
+
+    g_out, g_gate, g_up, cot_all, att, lse = attend_call(
+        z, q, k, v, qdoc, kdoc, hc, kvc, attend_cargo, (cotangent,), (), (g_out, g_gate, g_up, cot_all)
     )
 
     def second_script(link, ins, outs, scratch):
         att, cot = ins[:2]
-        g_gate, g_up, g_down, cot_all, att_all = outs
+        g_out, g_gate, g_up, cot_all, att_all = outs
         (hold,) = scratch
         load = pltpu.make_async_copy(cot, hold, link.sems[2].at[15])
         load.start()
         link.keep(att.at[link.c], att_all.at[link.c])
+        first = len(link.inflight)
+        pass_inner(link, out_slot(link, g_out), 3)
+        last_out = link.inflight[first:]
         exchange_ctx(link, att, lambda s: att_all.at[s])
-        own_outer(link, g_down, near)
-        for buf in (g_gate, g_up):
-            pass_inner(link, buf, near[1:])
+        for slot, step in ((by_owner(g_gate), 3), (by_owner(g_up), 2)):
+            ring_outer(link, slot, step)
+        pass_inner(link, by_owner(g_gate), 2)
         pass_core(link, cot_all, late)
         load.wait()
-        store = pltpu.make_async_copy(hold, cot_all.at[link.c], link.sems[2].at[14])
+        store = pltpu.make_async_copy(hold, cot_all.at[link.slot(link.y, True)], link.sems[2].at[14])
         store.start()
+        for copy in last_out:
+            link.arrived(copy)
+        both = g_out.at[:, :, link.k]
+        link.put(both, both, link.ctx_dev(link.y, 1 - link.k))
         store.wait()
 
-    g_gate, g_up, g_down, cot_all, att_all = communicate(
+    g_out, g_gate, g_up, cot_all, att_all = communicate(
         z,
         "exchange_heads",
         2,
@@ -779,39 +1080,45 @@
         (att, cotangent),
         (sds(att.shape),),
         [pltpu.VMEM((m, r, d), BF)],
-        (g_gate, g_up, g_down, cot_all),
-    )
-
-    att_rows = att_all.transpose(1, 2, 0, 3).reshape(m * r, H * HD)
+        (g_out, g_gate, g_up, cot_all),
+    )
+    wo = g_out.reshape(d, d)
+
+    def mix_cargo(cargo, moved, bufs):
+        g_gate, g_up, g_down = bufs
+        ring_outer(cargo, by_owner(g_up), 3)
+        ring_outer(cargo, by_owner(g_down), 1)
+        pass_inner(cargo, by_owner(g_gate), 3)
+        pass_inner(cargo, by_owner(g_up), 1)
+
+    g_gate, g_up, g_down, mid, normed, att_rows = mix_call(
+        z, att_all, inputs, gain_f, wo, mix_cargo, (), (), (g_gate, g_up, g_down)
+    )
+    att_rows = att_rows.reshape(m * r, H * HD)
     residual = inputs.astype(F32)
-    mid = residual + dot_nn(att_rows, wo).reshape(m, r, d)
-    scale_f = lax.rsqrt(jnp.mean(mid * mid, axis=-1, keepdims=True) + EPS)
-    normed = (mid * scale_f * gain_f).astype(BF)
 
     def third_script(link, ins, outs, scratch):
-        x, (g_gate, g_up, g_down, x_all), (hold,) = ins[0], outs, scratch
+        x, (g_up, g_down, x_all), (hold,) = ins[0], outs, scratch
         load = pltpu.make_async_copy(x, hold, link.sems[2].at[15])
         load.start()
-        ways = gather_ctx_start(link, x, x_all)
-        bufs = (g_gate, g_up, g_down)
-        coming = []
-        for buf in bufs:
-            for j in mid_way:
-                start = link.put(buf.at[link.d], buf.at[link.d], link.dp_dev(link.outer_to(j), link.i))
-                coming.append((buf, j, start))
-        own_inner(link, g_down)
-        pass_inner(link, g_down, near)
+        ways = gather_ctx_start(link, x, x_all, True)
+        way = ring_outer(link, by_owner(g_down), 2)
+        pass_inner(link, by_owner(g_down), 1)
+        pass_inner(link, by_owner(g_up), 2)
         load.wait()
-        store = pltpu.make_async_copy(hold, x_all.at[link.c], link.sems[2].at[14])
+        store = pltpu.make_async_copy(hold, x_all.at[link.slot(link.y, True)], link.sems[2].at[14])
         store.start()
-        for n, (buf, j, copy) in enumerate(coming):
-            if n == len(coming) - 1:
-                gather_ctx_forward(link, x_all, ways)
-            link.arrived(copy)
-            pass_inner(link, buf, [j])
+        link.arrived(way)
+        way = ring_outer(link, by_owner(g_down), 3)
+        pass_inner(link, by_owner(g_down), 0)
+        pass_inner(link, by_owner(g_up), 3)
+        pass_inner(link, by_owner(g_down), 2)
+        link.arrived(way)
+        pass_inner(link, by_owner(g_down), 3)
+        gather_ctx_forward(link, x_all, ways, True)
         store.wait()
 
-    g_gate, g_up, g_down, normed_all = communicate(
+    g_up, g_down, normed_all = communicate(
         z,
         "gather_third",
         3,
@@ -819,14 +1126,11 @@
         (normed,),
         (sds((ctx, m, r, d)),),
         [pltpu.VMEM((m, r, d), BF)],
-        (g_gate, g_up, g_down),
+        (g_up, g_down),
     )
     w_gate_c, w_up_c, w_down_c = g_gate.reshape(d, f), g_up.reshape(d, f), g_down.reshape(f, d)
 
-    core = ki.astype(jnp.int32).reshape(1)
-    hidden, d_gate, d_up, dn_other, dn_mine, out_other, out_mine = mlp_call(
-        z, core, normed_all, cot_all, w_gate_c, w_up_c, w_down_c
-    )
+    hidden, d_gate, d_up, dn_pair, out_pair = mlp_call(z, normed_all, cot_all, w_gate_c, w_up_c, w_down_c)
 
     dp_perm = lambda fn: [(o * inner + i, fn(o, i)) for o in range(outer) for i in range(inner)]
     ctx_perm = lambda fn: [(y * 2 + k, fn(y, k)) for y in range(ys) for k in range(2)]
@@ -839,15 +1143,13 @@
     def to_core(a):
         return lax.ppermute(a, "ctx", ctx_perm(lambda y, k: y * 2 + 1 - k))
 
-    def to_y(mine, got, dim=0):
-        both = lambda at: wide(dyn(mine, at, dim)) + wide(dyn(got, at, dim))
-        came = [
+    def to_y(pair):
+        return [
             lax.ppermute(
-                both((yi + j) % ys).astype(BF), "ctx", ctx_perm(lambda y, k: (y + j) % ys * 2 + k)
+                dyn(pair, (yi + j) % ys, 0), "ctx", ctx_perm(lambda y, k: (y + j) % ys * 2 + k)
             )
             for j in range(1, ys)
         ]
-        return both(yi), came
 
     def to_inner(part):
         return [
@@ -857,87 +1159,79 @@
             for j in range(1, inner)
         ]
 
-    def to_outer(part, came):
-        both = lambda at: wide(part[at, ii]) + sum(wide(dyn(a, at, 0)) for a in came)
-        got = [
-            lax.ppermute(
-                both((oi + j) % outer).astype(BF), "dp", dp_perm(lambda o, i: (o + j) % outer * inner + i)
-            )
-            for j in range(1, outer)
-        ]
-        return both(oi), got
-
-    close = lambda own, came: own + sum(wide(a) for a in came)
-
-    dn_got = to_core(dn_other)
+    column = lambda part, came: (wide(dyn(part, ii, 1)) + sum(wide(a) for a in came)).astype(BF)
+    close = lambda own, came: wide(own) + sum(wide(a) for a in came)
+
+    dn_came = to_y(dn_pair)
     part_down = dot_tn(flat(hidden), flat(cot_all)).astype(BF).reshape(outer, inner, frows, d)
     down_x = to_inner(part_down)
-    dn_own, dn_came = to_y(dn_mine, dn_got)
     shape_g = (outer, inner, ctx, rows, f)
     part_gate = dot_tn(flat(normed_all), flat(d_gate)).astype(BF).reshape(shape_g)
     gate_x = to_inner(part_gate)
-    part_up = dot_tn(flat(normed_all), flat(d_up)).astype(BF).reshape(shape_g)
-    up_x = to_inner(part_up)
-    out_got = to_core(out_other)
-
-    d_normed = close(dn_own, dn_came)
-    cot32 = cotangent.astype(F32)
-    e = d_normed * gain_f
-    d_mid = cot32 + (
-        scale_f * e - mid * (scale_f * scale_f * scale_f) * jnp.mean(e * mid, axis=-1, keepdims=True)
-    )
-    d_mid_low = d_mid.astype(BF).reshape(m * r, d)
-    d_att = dot_nt(d_mid_low, wo).astype(BF)
-    d_att = d_att.reshape(m, r, ctx, hc * HD).transpose(2, 0, 1, 3)
-
-    def fourth_script(link, ins, outs, scratch):
-        link.keep(ins[0].at[link.c], outs[0].at[link.c])
-        exchange_ctx(link, ins[0], lambda s: outs[0].at[s])
-
-    (d_att_all,) = communicate(z, "exchange_back", 6, fourth_script, (d_att,), (sds(d_att.shape),))
-
-    part_out = dot_tn(att_rows, d_mid_low).astype(BF).reshape(dp, ys, 2, rows, d)
-    po_got = to_core(dyn(part_out, 1 - ki, 2))
-    down_own, down_z = to_outer(part_down, after(down_x, d_att))
-    gate_own, gate_z = to_outer(part_gate, after(gate_x, d_att_all))
-    out_own, out_came = to_y(after(out_mine, d_att_all), out_got)
-    dq, dkv = attend_back_call(z, q, k, v, qdoc, kdoc, att, d_att_all, lse, cos, sin, hc, kvc)
-
-    part_q = dot_tn(flat(normed_a), flat(dq)).astype(BF).reshape(outer, inner, ctx, rows, hc * LANES)
-    q_x = to_inner(part_q)
-    part_kv = dot_tn(flat(normed_a), flat(dkv)).astype(BF).reshape(outer, inner, ctx, rows, 2 * kvc * LANES)
-    kv_x = to_inner(part_kv)
+    part_up = dot_tn(flat(normed_all), flat(after(d_up, part_gate))).astype(BF).reshape(shape_g)
+    near = [j for j in steps if j in (1, outer - 1)]
+    mid_way = [j for j in steps if j not in near]
+    down_col = column(part_down, after(down_x, part_up))
+
+    def turn_cargo(cargo, moved, bufs):
+        scatter_outer(cargo, moved[0], bufs[0], near)
+
+    down_z, d_mid, d_mid_low, d_att_all = turn_call(
+        z, dn_pair, dn_came, mid, cotangent, gain_f, wo, hc * HD,
+        turn_cargo, (down_col,), (sds((outer - 1, frows, d)),), (),
+    )
+
+    part_out = dot_tn(att_rows, d_mid_low.reshape(m * r, d)).astype(BF).reshape(dp, ys, 2, rows, d)
+    gate_col = column(part_gate, after(gate_x, d_att_all))
+
+    def back_cargo(cargo, moved, bufs):
+        (down_col, gate_col, part_up, part_out), (down_z, gate_z, up_x, po_in) = moved, bufs
+        scatter_inner(cargo, part_up, up_x)
+        scatter_outer(cargo, down_col, down_z, mid_way)
+        scatter_outer(cargo, gate_col, gate_z, near)
+        cargo.put(part_out.at[:, :, 1 - cargo.k], po_in, cargo.ctx_dev(cargo.y, 1 - cargo.k))
+
+    down_z, gate_z, up_x, po_in, dq, dkv = attend_back_call(
+        z, q, k, v, qdoc, kdoc, att, d_att_all, lse, cos, sin, hc, kvc,
+        back_cargo,
+        (down_col, gate_col, part_up, part_out),
+        (
+            sds((outer - 1,) + gate_col.shape[1:]),
+            sds((inner - 1, outer) + gate_col.shape[1:]),
+            sds((dp, ys, rows, d)),
+        ),
+        (down_z,),
+    )
+    po_both = lambda at: wide(dyn(dyn(part_out, ki, 2), at, 1)) + wide(dyn(po_in, at, 1))
+    po_came = [
+        lax.ppermute(
+            po_both((yi + j) % ys).astype(BF), "ctx", ctx_perm(lambda y, k: (y + j) % ys * 2 + k)
+        )
+        for j in range(1, ys)
+    ]
+    gate_far = [
+        lax.ppermute(
+            dyn(after(gate_col, dq), (oi + j) % outer, 0), "dp", dp_perm(lambda o, i: (o + j) % outer * inner + i)
+        )
+        for j in mid_way
+    ]
+    out_came = to_y(after(out_pair, po_came))
     da = dot_nt(flat(dq), wqkv[:, : hc * LANES]) + dot_nt(flat(dkv), wqkv[:, hc * LANES :])
     da = da.astype(BF).reshape(ys, 2, m, r, d)
-    da_own, da_came = to_y(dyn(da, ki, 1), to_core(dyn(da, 1 - ki, 1)))
-    up_own, up_z = to_outer(part_up, after(up_x, dq))
-    po_own, po_came = to_y(dyn(after(part_out, dq), ki, 2), po_got, 1)
-    q_own, q_z = to_outer(part_q, q_x)
-    kv_own, kv_z = to_outer(part_kv, kv_x)
-    po = close(po_own, po_came).astype(BF).reshape(outer, inner, rows, d)
-    po_own, po_z = to_outer(po, to_inner(po))
-    outputs = mid + close(out_own, after(out_came, dq))
-    grad_down = close(down_own, after(down_z, part_kv))
-    gate_mine = close(gate_own, after(gate_z, part_kv)).astype(BF)
-    up_mine = close(up_own, after(up_z, da_own)).astype(BF)
-    d_normed_a = close(da_own, da_came)
+    part_q = dot_tn(flat(normed_a), flat(dq)).astype(BF).reshape(outer, inner, ctx, rows, hc * LANES)
+    part_kv = dot_tn(flat(normed_a), flat(dkv)).astype(BF).reshape(outer, inner, ctx, rows, 2 * kvc * LANES)
+    up_col = column(part_up, [up_x[j] for j in range(inner - 1)])
+    po = close(po_both(yi), after(po_came, part_kv)).astype(BF).reshape(outer, inner, rows, d)
+    gate_near = [gate_z[j - 1] for j in near]
+    gate_mine = close(dyn(gate_col, oi, 0), gate_near + gate_far).astype(BF)
+
+    d_normed_a, q_all, kv_all, grad_out, gate_all, up_all = tail_call(z, da, part_q, part_kv, po, up_col, gate_mine)
+    grad_down = close(dyn(down_col, oi, 0), [down_z[j - 1] for j in steps])
+    outputs = mid + close(dyn(out_pair, yi, 0), out_came)
     scale_a = lax.rsqrt(jnp.mean(residual * residual, axis=-1, keepdims=True) + EPS)
     e = d_normed_a * gain_a
     input_grad = d_mid + (
         scale_a * e - residual * (scale_a * scale_a * scale_a) * jnp.mean(e * residual, axis=-1, keepdims=True)
-    )
-    q_mine = close(q_own, q_z).astype(BF)
-    kv_mine = close(kv_own, kv_z).astype(BF)
-    grad_out = close(po_own, po_z)
-
-    def seventh_script(link, ins, outs, scratch):
-        for src, dst in zip(ins, outs):
-            link.keep(src.at[link.c], dst.at[link.c])
-            exchange_ctx(link, src, lambda s: dst.at[s])
-
-    last = (gate_mine, up_mine, q_mine, kv_mine)
-    gate_all, up_all, q_all, kv_all = communicate(
-        z, "reduce_last", 9, seventh_script, last, [sds(a.shape) for a in last]
     )
     spread = lambda a: wide(a).reshape(ctx, rows, dp, frows).transpose(1, 2, 0, 3).reshape(rows, ff)
     grad_gate, grad_up = spread(gate_all), spread(up_all)

time: 705 us -> 596 us (0.85)
  waiting for transfers between devices: 109 us -> 15.5 us
  Pallas kernels: 357 us -> 434 us
  starting transfers between devices: 42.2 us -> 7.42 us
  other arithmetic: 59.2 us -> 35.9 us
  local copies, waits for them, and re-layouts: 55.2 us -> 31.9 us
  matrix products: 73.7 us -> 62.8 us
    ppermute x26 -> x4, waiting for transfers between devices: 100 us -> 0.01 us  [the longest x2 0.01 us: to_y(): lax.ppermute(dyn(pair, (yi + j) % ys, 0), 'ctx', ctx_perm(lambda y, k: (y...]
    pallas_call x2 -> x5, Pallas kernels: 57.8 us -> 152 us  [fused_call(): pl.pallas_call(kernel, name=name, grid=grid, in_specs=list(in_specs) + [h...]
    pallas_call x5 -> x3, Pallas kernels: 216 us -> 137 us  [communicate(): pl.pallas_call(kernel, name=name, out_shape=list(outs), in_specs=[hbm] *...]
    pallas_call x2, Pallas kernels: 83.3 us -> 145 us  [the longest x1 93.5 us: tail_call(): pl.pallas_call(body, name='tail', in_specs=[hbm, vmem, vmem, vmem, hbm, h...]
    ppermute x26 -> x4, starting transfers between devices: 37 us -> 5.12 us  [the longest x2 3.06 us: to_y(): lax.ppermute(dyn(pair, (yi + j) % ys, 0), 'ctx', ctx_perm(lambda y, k: (y...]
    convert_element_type x17 -> x6, other arithmetic: 27.4 us -> 13.9 us  [the longest x3 8.05 us: per_device(): (wide(dyn(part, ii, 1)) + sum((wide(a) for a in came))).astype(BF)]
    unnamed x72 -> x66, local copies, waits for them, and re-layouts: 9.78 us -> 2.5 us
    ppermute x6 -> x2, waiting for transfers between devices: 8.79 us -> 15.5 us  [to_inner(): lax.ppermute(dyn(part, (ii + j) % inner, 1), 'dp', dp_perm(lambda o, i: o...]
  transfers between devices with their start and end apart: 32 -> 6, of which waited for: 11 -> 2; matrix products, arithmetic and copies ran while one was open for 18% -> 16% of each run, Pallas kernels for 7% -> 20%
where the time goes in v3:
time: 596 us; the launch traced here: 590 us
  Pallas kernels  434 us (73%)
  matrix products  62.8 us (11%)
  other arithmetic  35.9 us (6%)
  local copies, waits for them, and re-layouts  31.9 us (5%)
  waiting for transfers between devices  15.5 us (3%)
  starting transfers between devices  7.42 us (1%)
    pallas_call x5, Pallas kernels, fused_call(): pl.pallas_call(kernel, name=name, grid=grid, in_specs=list(in_specs) + [h...  152 us
    pallas_call x3, Pallas kernels, communicate(): pl.pallas_call(kernel, name=name, out_shape=list(outs), in_specs=[hbm] *...  137 us
    pallas_call x1, Pallas kernels, tail_call(): pl.pallas_call(body, name='tail', in_specs=[hbm, vmem, vmem, vmem, hbm, h...  93.5 us
    pallas_call x1, Pallas kernels, mlp_call(): pl.pallas_call(functools.partial(mlp_kernel, z), name='mlp', grid=(2, z.y...  51.2 us
    dot_general x6, matrix products, dot_tn(): lax.dot_general(a, b, (((0,), (0,)), ((), ())), preferred_element_type=F32)  45.3 us
    dot_general x2, matrix products, dot_nt(): lax.dot_general(a, b, (((1,), (1,)), ((), ())), preferred_element_type=F32)  17.5 us
    ppermute x2, waiting for transfers between devices, to_inner(): lax.ppermute(dyn(part, (ii + j) % inner, 1), 'dp', dp_perm(lambda o, i: o...  15.5 us
  transfers between devices with their start and end apart: 6, of which 2 were waited for; matrix products, arithmetic and copies ran while one was open for 16% of the time, Pallas kernels for 20%

profile of v3, /device:TPU:0, one launch (start us, length us, event | category | flops | bytes accessed | tf_op | source)
XLA Modules:
  0.0 589.5 jit_solution(8746644693714337963)
XLA Ops:
  0.7 1.1 reshape.239
  1.9 1.1 reshape.238
  3.5 1.3 reshape.237
  5.8 0.9 reshape.241.refs_5_
  7.1 0.9 reshape.243.refs_6_
  8.0 1.9 multiply_sine_fusion
  9.9 1.0 pad_maximum_fusion
  11.6 0.8 maximum_bitcast_fusion.refs_2_
  12.4 61.3 %gather_first.1 = (bf16[4,2,256,1536]{3,2,1,0:T(8,128)(2,1)}, s32[4,2,256]{2,1,0:T(2,128)}, bf16[8,4,48,1024]{3,2,1,0:T(8,128)(2,1)}, f32[8,4,8,128]{3,2,1,0:T(8...) custom-call(bf16[2,256,1536]{2,1,0:T(8,128)(2,1)} %refs_1_.5, ...), custom_call_target="tpu_custom_call" | custom-call | tf_op jit(solution)/shard_map/gather_first/pallas_call | solution.py:160
  73.7 1.3 reshape.248.refs_4_
  75.0 1.6 slice_reduce_fusion
  76.6 0.7 reshape_squeeze.7.refs_2_.refs_4_
  78.0 2.1 copy.62.refs_3_
  80.1 1.0 pad_maximum_fusion.1
  81.1 28.7 %qkv.1 = (bf16[8,2,2,48,1536]{4,3,2,1,0:T(8,128)(2,1)}, bf16[8,4,48,1024]{3,2,1,0:T(8,128)(2,1)}, bf16[8,4,48,1024]{3,2,1,0:T(8,128)(2,1)}, bf16[4,2,256,1536]{3...) custom-call(bf16[4,2,256,1536]{3,2,1,0:T(8,128)(2,1)} %get-tuple-ele, ...), custom_call_target="tpu_custom_call", output_to_operand_aliasing={{0}: (7, {}), {1}: (8, {}), {2}: (9, {})} | custom-call | tf_op jit(solution)/shard_map/qkv/pallas_call | solution.py:296
  109.8 30.3 %attend.1 = (bf16[8,2,2,48,1536]{4,3,2,1,0:T(8,128)(2,1)}, bf16[8,4,48,1024]{3,2,1,0:T(8,128)(2,1)}, bf16[8,4,48,1024]{3,2,1,0:T(8,128)(2,1)}, bf16[4,2,256,1536...) custom-call(bf16[4,2,256,512]{3,2,1,0:T(8,128)(2,1)} %get-tuple-elem, ...), custom_call_target="tpu_custom_call", output_to_operand_aliasing={{0}: (6, {}), {1}: (7, {}), {2}: (8, {}), {3}: (9, {})} | custom-call | tf_op jit(solution)/shard_map/attend/pallas_call | solution.py:296
  140.1 21.8 %exchange_heads.1 = (bf16[8,2,2,48,1536]{4,3,2,1,0:T(8,128)(2,1)}, bf16[8,4,48,1024]{3,2,1,0:T(8,128)(2,1)}, bf16[8,4,48,1024]{3,2,1,0:T(8,128)(2,1)}, bf16[4,2,...) custom-call(bf16[4,2,256,384]{3,2,1,0:T(8,128)(2,1)} %get-tuple-elem, ...), custom_call_target="tpu_custom_call", output_to_operand_aliasing={{0}: (2, {}), {1}: (3, {}), {2}: (4, {}), {3}: (5, {})} | custom-call | tf_op jit(solution)/shard_map/exchange_heads/pallas_call | solution.py:160
  161.9 26.6 %mix.1 = (bf16[8,4,48,1024]{3,2,1,0:T(8,128)(2,1)}, bf16[8,4,48,1024]{3,2,1,0:T(8,128)(2,1)}, bf16[8,128,1536]{2,1,0:T(8,128)(2,1)}, f32[2,256,1536]{2,1,0:T(8,1...) custom-call(bf16[4,2,256,384]{3,2,1,0:T(8,128)(2,1)} %get-tuple-elem, ...), custom_call_target="tpu_custom_call", output_to_operand_aliasing={{0}: (4, {}), {1}: (5, {}), {2}: (6, {})} | custom-call | tf_op jit(solution)/shard_map/mix/pallas_call | solution.py:296
  188.5 54.3 %gather_third.1 = (bf16[8,4,48,1024]{3,2,1,0:T(8,128)(2,1)}, bf16[8,128,1536]{2,1,0:T(8,128)(2,1)}, bf16[4,2,256,1536]{3,2,1,0:T(8,128)(2,1)}) custom-call(bf16[2,256,1536]{2,1,0:T(8,128)(2,1)} %get-tuple-element.99.refs_0_, bf16[8,4,48,1024]{3,2,1,0:T(8,128)(2,1)} %get-tuple-element.100.refs_1_, ...), custom_call_target="tpu_custom_call", output_to_operand_aliasing={{0}: (1, {}), {1}: (2, {})} | custom-call | tf_op jit(solution)/shard_map/gather_third/pallas_call | solution.py:160
  242.8 51.2 %mlp.1 = (bf16[4,2,256,1024]{3,2,1,0:T(8,128)(2,1)}, bf16[4,2,256,1024]{3,2,1,0:T(8,128)(2,1)}, bf16[4,2,256,1024]{3,2,1,0:T(8,128)(2,1)}, bf16[2,2,256,1536]{3,2,1,0:T(8,128)(2,1)}, bf16[2,2,256,1536]{3,2,1,0:T(8,128)(2,1)}) custom-call(bf16[4,2,256,1536]{3,2,1,0:T(8,128)(2,1)} %get-tuple-element.102.x_ref, ...), custom_call_target="tpu_custom_call" | custom-call | tf_op jit(solution)/shard_map/mlp/pallas_call | solution.py:735
  294.1 2.7 dynamic-slice_bitcast_fusion.3
  296.8 1.5 collective-permute-start
  298.2 10.4 %bitcast_convert_fusion.3 = bf16[1024,1536]{1,0:T(8,128)(2,1)S(1)} fusion(bf16[4,2,256,1024]{3,2,1,0:T(8,128)(2,1)} %get-tuple-element.110, bf16[4,2,256,1536]{3,2,1,0:T(8,128)(2,1)} %get-tuple-element.103.cot_ref), kind=kOutput, calls=%fused_computation.4 | convolution fusion | flops 6444023808 | bytes 13631488 | tf_op jit(solution)/shard_map/dot_general | solution.py:40
  308.7 1.4 dynamic-slice_bitcast_fusion.2
  310.0 1.5 collective-permute-start.1
  311.5 10.1 %bitcast_convert_fusion.2 = bf16[1536,1024]{1,0:T(8,128)(2,1)S(1)} fusion(bf16[4,2,256,1536]{3,2,1,0:T(8,128)(2,1)} %get-tuple-element.102.x_ref, bf16[4,2,256,1024]{3,2,1,0:T(8,128)(2,1)} %get-tuple-element.112), kind=kOutput, calls=%fused_computation.3 | convolution fusion | flops 6444023808 | bytes 13631488 | tf_op jit(solution)/shard_map/dot_general | solution.py:40
  321.6 1.4 dynamic-slice_bitcast_fusion.1
  323.0 0.8 collective-permute-start.2
  323.8 0.8 mul.109
  324.6 11.4 %bitcast_convert_fusion.1 = bf16[1536,1024]{1,0:T(8,128)(2,1)} fusion(bf16[4,2,256,1536]{3,2,1,0:T(8,128)(2,1)} %get-tuple-element.102.x_ref, bf16[4,2,256,1024]{3,2,1,0:T(8,128)(2,1)} %get-tuple-element.113), kind=kOutput, calls=%fused_computation.2 | convolution fusion | flops 6444023808 | bytes 13631488 | tf_op jit(solution)/shard_map/dot_general | solution.py:40
  336.0 11.6 %collective-permute-done.1 = bf16[4,128,1536]{2,1,0:T(8,128)(2,1)} collective-permute-done((bf16[4,128,1536]{2,1,0:T(8,128)(2,1)}, bf16[4,128,1536]{2,1,0:T(8,128)(2,1)}, u32[]{:S(2)}, u32[]{:S(2)}) %collective-permute-start.1) | collective-permute-done | bytes 1572896 | tf_op jit(solution)/shard_map/ppermute | solution.py:1156
  347.6 2.9 fusion.7.refs_6_.refs_10_
  350.5 26.1 %turn.1 = (bf16[3,128,1536]{2,1,0:T(8,128)(2,1)}, f32[2,256,1536]{2,1,0:T(8,128)}, bf16[2,256,1536]{2,1,0:T(8,128)(2,1)}, bf16[4,2,256,384]{3,2,1,0:T(8,128)(2,1)}) custom-call(bf16[2,2,256,1536]{3,2,1,0:T(8,128)(2,1)} %get-tuple-element.109.refs_0_, bf16[2,256,1536]{2,1,0:T(8,128)(2,1)} %collective-permute-done.refs_1_, ...), custom_call_target="tpu_custom_call" | custom-call | tf_op jit(solution)/shard_map/turn/pallas_call | solution.py:296
  376.6 3.9 collective-permute-done.2
  380.5 3.3 fusion.6.refs_11_
  383.8 4.3 bitcast_convert_fusion
  388.1 40.5 %attend_back.1 = (bf16[3,128,1536]{2,1,0:T(8,128)(2,1)}, bf16[3,4,48,1024]{3,2,1,0:T(8,128)(2,1)}, bf16[1,4,4,48,1024]{4,3,2,1,0:T(8,128)(2,1)}, bf16[8,2,48,153...) custom-call(bf16[4,2,256,512]{3,2,1,0:T(8,128)(2,1)} %get-tuple-elem, ...), custom_call_target="tpu_custom_call", output_to_operand_aliasing={{0}: (14, {})} | custom-call | tf_op jit(solution)/shard_map/attend_back/pallas_call | solution.py:296
  428.6 1.6 collective-permute-start.5
  430.2 2.1 fusion.13
  432.8 8.2 %fusion.15 = f32[2048,1536]{1,0:T(8,128)} fusion(bf16[2048,512]{1,0:T(8,128)(2,1)} %bitcast.196, bf16[1536,1024]{1,0:T(8,128)(2,1)S(1)} %bitcast.171), kind=kOutput, calls=%fused_computation.31 | convolution fusion | flops 3221225472 | bytes 16252928 | tf_op jit(solution)/shard_map/dot_general | solution.py:36
  441.1 4.6 fusion.10
  445.6 9.2 %add_convert_fusion = bf16[2048,1536]{1,0:T(8,128)(2,1)} fusion(f32[2048,1536]{1,0:T(8,128)} %fusion.15, bf16[2048,512]{1,0:T(8,128)(2,1)} %bitcast.197, bf16[1536,1024]{1,0:T(8,128)(2,1)S(1)} %bitcast.172), kind=kOutput, calls=%fused_computation | convolution fusion | flops 3227516928 | bytes 22544384 | tf_op jit(solution)/shard_map/dot_general | solution.py:36
  454.9 4.6 fusion.9
  459.5 2.2 add_bitcast_fusion
  461.7 1.9 fusion.5.up
  463.6 1.0 fusion.17.gate
  464.6 1.2 dynamic-slice_bitcast_fusion
  465.8 1.6 collective-permute-start.4
  467.4 2.7 fusion.12
  470.1 93.5 %tail.1 = (f32[2,256,1536]{2,1,0:T(8,128)}, bf16[4,48,512]{2,1,0:T(8,128)(2,1)}, bf16[4,48,512]{2,1,0:T(8,128)(2,1)}, f32[48,1536]{1,0:T(8,128)}, bf16[4,48,1024...) custom-call(bf16[2,2,2,256,1536]{4,3,2,1,0:T(8,128)(2,1)} %bitcast.164, bf16[4,2,4,48,512]{4,3,2,1,0:T(8,128)(2,1)} %bitcast.180, ...), custom_call_target="tpu_custom_call" | custom-call | tf_op jit(solution)/shard_map/tail/pallas_call | solution.py:876
  563.6 1.2 reshape.263
  564.8 1.0 fusion.25
  566.2 0.8 reshape.296
  567.7 0.8 reshape.294
  568.8 1.0 reshape.307
  572.3 1.2 reshape.300
  573.5 1.2 multiply_reduce_fusion.3
  574.8 1.6 multiply_reduce_fusion
  576.9 1.2 convert_divide_fusion.1
  578.1 2.6 fusion
  580.8 2.5 fusion.3
  583.3 1.5 copy-done.8
  584.7 3.6 fusion.8
  588.4 0.7 copy.129
  (109 shorter events, 8.2 us)
Async XLA Ops:
  0.6 4.8 copy-start.15
  1.8 4.9 copy-start.16
  7.0 4.0 copy-start.23
  7.0 4.0 copy-start.24
  296.8 53.8 %collective-permute-start = (bf16[2,256,1536]{2,1,0:T(8,128)(2,1)}, bf16[2,256,1536]{2,1,0:T(8,128)(2,1)}, u32[]{:S(2)}, u32[]{:S(2)}) collective-permute-start(bf16[2,256,1536]{2,1,0:T(8,128)(2,1)} %dynamic-slice_bitcast_fusion.3), channel_id=1, source_target_pairs={{0,2},{1,3},{2,0},{3,1},{4,6},{5,7},{6,4},{7,5},{8,10},{9,11},{10,... | collective-permute-start | bytes 4718600 | tf_op jit(solution)/shard_map/ppermute | solution.py:1148
  308.6 2.9 copy-start.9
  310.0 37.6 %collective-permute-start.1 = (bf16[4,128,1536]{2,1,0:T(8,128)(2,1)}, bf16[4,128,1536]{2,1,0:T(8,128)(2,1)}, u32[]{:S(2)}, u32[]{:S(2)}) collective-permute-start(bf16[4,128,1536]{2,1,0:T(8,128)(2,1)} %dynamic-slice_bitcast_fusion.2), channel_id=1, source_target_pairs={{0,4},{4,0},{8,12},{12,8},{16,20},{20,16},{24,28},{28,24},{1,5},{5... | collective-permute-start | bytes 4718600 | tf_op jit(solution)/shard_map/ppermute | solution.py:1156
  323.0 57.6 %collective-permute-start.2 = (bf16[4,4,48,1024]{3,2,1,0:T(8,128)(2,1)}, bf16[4,4,48,1024]{3,2,1,0:T(8,128)(2,1)}, u32[]{:S(2)}, u32[]{:S(2)}) collective-permute-start(bf16[4,4,48,1024]{3,2,1,0:T(8,128)(2,1)} %dynamic-slice_bitcast_fusion.1), channel_id=1, source_target_pairs={{0,4},{4,0},{8,12},{12,8},{16,20},{20,16},{24,28},{28,24},{1,5},{5... | collective-permute-start | bytes 4718600 | tf_op jit(solution)/shard_map/ppermute | solution.py:1156
  324.6 23.0 %copy-start.10 = (bf16[1024,1536]{1,0:T(8,128)(2,1)S(1)}, bf16[1024,1536]{1,0:T(8,128)(2,1)}, u32[]{:S(2)}) copy-start(bf16[1024,1536]{1,0:T(8,128)(2,1)} %copy-done.9) | copy-start | bytes 9437188
  376.6 7.2 %copy-start.27 = (bf16[2,256,1536]{2,1,0:T(8,128)(2,1)S(1)}, bf16[2,256,1536]{2,1,0:T(8,128)(2,1)}, u32[]{:S(2)}) copy-start(bf16[2,256,1536]{2,1,0:T(8,128)(2,1)} %get-tuple-element.108) | copy-start | bytes 4718596
  376.6 7.2 %copy-start.28 = (bf16[2,256,1536]{2,1,0:T(8,128)(2,1)S(1)}, bf16[2,256,1536]{2,1,0:T(8,128)(2,1)}, u32[]{:S(2)}) copy-start(bf16[2,256,1536]{2,1,0:T(8,128)(2,1)} %get-tuple-element.115) | copy-start | bytes 4718596
  388.1 40.5 %copy-start.3 = (bf16[4,4,48,1024]{3,2,1,0:T(8,128)(2,1)S(1)}, bf16[4,4,48,1024]{3,2,1,0:T(8,128)(2,1)}, u32[]{:S(2)}) copy-start(bf16[4,4,48,1024]{3,2,1,0:T(8,128)(2,1)} %fusion.6.refs_11_) | copy-start | bytes 4718596
  428.6 4.2 copy-start.6
  428.6 34.9 %collective-permute-start.5 = (bf16[4,48,1024]{2,1,0:T(8,128)(2,1)S(1)}, bf16[4,48,1024]{2,1,0:T(8,128)(2,1)S(1)}, u32[]{:S(2)}, u32[]{:S(2)}) collective-permute-start(bf16[4,48,1024]{2,1,0:T(8,128)(2,1)S(1)} %dynamic-slice_bitcast_fusion.4), channel_id=1, source_target_pairs={{0,16},{4,20},{8,24},{12,28},{16,0},{20,4},{24,8},{28,12},{1,17},{... | collective-permute-start | bytes 1179656 | tf_op jit(solution)/shard_map/ppermute | solution.py:1213
  430.2 10.8 %slice-start = ((s8[6291456]{0:T(1024)(128)(4,1)}), s8[4194304]{0:T(1024)(128)(4,1)S(1)}, s32[]{:S(2)}) async-start(s8[6291456]{0:T(1024)(128)(4,1)} %bitcast.194), calls=%async_computation | async-start | bytes 8388608
  432.3 32.3 %collective-permute-start.3 = (bf16[8,48,1536]{2,1,0:T(8,128)(2,1)S(1)}, bf16[8,48,1536]{2,1,0:T(8,128)(2,1)S(1)}, u32[]{:S(2)}, u32[]{:S(2)}) collective-permute-start(bf16[8,48,1536]{2,1,0:T(8,128)(2,1)S(1)} %fusion.13), channel_id=1, source_target_pairs={{0,2},{1,3},{2,0},{3,1},{4,6},{5,7},{6,4},{7,5},{8,10},{9,11},{10,... | collective-permute-start | bytes 3538952 | tf_op jit(solution)/shard_map/ppermute | solution.py:1207
  432.8 8.3 %slice-start.1 = ((s8[6291456]{0:T(1024)(128)(4,1)}), s8[2097152]{0:T(1024)(128)(4,1)S(1)}, s32[]{:S(2)}) async-start(s8[6291456]{0:T(1024)(128)(4,1)} %bitcast.194), calls=%async_computation.1 | async-start | bytes 4194304
  432.8 8.3 %copy-start.26 = (bf16[4,2,256,512]{3,2,1,0:T(8,128)(2,1)S(1)}, bf16[4,2,256,512]{3,2,1,0:T(8,128)(2,1)}, u32[]{:S(2)}) copy-start(bf16[4,2,256,512]{3,2,1,0:T(8,128)(2,1)} %get-tuple-element.124) | copy-start | bytes 6291460
  445.6 9.2 %copy-start.25 = (bf16[4,2,256,512]{3,2,1,0:T(8,128)(2,1)S(1)}, bf16[4,2,256,512]{3,2,1,0:T(8,128)(2,1)}, u32[]{:S(2)}) copy-start(bf16[4,2,256,512]{3,2,1,0:T(8,128)(2,1)} %get-tuple-element.123) | copy-start | bytes 6291460
  454.9 4.6 copy-start.5
  454.9 6.8 %copy-start.4 = (bf16[1536,1024]{1,0:T(8,128)(2,1)S(1)}, bf16[1536,1024]{1,0:T(8,128)(2,1)}, u32[]{:S(2)}) copy-start(bf16[1536,1024]{1,0:T(8,128)(2,1)} %bitcast_convert_fusion.1) | copy-start | bytes 9437188
  459.5 2.2 copy-start.14
  459.5 4.1 copy-start.19
  461.7 2.9 copy-start.7
  463.6 3.9 copy-start.13
  465.8 117.5 %collective-permute-start.4 = (bf16[2,256,1536]{2,1,0:T(8,128)(2,1)}, bf16[2,256,1536]{2,1,0:T(8,128)(2,1)}, u32[]{:S(2)}, u32[]{:S(2)}) collective-permute-start(bf16[2,256,1536]{2,1,0:T(8,128)(2,1)} %dynamic-slice_bitcast_fusion), channel_id=1, source_target_pairs={{0,2},{1,3},{2,0},{3,1},{4,6},{5,7},{6,4},{7,5},{8,10},{9,11},{10,... | collective-permute-start | bytes 4718600 | tf_op jit(solution)/shard_map/ppermute | solution.py:1148
  566.0 3.9 copy-start.18
  566.2 4.5 copy-start.21
  569.9 0.7 copy-start.17
  570.0 1.7 copy-start.20
  571.6 3.1 copy-start.11
  571.8 6.3 %copy-start = (bf16[2,256,1536]{2,1,0:T(8,128)(2,1)S(1)}, bf16[2,256,1536]{2,1,0:T(8,128)(2,1)}, u32[]{:S(2)}) copy-start(bf16[2,256,1536]{2,1,0:T(8,128)(2,1)} %refs_1_.5) | copy-start | bytes 4718596
  574.7 6.0 %copy-start.2 = (f32[2,256,1536]{2,1,0:T(8,128)S(1)}, f32[2,256,1536]{2,1,0:T(8,128)}, u32[]{:S(2)}) copy-start(f32[2,256,1536]{2,1,0:T(8,128)} %get-tuple-element.130) | copy-start | bytes 9437188
  574.7 6.0 %copy-start.12 = (f32[2,256,1536]{2,1,0:T(8,128)S(1)}, f32[2,256,1536]{2,1,0:T(8,128)}, u32[]{:S(2)}) copy-start(f32[2,256,1536]{2,1,0:T(8,128)} %get-tuple-element.122) | copy-start | bytes 9437188
  580.8 2.5 copy-start.1
  580.8 4.0 copy-start.8
  583.3 5.1 copy-start.22

commit v4 on v3

--- a/solution.py
+++ b/solution.py
@@ -310,6 +310,11 @@
 
 def ring_outer(link, slot_of, step):
     slot = slot_of(link.outer_from(step - 1) * link.z.inner + link.i)
+    return link.put(slot, slot, link.dp_dev(link.outer_to(1), link.i))
+
+
+def ring_columns(link, buf, step):
+    slot = buf.at[pl.ds(link.outer_from(step - 1) * link.z.inner, link.z.inner)]
     return link.put(slot, slot, link.dp_dev(link.outer_to(1), link.i))
 
 
@@ -748,67 +753,47 @@
 
 
 def tail_kernel(
-    z, da_ref, q_ref, kv_ref, po_ref, up_ref, gate_ref,
-    da_out, q_out, kv_out, po_out, gate_out, up_out,
-    da_mine, da_got, da_send, da_came, q_x, q_col, q_z, kv_x, kv_col, kv_z, po_x, po_col, po_z,
-    up_mine, up_z, mine_q, mine_kv, mine_up, send_sems, recv_sems, local_sems,
+    z, hc, dq_hbm, dkv_hbm, w_ref, q_ref, kv_ref, po_own, po_send, up_ref, gain_ref, gate_hbm,
+    x_hbm, d_mid_hbm, mid_hbm, out_hbm, came_hbm,
+    outputs_ref, grad_ref, po_out, q_out, kv_out, gate_out, up_out,
+    dq, dkv, x, d_mid, mid, out_own, out_came, da_core, da_got, da_send, da_came,
+    po_came, po_ref, q_x, q_col, q_z, kv_x, kv_col, kv_z, po_x, po_col, po_z, up_z, mine_q, mine_kv, mine_up,
+    send_sems, recv_sems, local_sems,
 ):
     link = Link(z, send_sems, recv_sems, local_sems)
     link.landed = []
+    wide = lambda a: a.astype(F32)
+    ys, seqs, r = z.ys, x.shape[0], x.shape[1]
+    half = dq.shape[-1]
+    loads = [link.keep(dq_hbm, dq), link.keep(dkv_hbm, dkv)]
+    later = [
+        link.keep(x_hbm, x),
+        link.keep(d_mid_hbm, d_mid),
+        link.keep(mid_hbm, mid),
+        link.keep(out_hbm.at[link.y], out_own),
+        link.keep(came_hbm, out_came),
+    ]
     link.barrier()
-    peer = link.ctx_dev(link.y, 1 - link.k)
-    far = list(range(1, z.outer))
-    order = [j for j in far if j in (1, z.outer - 1)] + [j for j in far if j not in (1, z.outer - 1)]
-    wide = lambda a: a.astype(F32)
-
-    core = link.put(da_ref.at[:, 1 - link.k], da_got, peer)
-    scatter = lambda src, dst: [
-        link.put(src.at[:, link.inner_to(j)], dst.at[j - 1], link.dp_dev(link.o, link.inner_to(j)))
-        for j in range(1, z.inner)
-    ]
-    x_ways = [(q_ref, q_x, q_col, q_z, scatter(q_ref, q_x)), (kv_ref, kv_x, kv_col, kv_z, scatter(kv_ref, kv_x))]
-    po_way = (po_ref, po_x, po_col, po_z, scatter(po_ref, po_x))
-    up_ways = []
-    near = [j for j in order if j in (1, z.outer - 1)]
-    rest = [j for j in order if j not in near]
-
-    def outer_put(src, dst, j):
-        to = link.outer_to(j)
-        return link.put(src.at[to], dst.at[j - 1], link.dp_dev(to, link.i))
-
-    up_ways += [outer_put(up_ref, up_z, j) for j in near]
-    load = link.keep(da_ref.at[:, link.k], da_mine)
-    load_up = link.keep(up_ref.at[link.o], up_mine)
-    link.keep(gate_ref.at[link.c], gate_out.at[link.c])
-    exchange_ctx(link, gate_ref, lambda s: gate_out.at[s])
-
-    link.arrived(core)
-    load.wait()
-    load_up.wait()
-    link.local = [copy for copy in link.local if copy is not load and copy is not load_up]
-    rows = 32 if da_mine.shape[2] % 32 == 0 else da_mine.shape[2]
-    count = da_mine.shape[2] // rows
-    seqs = da_mine.shape[1]
-
-    def add_core(step, _):
-        b, at = lax.div(step, count), pl.ds(pl.multiple_of(lax.rem(step, count) * rows, rows), rows)
-        for j in range(z.ys):
-            y = lax.rem(link.y + j, z.ys)
-            total = wide(da_mine[y, b, at]) + wide(da_got[y, b, at])
-            if j == 0:
-                da_out[b, at] = total
-            else:
-                da_send[j - 1, b, at] = total.astype(BF)
-        return 0
-
-    lax.fori_loop(0, seqs * count, add_core, 0)
-    y_ways = []
-    for j in range(1, z.ys):
-        to = lax.rem(link.y + j, z.ys)
-        y_ways.append(link.put(da_send.at[j - 1], da_came.at[j - 1], link.ctx_dev(to, link.k)))
-
-    def columns(way):
-        part, came, col, got, copies = way
+
+    def inner_puts(src, dst):
+        return [
+            link.put(src.at[:, link.inner_to(j)], dst.at[j - 1], link.dp_dev(link.o, link.inner_to(j)))
+            for j in range(1, z.inner)
+        ]
+
+    def ring(col, got, step, copies):
+        if copies:
+            link.arrived(copies[-1])
+            total = wide(got[step - 2]) + wide(col[link.outer_from(step)])
+            if step == z.outer:
+                return total
+            got[step - 2] = total.astype(BF)
+            src = got.at[step - 2]
+        else:
+            src = col.at[link.outer_from(1)]
+        copies.append(link.put(src, got.at[step - 1], link.dp_dev(link.outer_to(1), link.i)))
+
+    def columns(part, came, col, copies):
         for copy in copies:
             link.arrived(copy)
         for o in range(z.outer):
@@ -816,74 +801,150 @@
             for j in range(z.inner - 1):
                 total += wide(came[j, o])
             col[o] = total.astype(BF)
-        return [outer_put(col, got, j) for j in order]
-
-    z_ways = [columns(way) for way in x_ways]
-    z_ways.append(columns(po_way))
-    up_ways += [outer_put(up_ref, up_z, j) for j in rest]
-
-    def close(col, got, copies):
-        for copy in copies:
-            link.arrived(copy)
-        total = wide(col)
-        for j in range(z.outer - 1):
-            total += wide(got[j])
-        return total
-
-    for way, copies, mine, out in zip(x_ways, z_ways, (mine_q, mine_kv), (q_out, kv_out)):
-        mine[...] = close(way[2][link.o], way[3], copies).astype(BF)
-        exchange_ctx(link, mine, lambda s: out.at[s])
-        link.keep(mine.at[link.c], out.at[link.c])
+
+    up_way, q_way, kv_way, po_way = [], [], [], []
+    ring(up_ref, up_z, 1, up_way)
+    q_in = inner_puts(q_ref, q_x)
+    po_y = []
+    for j in range(1, ys):
+        to = lax.rem(link.y + j, ys)
+        po_y.append(link.put(po_send.at[j - 1], po_came.at[j - 1], link.ctx_dev(to, link.k)))
+    exchange_ctx(link, gate_hbm, lambda s: gate_out.at[s])
+    link.keep(gate_hbm.at[link.c], gate_out.at[link.c])
+    for copy in loads:
+        copy.wait()
+
+    def da_of(place, b):
+        left = dot_nt(dq[place, b], w_ref[:, :half])
+        return left + dot_nt(dkv[place, b], w_ref[:, half:])
+
+    core = []
+    for y in range(ys):
+        for b in range(seqs):
+            da_core[y, b] = da_of(y * 2 + 1 - link.k, b).astype(BF)
+            core.append(link.put(da_core.at[y, b], da_got.at[y, b], link.ctx_dev(link.y, 1 - link.k)))
+    kv_in = inner_puts(kv_ref, kv_x)
+    for copy in core:
+        link.arrived(copy)
+    y_ways = []
+    for j in list(range(1, ys)) + [0]:
+        y = lax.rem(link.y + j, ys)
+        for b in range(seqs):
+            total = da_of(y * 2 + link.k, b) + wide(da_got[y, b])
+            if j == 0:
+                grad_ref[b] = total
+            else:
+                da_send[j - 1, b] = total.astype(BF)
+        if j > 0:
+            y_ways.append(link.put(da_send.at[j - 1], da_came.at[j - 1], link.ctx_dev(y, link.k)))
+    ring(up_ref, up_z, 2, up_way)
+    columns(q_ref, q_x, q_col, q_in)
+    ring(q_col, q_z, 1, q_way)
+    for copy in po_y:
+        link.arrived(copy)
+    for o in range(z.outer):
+        total = wide(po_own[o])
+        for j in range(ys - 1):
+            total += wide(po_came[j, o])
+        po_ref[o] = total.astype(BF)
+    po_in = inner_puts(po_ref, po_x)
+    for copy in later:
+        copy.wait()
+    link.local = link.local[len(loads) + len(later) :]
+
+    rows = 32 if r % 32 == 0 else r
+    count = r // rows
+    at_of = lambda step: (lax.div(step, count), pl.ds(pl.multiple_of(lax.rem(step, count) * rows, rows), rows))
+
+    def finish_outputs(step, _):
+        b, at = at_of(step)
+        total = mid[b, at] + wide(out_own[b, at])
+        for j in range(ys - 1):
+            total += wide(out_came[j, b, at])
+        outputs_ref[b, at] = total
+        return 0
+
+    lax.fori_loop(0, seqs * count, finish_outputs, 0)
+    for step in range(3, z.outer):
+        ring(up_ref, up_z, step, up_way)
+    columns(kv_ref, kv_x, kv_col, kv_in)
+    ring(kv_col, kv_z, 1, kv_way)
+    ring(q_col, q_z, 2, q_way)
+    mine_up[...] = ring(up_ref, up_z, z.outer, up_way).astype(BF)
+    exchange_ctx(link, mine_up, lambda s: up_out.at[s])
+    link.keep(mine_up.at[link.c], up_out.at[link.c])
+    columns(po_ref, po_x, po_col, po_in)
+    ring(po_col, po_z, 1, po_way)
+    for step in range(3, z.outer + 1):
+        ring(kv_col, kv_z, step - 1, kv_way)
+        if step < z.outer:
+            ring(q_col, q_z, step, q_way)
+        ring(po_col, po_z, step - 1, po_way)
     for copy in y_ways:
         link.arrived(copy)
-
-    def add_y(step, _):
-        b, at = lax.div(step, count), pl.ds(pl.multiple_of(lax.rem(step, count) * rows, rows), rows)
-        total = da_out[b, at]
-        for j in range(z.ys - 1):
+    gain = gain_ref[...]
+
+    def finish_grad(step, _):
+        b, at = at_of(step)
+        total = grad_ref[b, at]
+        for j in range(ys - 1):
             total += wide(da_came[j, b, at])
-        da_out[b, at] = total
+        value = wide(x[b, at])
+        scale = lax.rsqrt(jnp.mean(value * value, axis=-1, keepdims=True) + EPS)
+        e = total * gain
+        grad_ref[b, at] = d_mid[b, at] + (
+            scale * e - value * (scale * scale * scale) * jnp.mean(e * value, axis=-1, keepdims=True)
+        )
         return 0
 
-    lax.fori_loop(0, seqs * count, add_y, 0)
-    po_out[...] = close(po_col[link.o], po_z, z_ways[2])
-    mine_up[...] = close(up_mine[...], up_z, up_ways).astype(BF)
-    exchange_ctx(link, mine_up, lambda s: up_out.at[s])
-    link.keep(mine_up.at[link.c], up_out.at[link.c])
+    lax.fori_loop(0, seqs * count, finish_grad, 0)
+    mine_q[...] = ring(q_col, q_z, z.outer, q_way).astype(BF)
+    exchange_ctx(link, mine_q, lambda s: q_out.at[s])
+    link.keep(mine_q.at[link.c], q_out.at[link.c])
+    mine_kv[...] = ring(kv_col, kv_z, z.outer, kv_way).astype(BF)
+    exchange_ctx(link, mine_kv, lambda s: kv_out.at[s])
+    link.keep(mine_kv.at[link.c], kv_out.at[link.c])
+    po_out[...] = ring(po_col, po_z, z.outer, po_way)
     link.finish()
 
 
-def tail_call(z, da, part_q, part_kv, po, up_col, gate_mine):
-    ys, _, m, r, d = da.shape
+def tail_call(z, hc, dq, dkv, w, part_q, part_kv, po, po_send, up_col, gain, gate_mine, x, d_mid, mid, out_pair, out_came):
+    m, r, d = x.shape
     one = lambda a: a.shape[2:]
-    grown = lambda n, a: (n,) + tuple(a)
     q1, kv1, po1, up1 = one(part_q), one(part_kv), one(po), up_col.shape[1:]
-    vm = lambda shape: pltpu.VMEM(tuple(shape), BF)
+    vm = lambda shape, dtype=BF: pltpu.VMEM(tuple(shape), dtype)
     hbm, vmem = pl.BlockSpec(memory_space=pltpu.HBM), pl.BlockSpec(memory_space=pltpu.VMEM)
-    scratch = [vm((ys, m, r, d)), vm((ys, m, r, d)), vm((ys - 1, m, r, d)), vm((ys - 1, m, r, d))]
+    scratch = [vm(dq.shape), vm(dkv.shape), vm(x.shape), vm(x.shape, F32), vm(x.shape, F32), vm(x.shape)]
+    scratch += [vm((z.ys - 1,) + x.shape), vm((z.ys,) + x.shape), vm((z.ys,) + x.shape)]
+    scratch += [vm((z.ys - 1,) + x.shape), vm((z.ys - 1,) + x.shape)]
+    scratch += [vm(po_send.shape), vm(po.shape)]
     for shape in (q1, kv1, po1):
         scratch += [vm((z.inner - 1, z.outer) + shape), vm((z.outer,) + shape), vm((z.outer - 1,) + shape)]
-    scratch += [vm(up1), vm((z.outer - 1,) + up1), vm(q1), vm(kv1), vm(up1)]
+    scratch += [vm((z.outer - 1,) + up1), vm(q1), vm(kv1), vm(up1)]
     scratch += [
         pltpu.SemaphoreType.DMA((64,)),
         pltpu.SemaphoreType.DMA((64,)),
         pltpu.SemaphoreType.DMA((16,)),
     ]
-
-    def body(da, q, kv, po, up, gate, *rest):
-        tail_kernel(z, da, q, kv, po, up, gate, *rest)
-
     return pl.pallas_call(
-        body,
+        functools.partial(tail_kernel, z, hc),
         name="tail",
-        in_specs=[hbm, vmem, vmem, vmem, hbm, hbm],
-        out_specs=[vmem, hbm, hbm, vmem, hbm, hbm],
-        out_shape=[sds((m, r, d), F32), sds(q1), sds(kv1), sds(po1, F32), sds(gate_mine.shape), sds(up1)],
+        in_specs=[hbm, hbm] + [vmem] * 7 + [hbm] * 6,
+        out_specs=[vmem, vmem, vmem, hbm, hbm, hbm, hbm],
+        out_shape=[
+            sds(x.shape, F32),
+            sds(x.shape, F32),
+            sds(po1, F32),
+            sds(q1),
+            sds(kv1),
+            sds(gate_mine.shape),
+            sds(up1),
+        ],
         scratch_shapes=scratch,
         compiler_params=pltpu.CompilerParams(
             collective_id=15, has_side_effects=True, vmem_limit_bytes=VMEM_LIMIT
         ),
-    )(da, part_q, part_kv, po, up_col, gate_mine)
+    )(dq, dkv, w, part_q, part_kv, po, po_send, up_col, gain, gate_mine, x, d_mid, mid, out_pair, out_came)
 
 
 def pad_heads(w, heads, split):
@@ -973,7 +1034,8 @@
         for copy in mine:
             copy.wait()
         link.local = []
-        small = [by_owner(g_qkv), by_owner(g_gain)]
+        split = ctx // 2
+        small = [lambda s: g_qkv.at[s, :split], lambda s: g_qkv.at[s, split:], by_owner(g_gain)]
         ways = [ring_outer(link, slot, 1) for slot in small]
         for slot in small:
             pass_inner(link, slot, 0)
@@ -1024,33 +1086,31 @@
     early, late = range(m // 2), range(m // 2, m)
 
     def qkv_cargo(cargo, moved, bufs):
-        (cot, pu), (g_out, g_gate, g_up, cot_all) = moved, bufs
+        (pu,), (g_out, g_gate, g_up) = moved, bufs
         exchange_ctx(cargo, pu, lambda s: g_up.at[cargo.d, s])
-        own_y(cargo, cot, cot_all, early)
         for slot, step in ((out_slot(cargo, g_out), 2), (by_owner(g_gate), 1)):
             ring_outer(cargo, slot, step)
             pass_inner(cargo, slot, step - 1)
 
-    g_out, g_gate, g_up, cot_all, normed_a, q, k, v = qkv_call(
+    g_out, g_gate, g_up, normed_a, q, k, v = qkv_call(
         z, x_all, gain_a, wqkv, cos, sin, hc, kvc,
-        qkv_cargo, (cotangent, pack_up), (sds((ctx, m, r, d)),), (g_out, g_gate, g_up),
+        qkv_cargo, (pack_up,), (), (g_out, g_gate, g_up),
     )
 
     def attend_cargo(cargo, moved, bufs):
         (cot,), (g_out, g_gate, g_up, cot_all) = moved, bufs
-        own_y(cargo, cot, cot_all, late)
-        pass_core(cargo, cot_all, early)
+        own_y(cargo, cot, cot_all, early)
         for slot, step in ((out_slot(cargo, g_out), 3), (by_owner(g_gate), 2), (by_owner(g_up), 1)):
             ring_outer(cargo, slot, step)
             pass_inner(cargo, slot, step - 1)
 
     g_out, g_gate, g_up, cot_all, att, lse = attend_call(
-        z, q, k, v, qdoc, kdoc, hc, kvc, attend_cargo, (cotangent,), (), (g_out, g_gate, g_up, cot_all)
+        z, q, k, v, qdoc, kdoc, hc, kvc, attend_cargo, (cotangent,), (sds((ctx, m, r, d)),), (g_out, g_gate, g_up)
     )
 
     def second_script(link, ins, outs, scratch):
         att, cot = ins[:2]
-        g_out, g_gate, g_up, cot_all, att_all = outs
+        g_out, g_gate, g_up, g_down, cot_all, att_all = outs
         (hold,) = scratch
         load = pltpu.make_async_copy(cot, hold, link.sems[2].at[15])
         load.start()
@@ -1062,7 +1122,8 @@
         for slot, step in ((by_owner(g_gate), 3), (by_owner(g_up), 2)):
             ring_outer(link, slot, step)
         pass_inner(link, by_owner(g_gate), 2)
-        pass_core(link, cot_all, late)
+        pass_inner(link, by_owner(g_down), 0)
+        pass_core(link, cot_all, early)
         load.wait()
         store = pltpu.make_async_copy(hold, cot_all.at[link.slot(link.y, True)], link.sems[2].at[14])
         store.start()
@@ -1072,7 +1133,7 @@
         link.put(both, both, link.ctx_dev(link.y, 1 - link.k))
         store.wait()
 
-    g_out, g_gate, g_up, cot_all, att_all = communicate(
+    g_out, g_gate, g_up, g_down, cot_all, att_all = communicate(
         z,
         "exchange_heads",
         2,
@@ -1080,45 +1141,42 @@
         (att, cotangent),
         (sds(att.shape),),
         [pltpu.VMEM((m, r, d), BF)],
-        (g_out, g_gate, g_up, cot_all),
+        (g_out, g_gate, g_up, g_down, cot_all),
     )
     wo = g_out.reshape(d, d)
 
     def mix_cargo(cargo, moved, bufs):
-        g_gate, g_up, g_down = bufs
+        (cot,), (g_gate, g_up, g_down, cot_all) = moved, bufs
+        own_y(cargo, cot, cot_all, late)
         ring_outer(cargo, by_owner(g_up), 3)
-        ring_outer(cargo, by_owner(g_down), 1)
+        ring_columns(cargo, g_down, 1)
         pass_inner(cargo, by_owner(g_gate), 3)
         pass_inner(cargo, by_owner(g_up), 1)
 
-    g_gate, g_up, g_down, mid, normed, att_rows = mix_call(
-        z, att_all, inputs, gain_f, wo, mix_cargo, (), (), (g_gate, g_up, g_down)
+    g_gate, g_up, g_down, cot_all, mid, normed, att_rows = mix_call(
+        z, att_all, inputs, gain_f, wo, mix_cargo, (cotangent,), (), (g_gate, g_up, g_down, cot_all)
     )
     att_rows = att_rows.reshape(m * r, H * HD)
-    residual = inputs.astype(F32)
 
     def third_script(link, ins, outs, scratch):
-        x, (g_up, g_down, x_all), (hold,) = ins[0], outs, scratch
+        x, (g_up, g_down, cot_all, x_all), (hold,) = ins[0], outs, scratch
         load = pltpu.make_async_copy(x, hold, link.sems[2].at[15])
         load.start()
         ways = gather_ctx_start(link, x, x_all, True)
-        way = ring_outer(link, by_owner(g_down), 2)
-        pass_inner(link, by_owner(g_down), 1)
+        way = ring_columns(link, g_down, 2)
         pass_inner(link, by_owner(g_up), 2)
+        pass_inner(link, by_owner(g_up), 3)
+        pass_core(link, cot_all, late)
         load.wait()
         store = pltpu.make_async_copy(hold, x_all.at[link.slot(link.y, True)], link.sems[2].at[14])
         store.start()
-        link.arrived(way)
-        way = ring_outer(link, by_owner(g_down), 3)
-        pass_inner(link, by_owner(g_down), 0)
-        pass_inner(link, by_owner(g_up), 3)
-        pass_inner(link, by_owner(g_down), 2)
-        link.arrived(way)
-        pass_inner(link, by_owner(g_down), 3)
+        for step in steps[2:]:
+            link.arrived(way)
+            way = ring_columns(link, g_down, step)
         gather_ctx_forward(link, x_all, ways, True)
         store.wait()
 
-    g_up, g_down, normed_all = communicate(
+    g_up, g_down, cot_all, normed_all = communicate(
         z,
         "gather_third",
         3,
@@ -1126,7 +1184,7 @@
         (normed,),
         (sds((ctx, m, r, d)),),
         [pltpu.VMEM((m, r, d), BF)],
-        (g_up, g_down),
+        (g_up, g_down, cot_all),
     )
     w_gate_c, w_up_c, w_down_c = g_gate.reshape(d, f), g_up.reshape(d, f), g_down.reshape(f, d)
 
@@ -1164,75 +1222,82 @@
 
     dn_came = to_y(dn_pair)
     part_down = dot_tn(flat(hidden), flat(cot_all)).astype(BF).reshape(outer, inner, frows, d)
-    down_x = to_inner(part_down)
+    par = oi % 2
+    by_parity = part_down.reshape(outer // 2, 2, inner, frows, d)
+    down_near, down_rest = dyn(by_parity, 1 - par, 1), dyn(by_parity, par, 1)
+    near_x = to_inner(down_near)
+    rest_x = to_inner(down_rest)
     shape_g = (outer, inner, ctx, rows, f)
     part_gate = dot_tn(flat(normed_all), flat(d_gate)).astype(BF).reshape(shape_g)
     gate_x = to_inner(part_gate)
     part_up = dot_tn(flat(normed_all), flat(after(d_up, part_gate))).astype(BF).reshape(shape_g)
     near = [j for j in steps if j in (1, outer - 1)]
     mid_way = [j for j in steps if j not in near]
-    down_col = column(part_down, after(down_x, part_up))
+    near_col = column(down_near, after(near_x, part_up))
+
+    def to_near(link, col, dst):
+        for j in near:
+            to = link.outer_to(j)
+            link.put(col.at[lax.div(to, 2)], dst.at[j - 1], link.dp_dev(to, link.i))
+
+    def to_rest(link, col, dst):
+        for j in mid_way:
+            to = link.outer_to(j)
+            link.put(col.at[lax.div(to, 2)], dst.at[j - 1], link.dp_dev(to, link.i))
 
     def turn_cargo(cargo, moved, bufs):
-        scatter_outer(cargo, moved[0], bufs[0], near)
+        to_near(cargo, moved[0], bufs[0])
 
     down_z, d_mid, d_mid_low, d_att_all = turn_call(
         z, dn_pair, dn_came, mid, cotangent, gain_f, wo, hc * HD,
-        turn_cargo, (down_col,), (sds((outer - 1, frows, d)),), (),
+        turn_cargo, (near_col,), (sds((outer - 1, frows, d)),), (),
     )
 
     part_out = dot_tn(att_rows, d_mid_low.reshape(m * r, d)).astype(BF).reshape(dp, ys, 2, rows, d)
+    rest_col = column(down_rest, after(rest_x, d_att_all))
     gate_col = column(part_gate, after(gate_x, d_att_all))
 
     def back_cargo(cargo, moved, bufs):
-        (down_col, gate_col, part_up, part_out), (down_z, gate_z, up_x, po_in) = moved, bufs
+        (rest_col, gate_col, part_up, part_out, out_pair), (down_z, gate_z, up_x, po_in, out_came) = moved, bufs
+        scatter_y(cargo, out_pair, out_came)
         scatter_inner(cargo, part_up, up_x)
-        scatter_outer(cargo, down_col, down_z, mid_way)
+        to_rest(cargo, rest_col, down_z)
         scatter_outer(cargo, gate_col, gate_z, near)
         cargo.put(part_out.at[:, :, 1 - cargo.k], po_in, cargo.ctx_dev(cargo.y, 1 - cargo.k))
 
-    down_z, gate_z, up_x, po_in, dq, dkv = attend_back_call(
+    down_z, gate_z, up_x, po_in, out_came, dq, dkv = attend_back_call(
         z, q, k, v, qdoc, kdoc, att, d_att_all, lse, cos, sin, hc, kvc,
         back_cargo,
-        (down_col, gate_col, part_up, part_out),
+        (rest_col, gate_col, part_up, part_out, out_pair),
         (
             sds((outer - 1,) + gate_col.shape[1:]),
             sds((inner - 1, outer) + gate_col.shape[1:]),
             sds((dp, ys, rows, d)),
+            sds((ys - 1, m, r, d)),
         ),
         (down_z,),
     )
     po_both = lambda at: wide(dyn(dyn(part_out, ki, 2), at, 1)) + wide(dyn(po_in, at, 1))
-    po_came = [
-        lax.ppermute(
-            po_both((yi + j) % ys).astype(BF), "ctx", ctx_perm(lambda y, k: (y + j) % ys * 2 + k)
-        )
-        for j in range(1, ys)
-    ]
+    po_send = jnp.stack([po_both((yi + j) % ys).astype(BF) for j in range(1, ys)])
+    po_send = po_send.reshape(ys - 1, outer, inner, rows, d)
     gate_far = [
         lax.ppermute(
             dyn(after(gate_col, dq), (oi + j) % outer, 0), "dp", dp_perm(lambda o, i: (o + j) % outer * inner + i)
         )
         for j in mid_way
     ]
-    out_came = to_y(after(out_pair, po_came))
-    da = dot_nt(flat(dq), wqkv[:, : hc * LANES]) + dot_nt(flat(dkv), wqkv[:, hc * LANES :])
-    da = da.astype(BF).reshape(ys, 2, m, r, d)
     part_q = dot_tn(flat(normed_a), flat(dq)).astype(BF).reshape(outer, inner, ctx, rows, hc * LANES)
     part_kv = dot_tn(flat(normed_a), flat(dkv)).astype(BF).reshape(outer, inner, ctx, rows, 2 * kvc * LANES)
     up_col = column(part_up, [up_x[j] for j in range(inner - 1)])
-    po = close(po_both(yi), after(po_came, part_kv)).astype(BF).reshape(outer, inner, rows, d)
+    po = po_both(yi).astype(BF).reshape(outer, inner, rows, d)
     gate_near = [gate_z[j - 1] for j in near]
     gate_mine = close(dyn(gate_col, oi, 0), gate_near + gate_far).astype(BF)
 
-    d_normed_a, q_all, kv_all, grad_out, gate_all, up_all = tail_call(z, da, part_q, part_kv, po, up_col, gate_mine)
-    grad_down = close(dyn(down_col, oi, 0), [down_z[j - 1] for j in steps])
-    outputs = mid + close(dyn(out_pair, yi, 0), out_came)
-    scale_a = lax.rsqrt(jnp.mean(residual * residual, axis=-1, keepdims=True) + EPS)
-    e = d_normed_a * gain_a
-    input_grad = d_mid + (
-        scale_a * e - residual * (scale_a * scale_a * scale_a) * jnp.mean(e * residual, axis=-1, keepdims=True)
-    )
+    outputs, input_grad, grad_out, q_all, kv_all, gate_all, up_all = tail_call(
+        z, hc, dq, dkv, wqkv, part_q, part_kv, po, po_send, up_col, gain_a, gate_mine,
+        inputs, d_mid, mid, out_pair, out_came,
+    )
+    grad_down = close(dyn(rest_col, oi // 2, 0), [down_z[j - 1] for j in steps])
     spread = lambda a: wide(a).reshape(ctx, rows, dp, frows).transpose(1, 2, 0, 3).reshape(rows, ff)
     grad_gate, grad_up = spread(gate_all), spread(up_all)
     cols = lambda a, heads, split: (

time: 596 us -> 550 us (0.923)
  Pallas kernels: 434 us -> 417 us
  matrix products: 62.8 us -> 46.8 us
  other arithmetic: 35.9 us -> 25.9 us
    dot_general x2 -> x0, matrix products: 17.5 us -> none  [dot_nt(): lax.dot_general(a, b, (((1,), (1,)), ((), ())), preferred_element_type=F32)]
    ppermute x2 -> x3, waiting for transfers between devices: 15.5 us -> 1.69 us  [to_inner(): lax.ppermute(dyn(part, (ii + j) % inner, 1), 'dp', dp_perm(lambda o, i: o...]
    ppermute x2 -> x1, waiting for transfers between devices: 0.01 us -> 10.9 us  [to_y(): lax.ppermute(dyn(pair, (yi + j) % ys, 0), 'ctx', ctx_perm(lambda y, k: (y...]
    pallas_call x1, Pallas kernels: 93.5 us -> 82.7 us  [tail_call(): pl.pallas_call(functools.partial(tail_kernel, z, hc), name='tail', in_spe...]
    pallas_call x3, Pallas kernels: 137 us -> 128 us  [communicate(): pl.pallas_call(kernel, name=name, out_shape=list(outs), in_specs=[hbm] *...]
    add x2 -> x0, other arithmetic: 6.15 us -> none  [the longest x1 3.65 us: per_device(): outputs = mid + close(dyn(out_pair, yi, 0), out_came)]
  transfers between devices with their start and end apart: 6 -> 5, of which waited for: 2 -> 2; matrix products, arithmetic and copies ran while one was open for 16% -> 9% of each run, Pallas kernels for 20% -> 5%
where the time goes in v4:
time: 550 us; the launch traced here: 544 us
  Pallas kernels  417 us (76%)
  matrix products  46.8 us (9%)
  local copies, waits for them, and re-layouts  34.4 us (6%)
  other arithmetic  25.9 us (5%)
  waiting for transfers between devices  12.6 us (2%)
    pallas_call x5, Pallas kernels, fused_call(): pl.pallas_call(kernel, name=name, grid=grid, in_specs=list(in_specs) + [h...  155 us
    pallas_call x3, Pallas kernels, communicate(): pl.pallas_call(kernel, name=name, out_shape=list(outs), in_specs=[hbm] *...  128 us
    pallas_call x1, Pallas kernels, tail_call(): pl.pallas_call(functools.partial(tail_kernel, z, hc), name='tail', in_spe...  82.7 us
    pallas_call x1, Pallas kernels, mlp_call(): pl.pallas_call(functools.partial(mlp_kernel, z), name='mlp', grid=(2, z.y...  51.6 us
    dot_general x6, matrix products, dot_tn(): lax.dot_general(a, b, (((0,), (0,)), ((), ())), preferred_element_type=F32)  46.8 us
  transfers between devices with their start and end apart: 5, of which 2 were waited for; matrix products, arithmetic and copies ran while one was open for 9% of the time, Pallas kernels for 5%

profile of v4, /device:TPU:0, one launch (start us, length us, event | category | flops | bytes accessed | tf_op | source)
XLA Modules:
  0.0 543.9 jit_solution(9115761864829089762)
XLA Ops:
  0.8 1.3 reshape.245
  2.1 0.9 reshape.246.refs_6_.refs_5_
  3.0 1.3 reshape.240
  6.4 0.9 reshape.244.refs_5_
  7.3 0.6 fusion.15.refs_3_
  7.9 0.8 maximum_bitcast_fusion.refs_2_
  8.7 58.8 %gather_first.1 = (bf16[4,2,256,1536]{3,2,1,0:T(8,128)(2,1)}, s32[4,2,256]{2,1,0:T(2,128)}, bf16[8,4,48,1024]{3,2,1,0:T(8,128)(2,1)}, f32[8,4,8,128]{3,2,1,0:T(8...) custom-call(bf16[2,256,1536]{2,1,0:T(8,128)(2,1)} %x_hbm.1, ...), custom_call_target="tpu_custom_call" | custom-call | tf_op jit(solution)/shard_map/gather_first/pallas_call | solution.py:160
  67.5 1.1 slice_reduce_fusion
  68.6 0.7 reshape_squeeze.6.refs_1_.gain_ref
  69.3 1.9 multiply_sine_fusion
  71.3 1.0 pad_maximum_fusion
  72.3 0.6 reshape.251.refs_4_
  72.9 1.4 copy.69.refs_3_
  74.3 0.7 reshape_squeeze.7.refs_2_.refs_4_
  75.0 1.0 pad_maximum_fusion.1
  76.0 23.0 %qkv.1 = (bf16[8,2,2,48,1536]{4,3,2,1,0:T(8,128)(2,1)}, bf16[8,4,48,1024]{3,2,1,0:T(8,128)(2,1)}, bf16[8,4,48,1024]{3,2,1,0:T(8,128)(2,1)}, bf16[4,2,256,1536]{3...) custom-call(bf16[4,2,256,1536]{3,2,1,0:T(8,128)(2,1)} %get-tuple-ele, ...), custom_call_target="tpu_custom_call", output_to_operand_aliasing={{0}: (6, {}), {1}: (7, {}), {2}: (8, {})} | custom-call | tf_op jit(solution)/shard_map/qkv/pallas_call | solution.py:296
  99.1 29.2 %attend.1 = (bf16[8,2,2,48,1536]{4,3,2,1,0:T(8,128)(2,1)}, bf16[8,4,48,1024]{3,2,1,0:T(8,128)(2,1)}, bf16[8,4,48,1024]{3,2,1,0:T(8,128)(2,1)}, bf16[4,2,256,1536...) custom-call(bf16[4,2,256,512]{3,2,1,0:T(8,128)(2,1)} %get-tuple-elem, ...), custom_call_target="tpu_custom_call", output_to_operand_aliasing={{0}: (6, {}), {1}: (7, {}), {2}: (8, {})} | custom-call | tf_op jit(solution)/shard_map/attend/pallas_call | solution.py:296
  128.3 27.8 %exchange_heads.1 = (bf16[8,2,2,48,1536]{4,3,2,1,0:T(8,128)(2,1)}, bf16[8,4,48,1024]{3,2,1,0:T(8,128)(2,1)}, bf16[8,4,48,1024]{3,2,1,0:T(8,128)(2,1)}, bf16[8,12...) custom-call(bf16[4,2,256,384]{3,2,1,0:T(8,128)(2,1)} %get-tuple-elem, ...), custom_call_target="tpu_custom_call", output_to_operand_aliasing={{0}: (2, {}), {1}: (3, {}), {2}: (4, {}), {3}: (5, {}), {4}... | custom-call | tf_op jit(solution)/shard_map/exchange_heads/pallas_call | solution.py:160
  156.1 34.6 %mix.1 = (bf16[8,4,48,1024]{3,2,1,0:T(8,128)(2,1)}, bf16[8,4,48,1024]{3,2,1,0:T(8,128)(2,1)}, bf16[8,128,1536]{2,1,0:T(8,128)(2,1)}, bf16[4,2,256,1536]{3,2,1,0:...) custom-call(bf16[4,2,256,384]{3,2,1,0:T(8,128)(2,1)} %get-tuple-elem, ...), custom_call_target="tpu_custom_call", output_to_operand_aliasing={{0}: (5, {}), {1}: (6, {}), {2}: (7, {}), {3}: (8, {})} | custom-call | tf_op jit(solution)/shard_map/mix/pallas_call | solution.py:296
  190.7 41.8 %gather_third.1 = (bf16[8,4,48,1024]{3,2,1,0:T(8,128)(2,1)}, bf16[8,128,1536]{2,1,0:T(8,128)(2,1)}, bf16[4,2,256,1536]{3,2,1,0:T(8,128)(2,1)}, bf16[4,2,256,1536]{3,2,1,0:T(8,128)(2,1)}) custom-call(bf16[2,256,1536]{2,1,0:T(8,128)(2,1)} %get-tuple-element.102.refs_0_, ...), custom_call_target="tpu_custom_call", output_to_operand_aliasing={{0}: (1, {}), {1}: (2, {}), {2}: (3, {})} | custom-call | tf_op jit(solution)/shard_map/gather_third/pallas_call | solution.py:160
  232.5 51.6 %mlp.1 = (bf16[4,2,256,1024]{3,2,1,0:T(8,128)(2,1)}, bf16[4,2,256,1024]{3,2,1,0:T(8,128)(2,1)}, bf16[4,2,256,1024]{3,2,1,0:T(8,128)(2,1)}, bf16[2,2,256,1536]{3,2,1,0:T(8,128)(2,1)}, bf16[2,2,256,1536]{3,2,1,0:T(8,128)(2,1)}) custom-call(bf16[4,2,256,1536]{3,2,1,0:T(8,128)(2,1)} %get-tuple-element.106.x_ref, ...), custom_call_target="tpu_custom_call" | custom-call | tf_op jit(solution)/shard_map/mlp/pallas_call | solution.py:740
  284.1 11.6 %bitcast_convert_fusion.3 = bf16[1024,1536]{1,0:T(8,128)(2,1)} fusion(bf16[4,2,256,1024]{3,2,1,0:T(8,128)(2,1)} %get-tuple-element.113, bf16[4,2,256,1536]{3,2,1,0:T(8,128)(2,1)} %get-tuple-element.107.cot_ref), kind=kOutput, calls=%fused_computation.3 | convolution fusion | flops 6444023808 | bytes 13631488 | tf_op jit(solution)/shard_map/dot_general | solution.py:40
  295.6 2.8 dynamic-slice_bitcast_fusion.2
  298.4 0.8 collective-permute-start.1
  299.2 1.3 dynamic-slice_bitcast_fusion.1
  300.5 1.3 collective-permute-start
  301.8 10.2 %bitcast_convert_fusion.2 = bf16[1536,1024]{1,0:T(8,128)(2,1)S(1)} fusion(bf16[4,2,256,1536]{3,2,1,0:T(8,128)(2,1)} %get-tuple-element.106.x_ref, bf16[4,2,256,1024]{3,2,1,0:T(8,128)(2,1)} %get-tuple-element.115), kind=kOutput, calls=%fused_computation.2 | convolution fusion | flops 6444023808 | bytes 13631488 | tf_op jit(solution)/shard_map/dot_general | solution.py:40
  312.0 1.3 dynamic-slice_bitcast_fusion
  313.4 1.5 collective-permute-start.3
  314.9 0.5 collective-permute-start.2
  315.4 8.2 %bitcast_convert_fusion.1 = bf16[1536,1024]{1,0:T(8,128)(2,1)} fusion(bf16[4,2,256,1536]{3,2,1,0:T(8,128)(2,1)S(1)} %bitcast.159, bf16[4,2,256,1024]{3,2,1,0:T(8,128)(2,1)S(1)} %copy-done.26), kind=kOutput, calls=%fused_computation.1 | convolution fusion | flops 6444023808 | bytes 13631488 | tf_op jit(solution)/shard_map/dot_general | solution.py:40
  323.6 2.4 fusion.7.refs_6_
  326.0 10.9 %collective-permute-done.refs_1_ = bf16[2,256,1536]{2,1,0:T(8,128)(2,1)} collective-permute-done((bf16[2,256,1536]{2,1,0:T(8,128)(2,1)}, bf16[2,256,1536]{2,1,0:T(8,128)(2,1)}, u32[]{:S(2)}, u32[]{:S(2)}) %collective-permute-start) | collective-permute-done | bytes 1572896 | tf_op jit(solution)/shard_map/ppermute | solution.py:1206
  337.0 26.7 %turn.1 = (bf16[3,128,1536]{2,1,0:T(8,128)(2,1)}, f32[2,256,1536]{2,1,0:T(8,128)}, bf16[2,256,1536]{2,1,0:T(8,128)(2,1)}, bf16[4,2,256,384]{3,2,1,0:T(8,128)(2,1)}) custom-call(bf16[2,2,256,1536]{3,2,1,0:T(8,128)(2,1)} %get-tuple-element.111.refs_0_, bf16[2,256,1536]{2,1,0:T(8,128)(2,1)} %collective-permute-done.refs_1_, ...), custom_call_target="tpu_custom_call" | custom-call | tf_op jit(solution)/shard_map/turn/pallas_call | solution.py:296
  363.8 3.4 fusion.1.refs_11_
  367.1 1.7 collective-permute-done.2
  368.8 2.4 fusion.6.refs_10_
  371.3 4.4 bitcast_convert_fusion
  375.6 41.1 %attend_back.1 = (bf16[3,128,1536]{2,1,0:T(8,128)(2,1)}, bf16[3,4,48,1024]{3,2,1,0:T(8,128)(2,1)}, bf16[1,4,4,48,1024]{4,3,2,1,0:T(8,128)(2,1)}, bf16[8,2,48,153...) custom-call(bf16[4,2,256,512]{3,2,1,0:T(8,128)(2,1)} %get-tuple-elem, ...), custom_call_target="tpu_custom_call", output_to_operand_aliasing={{0}: (15, {})} | custom-call | tf_op jit(solution)/shard_map/attend_back/pallas_call | solution.py:296
  416.8 1.1 collective-permute-start.4
  417.9 1.9 constant_dynamic-slice_fusion
  419.9 7.5 %fusion.2 = bf16[1536,512]{1,0:T(8,128)(2,1)} fusion(bf16[4,2,256,1536]{3,2,1,0:T(8,128)(2,1)} %get-tuple-element.128, bf16[4,2,256,512]{3,2,1,0:T(8,128)(2,1)S(1)} %copy-done.7), kind=kOutput, calls=%fused_computation.10 | convolution fusion | flops 3222011904 | bytes 9961472 | tf_op jit(solution)/shard_map/dot_general | solution.py:40
  427.5 4.9 fusion.3
  432.6 1.4 fusion.4.po_send
  434.1 1.4 fusion.5.po_own
  435.4 1.1 add_bitcast_fusion
  436.5 0.7 copy-done.9
  437.2 1.9 fusion.up_ref
  439.1 1.0 fusion.8.gate_hbm
  440.1 82.7 %tail.1 = (f32[2,256,1536]{2,1,0:T(8,128)}, f32[2,256,1536]{2,1,0:T(8,128)}, f32[48,1536]{1,0:T(8,128)}, bf16[4,48,512]{2,1,0:T(8,128)(2,1)}, bf16[4,48,512]{2,1...) custom-call(bf16[4,2,256,512]{3,2,1,0:T(8,128)(2,1)} %get-tuple-element.126.dq_hbm, ...), custom_call_target="tpu_custom_call" | custom-call | tf_op jit(solution)/shard_map/tail/pallas_call | solution.py:929
  522.8 1.1 copy.94
  524.5 1.2 reshape.296
  526.3 1.2 reshape.298
  528.3 0.8 reshape.292
  529.5 0.8 reshape.294
  530.5 1.2 slice_convert_fusion
  531.7 2.2 reshape.305
  534.1 1.2 multiply_reduce_fusion.2
  535.2 1.9 multiply_reduce_fusion
  537.1 0.5 convert_divide_fusion
  538.3 1.7 copy.126
  540.0 1.4 copy-done.5
  541.3 1.7 copy.127
  543.0 0.7 copy.128
  (113 shorter events, 5.7 us)
Async XLA Ops:
  0.6 4.4 copy-start.19
  0.7 5.1 copy-start.17
  0.7 5.3 copy-start.10
  4.4 2.9 copy-start.24
  4.4 2.9 copy-start.25
  67.5 4.8 copy-start.23
  295.6 3.6 copy-start.1
  298.4 25.2 %collective-permute-start.1 = (bf16[2,128,1536]{2,1,0:T(8,128)(2,1)}, bf16[2,128,1536]{2,1,0:T(8,128)(2,1)}, u32[]{:S(2)}, u32[]{:S(2)}) collective-permute-start(bf16[2,128,1536]{2,1,0:T(8,128)(2,1)} %get-tuple-element.148), channel_id=1, source_target_pairs={{0,4},{4,0},{8,12},{12,8},{16,20},{20,16},{24,28},{28,24},{1,5},{5... | collective-permute-start | bytes 2359304 | tf_op jit(solution)/shard_map/ppermute | solution.py:1214
  299.2 16.2 %slice-start.2 = ((s8[6291456]{0:T(1024)(128)(4,1)}), s8[4194304]{0:T(1024)(128)(4,1)S(1)}, s32[]{:S(2)}) async-start(s8[6291456]{0:T(1024)(128)(4,1)} %bitcast.158), calls=%async_computation.2 | async-start | bytes 8388608
  300.5 36.5 %collective-permute-start = (bf16[2,256,1536]{2,1,0:T(8,128)(2,1)}, bf16[2,256,1536]{2,1,0:T(8,128)(2,1)}, u32[]{:S(2)}, u32[]{:S(2)}) collective-permute-start(bf16[2,256,1536]{2,1,0:T(8,128)(2,1)} %dynamic-slice_bitcast_fusion.1), channel_id=1, source_target_pairs={{0,2},{1,3},{2,0},{3,1},{4,6},{5,7},{6,4},{7,5},{8,10},{9,11},{10,... | collective-permute-start | bytes 4718600 | tf_op jit(solution)/shard_map/ppermute | solution.py:1206
  301.8 13.6 %slice-start.3 = ((s8[6291456]{0:T(1024)(128)(4,1)}), s8[2097152]{0:T(1024)(128)(4,1)S(1)}, s32[]{:S(2)}) async-start(s8[6291456]{0:T(1024)(128)(4,1)} %bitcast.158), calls=%async_computation.3 | async-start | bytes 4194304
  301.8 13.6 %copy-start.26 = (bf16[4,2,256,1024]{3,2,1,0:T(8,128)(2,1)S(1)}, bf16[4,2,256,1024]{3,2,1,0:T(8,128)(2,1)}, u32[]{:S(2)}) copy-start(bf16[4,2,256,1024]{3,2,1,0:T(8,128)(2,1)} %get-tuple-element.116) | copy-start | bytes 12582916
  313.4 50.4 %collective-permute-start.3 = (bf16[4,4,48,1024]{3,2,1,0:T(8,128)(2,1)}, bf16[4,4,48,1024]{3,2,1,0:T(8,128)(2,1)}, u32[]{:S(2)}, u32[]{:S(2)}) collective-permute-start(bf16[4,4,48,1024]{3,2,1,0:T(8,128)(2,1)} %dynamic-slice_bitcast_fusion), channel_id=1, source_target_pairs={{0,4},{4,0},{8,12},{12,8},{16,20},{20,16},{24,28},{28,24},{1,5},{5... | collective-permute-start | bytes 4718600 | tf_op jit(solution)/shard_map/ppermute | solution.py:1214
  314.9 54.0 %collective-permute-start.2 = (bf16[2,128,1536]{2,1,0:T(8,128)(2,1)}, bf16[2,128,1536]{2,1,0:T(8,128)(2,1)}, u32[]{:S(2)}, u32[]{:S(2)}) collective-permute-start(bf16[2,128,1536]{2,1,0:T(8,128)(2,1)} %get-tuple-element.147), channel_id=1, source_target_pairs={{0,4},{4,0},{8,12},{12,8},{16,20},{20,16},{24,28},{28,24},{1,5},{5... | collective-permute-start | bytes 2359304 | tf_op jit(solution)/shard_map/ppermute | solution.py:1214
  363.7 7.5 %copy-start.27 = (bf16[2,256,1536]{2,1,0:T(8,128)(2,1)S(1)}, bf16[2,256,1536]{2,1,0:T(8,128)(2,1)}, u32[]{:S(2)}) copy-start(bf16[2,256,1536]{2,1,0:T(8,128)(2,1)} %get-tuple-element.122) | copy-start | bytes 4718596
  363.8 7.5 %copy-start.28 = (bf16[2,256,1536]{2,1,0:T(8,128)(2,1)S(1)}, bf16[2,256,1536]{2,1,0:T(8,128)(2,1)}, u32[]{:S(2)}) copy-start(bf16[2,256,1536]{2,1,0:T(8,128)(2,1)} %get-tuple-element.123) | copy-start | bytes 4718596
  375.6 41.1 %copy-start = (bf16[4,4,48,1024]{3,2,1,0:T(8,128)(2,1)S(1)}, bf16[4,4,48,1024]{3,2,1,0:T(8,128)(2,1)}, u32[]{:S(2)}) copy-start(bf16[4,4,48,1024]{3,2,1,0:T(8,128)(2,1)} %fusion.1.refs_11_) | copy-start | bytes 4718596
  416.7 3.1 copy-start.7
  416.8 22.3 %collective-permute-start.4 = (bf16[4,48,1024]{2,1,0:T(8,128)(2,1)S(1)}, bf16[4,48,1024]{2,1,0:T(8,128)(2,1)S(1)}, u32[]{:S(2)}, u32[]{:S(2)}) collective-permute-start(bf16[4,48,1024]{2,1,0:T(8,128)(2,1)S(1)} %dynamic-slice_bitcast_fusion.4), channel_id=1, source_target_pairs={{0,16},{4,20},{8,24},{12,28},{16,0},{20,4},{24,8},{28,12},{1,17},{... | collective-permute-start | bytes 1179656 | tf_op jit(solution)/shard_map/ppermute | solution.py:1284
  417.9 9.5 %slice-start.4 = ((s8[6291456]{0:T(1024)(128)(4,1)}), s8[4194304]{0:T(1024)(128)(4,1)S(1)}, s32[]{:S(2)}) async-start(s8[6291456]{0:T(1024)(128)(4,1)} %bitcast.189), calls=%async_computation.4 | async-start | bytes 8388608
  419.9 7.6 %copy-start.8 = (bf16[4,2,256,512]{3,2,1,0:T(8,128)(2,1)S(1)}, bf16[4,2,256,512]{3,2,1,0:T(8,128)(2,1)}, u32[]{:S(2)}) copy-start(bf16[4,2,256,512]{3,2,1,0:T(8,128)(2,1)} %get-tuple-element.127.dkv_hbm) | copy-start | bytes 6291460
  419.9 7.6 %slice-start.5 = ((s8[6291456]{0:T(1024)(128)(4,1)}), s8[2097152]{0:T(1024)(128)(4,1)S(1)}, s32[]{:S(2)}) async-start(s8[6291456]{0:T(1024)(128)(4,1)} %bitcast.189), calls=%async_computation.5 | async-start | bytes 4194304
  419.9 12.5 %slice-start = ((s8[4718592]{0:T(1024)(128)(4,1)}), s8[4194304]{0:T(1024)(128)(4,1)S(1)}, s32[]{:S(2)}) async-start(s8[4718592]{0:T(1024)(128)(4,1)} %bitcast.153), calls=%async_computation | async-start | bytes 8388608
  427.4 5.0 slice-start.1
  432.6 2.8 copy-start.3
  432.6 2.8 copy-start.4
  434.1 2.4 copy-start.2
  434.1 3.1 copy-start.9
  435.4 3.6 copy-start.14
  522.8 2.9 copy-start.15
  525.7 1.9 copy-start.21
  526.3 4.0 copy-start.22
  530.5 7.8 %copy-start.6 = (f32[2,256,1536]{2,1,0:T(8,128)S(1)}, f32[2,256,1536]{2,1,0:T(8,128)}, u32[]{:S(2)}) copy-start(f32[2,256,1536]{2,1,0:T(8,128)} %get-tuple-element.172) | copy-start | bytes 9437188
  531.7 5.9 %copy-start.18 = (bf16[48,768]{1,0:T(8,128)(2,1)S(1)}, bf16[48,768]{1,0:T(8,128)(2,1)}, u32[]{:S(2)}) copy-start(bf16[48,768]{1,0:T(8,128)(2,1)} %param.17) | copy-start | bytes 221188
  533.9 3.7 copy-start.12
  533.9 3.7 copy-start.13
  533.9 3.7 copy-start.20
  534.1 5.9 %copy-start.11 = (f32[6,8,4,384]{3,1,2,0:T(8,128)}, f32[6,8,4,384]{3,1,2,0:T(8,128)S(1)}, u32[]{:S(2)}) copy-start(f32[6,8,4,384]{3,1,2,0:T(8,128)S(1)} %copy.93) | copy-start | bytes 884740
  538.3 3.0 copy-start.5
  541.3 1.7 copy-start.16

commit v5 on v4

--- a/solution.py
+++ b/solution.py
@@ -342,17 +342,23 @@
         link.put(src.at[part], slot, link.ctx_dev(link.y, 1 - link.k))
 
 
+def turns(table):
+    half = LANES // 2
+    cos, sin = table[:, :half], table[:, half:]
+    return jnp.concatenate([cos, cos], axis=1), jnp.concatenate([-sin, sin], axis=1)
+
+
 def rotated(u, cos, sin):
     return u * cos + pltpu.roll(u, LANES // 2, 1) * sin
 
 
-def qkv_kernel(hc, kvc, x_ref, gain_ref, w_ref, cos_ref, sin_ref, n_ref, q_ref, k_ref, v_ref):
+def qkv_kernel(hc, kvc, x_ref, gain_ref, w_ref, table_ref, n_ref, q_ref, k_ref, v_ref):
     x = x_ref[0, 0].astype(F32)
     scale = lax.rsqrt(jnp.mean(x * x, axis=-1, keepdims=True) + EPS)
     normed = (x * scale * gain_ref[...]).astype(BF)
     n_ref[0, 0] = normed
     full = dot_nn(normed, w_ref[...])
-    cos, sin = cos_ref[0], sin_ref[0]
+    cos, sin = turns(table_ref[0])
     for h in range(hc + kvc):
         piece = rotated(full[:, h * LANES : (h + 1) * LANES], cos, sin).astype(BF)
         if h < hc:
@@ -362,7 +368,7 @@
     v_ref[0, 0] = full[:, (hc + kvc) * LANES :].astype(BF)
 
 
-def qkv_call(z, x_all, gain, w, cos, sin, hc, kvc, script, moved, new, filled):
+def qkv_call(z, x_all, gain, w, positions, hc, kvc, script, moved, new, filled):
     ctx, m, r, d = x_all.shape
     row = lambda s, b: (s, b, 0, 0)
     whole = lambda s, b: (0, 0)
@@ -378,7 +384,6 @@
             pl.BlockSpec((1, d), whole),
             pl.BlockSpec(w.shape, whole, pipeline_mode=pl.Buffered(1)),
             table,
-            table,
         ],
         [
             pl.BlockSpec((1, 1, r, d), row),
@@ -392,7 +397,7 @@
             sds((ctx, m, r, kvc * LANES)),
             sds((ctx, m, r, kvc * LANES)),
         ],
-        (x_all, gain, w, cos, sin),
+        (x_all, gain, w, positions),
         script,
         moved,
         new,
@@ -468,7 +473,7 @@
 
 
 def attend_back_kernel(
-    hc, kvc, ctx, q_ref, k_ref, v_ref, qdoc_ref, kdoc_ref, o_ref, do_ref, lse_ref, cos_ref, sin_ref,
+    hc, kvc, ctx, q_ref, k_ref, v_ref, qdoc_ref, kdoc_ref, o_ref, do_ref, lse_ref, table_ref,
     dq_ref, dkv_ref, dk_acc, dv_acc,
 ):
     s = pl.program_id(1)
@@ -481,7 +486,7 @@
         dk_acc[...] = jnp.zeros_like(dk_acc)
         dv_acc[...] = jnp.zeros_like(dv_acc)
 
-    cos, sin = cos_ref[s], sin_ref[s]
+    cos, sin = turns(table_ref[s])
     lse_all = lse_ref[0, 0]
     for h in range(hc):
         g = h * kvc // hc
@@ -507,16 +512,17 @@
     @pl.when(s == ctx - 1)
     def _():
         for b in range(ctx):
+            cos_b, sin_b = turns(table_ref[b])
             for g in range(kvc):
                 here = slice(g * LANES, (g + 1) * LANES)
                 at = g * LANES
-                dk = rotated(dk_acc[b, :, here], cos_ref[b], -sin_ref[b])
+                dk = rotated(dk_acc[b, :, here], cos_b, -sin_b)
                 dkv_ref[b, 0, :, at : at + LANES] = dk.astype(BF)
                 at += kvc * LANES
                 dkv_ref[b, 0, :, at : at + LANES] = dv_acc[b, :, here].astype(BF)
 
 
-def attend_back_call(z, q, k, v, qdoc, kdoc, o, do, lse, cos, sin, hc, kvc, script, moved, new, filled):
+def attend_back_call(z, q, k, v, qdoc, kdoc, o, do, lse, positions, hc, kvc, script, moved, new, filled):
     ctx, m, r, _ = q.shape
     row = lambda b, s: (s, b, 0, 0)
     seq = lambda b, s: (0, b, 0, 0)
@@ -537,14 +543,13 @@
             pl.BlockSpec((1, 1, r, hc * HD), row),
             pl.BlockSpec((1, 1, r, LANES), row),
             table,
-            table,
         ],
         [
             pl.BlockSpec((1, 1, r, hc * LANES), row),
             pl.BlockSpec((ctx, 1, r, 2 * kvc * LANES), seq),
         ],
         [sds((ctx, m, r, hc * LANES)), sds((ctx, m, r, 2 * kvc * LANES))],
-        (q, k, v, qdoc, kdoc, o, do, lse, cos, sin),
+        (q, k, v, qdoc, kdoc, o, do, lse, positions),
         script,
         moved,
         new,
@@ -805,14 +810,18 @@
     up_way, q_way, kv_way, po_way = [], [], [], []
     ring(up_ref, up_z, 1, up_way)
     q_in = inner_puts(q_ref, q_x)
+    exchange_ctx(link, gate_hbm, lambda s: gate_out.at[s])
+    link.keep(gate_hbm.at[link.c], gate_out.at[link.c])
     po_y = []
     for j in range(1, ys):
         to = lax.rem(link.y + j, ys)
         po_y.append(link.put(po_send.at[j - 1], po_came.at[j - 1], link.ctx_dev(to, link.k)))
-    exchange_ctx(link, gate_hbm, lambda s: gate_out.at[s])
-    link.keep(gate_hbm.at[link.c], gate_out.at[link.c])
     for copy in loads:
         copy.wait()
+
+    def home(mine, out):
+        exchange_ctx(link, mine, lambda s: out.at[s])
+        link.keep(mine.at[link.c], out.at[link.c])
 
     def da_of(place, b):
         left = dot_nt(dq[place, b], w_ref[:, :half])
@@ -823,10 +832,8 @@
         for b in range(seqs):
             da_core[y, b] = da_of(y * 2 + 1 - link.k, b).astype(BF)
             core.append(link.put(da_core.at[y, b], da_got.at[y, b], link.ctx_dev(link.y, 1 - link.k)))
-    kv_in = inner_puts(kv_ref, kv_x)
     for copy in core:
         link.arrived(copy)
-    y_ways = []
     for j in list(range(1, ys)) + [0]:
         y = lax.rem(link.y + j, ys)
         for b in range(seqs):
@@ -835,19 +842,10 @@
                 grad_ref[b] = total
             else:
                 da_send[j - 1, b] = total.astype(BF)
-        if j > 0:
-            y_ways.append(link.put(da_send.at[j - 1], da_came.at[j - 1], link.ctx_dev(y, link.k)))
     ring(up_ref, up_z, 2, up_way)
     columns(q_ref, q_x, q_col, q_in)
     ring(q_col, q_z, 1, q_way)
-    for copy in po_y:
-        link.arrived(copy)
-    for o in range(z.outer):
-        total = wide(po_own[o])
-        for j in range(ys - 1):
-            total += wide(po_came[j, o])
-        po_ref[o] = total.astype(BF)
-    po_in = inner_puts(po_ref, po_x)
+    kv_in = inner_puts(kv_ref, kv_x)
     for copy in later:
         copy.wait()
     link.local = link.local[len(loads) + len(later) :]
@@ -867,18 +865,36 @@
     lax.fori_loop(0, seqs * count, finish_outputs, 0)
     for step in range(3, z.outer):
         ring(up_ref, up_z, step, up_way)
+    for copy in po_y:
+        link.arrived(copy)
+    y_ways = []
+    for j in range(1, ys):
+        to = lax.rem(link.y + j, ys)
+        y_ways.append(link.put(da_send.at[j - 1], da_came.at[j - 1], link.ctx_dev(to, link.k)))
+    for o in range(z.outer):
+        total = wide(po_own[o])
+        for j in range(ys - 1):
+            total += wide(po_came[j, o])
+        po_ref[o] = total.astype(BF)
+    ring(q_col, q_z, 2, q_way)
+    mine_up[...] = ring(up_ref, up_z, z.outer, up_way).astype(BF)
+    home(mine_up, up_out)
+    for step in range(3, z.outer):
+        ring(q_col, q_z, step, q_way)
     columns(kv_ref, kv_x, kv_col, kv_in)
     ring(kv_col, kv_z, 1, kv_way)
-    ring(q_col, q_z, 2, q_way)
-    mine_up[...] = ring(up_ref, up_z, z.outer, up_way).astype(BF)
-    exchange_ctx(link, mine_up, lambda s: up_out.at[s])
-    link.keep(mine_up.at[link.c], up_out.at[link.c])
+    po_in = inner_puts(po_ref, po_x)
+    mine_q[...] = ring(q_col, q_z, z.outer, q_way).astype(BF)
+    home(mine_q, q_out)
+    ring(kv_col, kv_z, 2, kv_way)
     columns(po_ref, po_x, po_col, po_in)
     ring(po_col, po_z, 1, po_way)
     for step in range(3, z.outer + 1):
-        ring(kv_col, kv_z, step - 1, kv_way)
         if step < z.outer:
-            ring(q_col, q_z, step, q_way)
+            ring(kv_col, kv_z, step, kv_way)
+        else:
+            mine_kv[...] = ring(kv_col, kv_z, step, kv_way).astype(BF)
+            home(mine_kv, kv_out)
         ring(po_col, po_z, step - 1, po_way)
     for copy in y_ways:
         link.arrived(copy)
@@ -898,12 +914,6 @@
         return 0
 
     lax.fori_loop(0, seqs * count, finish_grad, 0)
-    mine_q[...] = ring(q_col, q_z, z.outer, q_way).astype(BF)
-    exchange_ctx(link, mine_q, lambda s: q_out.at[s])
-    link.keep(mine_q.at[link.c], q_out.at[link.c])
-    mine_kv[...] = ring(kv_col, kv_z, z.outer, kv_way).astype(BF)
-    exchange_ctx(link, mine_kv, lambda s: kv_out.at[s])
-    link.keep(mine_kv.at[link.c], kv_out.at[link.c])
     po_out[...] = ring(po_col, po_z, z.outer, po_way)
     link.finish()
 
@@ -964,14 +974,12 @@
     return w.reshape(w.shape[: w.ndim - (3 if split else 2)] + (heads * HD,))
 
 
-def rope_tables(ctx, r):
+def rope_table(ctx, r):
     frequency = THETA ** (-(jnp.arange(HALF, dtype=F32) * (2.0 / HD)))
     angles = jnp.arange(ctx * r, dtype=jnp.int32).astype(F32)[:, None] * frequency[None, :]
     pad = ((0, 0), (0, LANES // 2 - HALF))
-    cos, sin = jnp.pad(jnp.cos(angles), pad), jnp.pad(jnp.sin(angles), pad)
-    cos = jnp.concatenate([cos, cos], axis=1).reshape(ctx, r, LANES)
-    sin = jnp.concatenate([-sin, sin], axis=1).reshape(ctx, r, LANES)
-    return cos, sin
+    table = jnp.concatenate([jnp.pad(jnp.cos(angles), pad), jnp.pad(jnp.sin(angles), pad)], axis=1)
+    return table.reshape(ctx, r, LANES)
 
 
 def per_device(
@@ -1080,7 +1088,7 @@
     gain_a = g_gain[:, :, 0, :rows].reshape(1, d)
     gain_f = g_gain[:, :, 1, :rows].reshape(1, d)
     wqkv = g_qkv.reshape(d, width)
-    cos, sin = rope_tables(ctx, r)
+    table = rope_table(ctx, r)
     qdoc = seg_all.reshape(ctx, m, r, 1)
     kdoc = seg_all.reshape(ctx, m, 1, r)
     early, late = range(m // 2), range(m // 2, m)
@@ -1093,7 +1101,7 @@
             pass_inner(cargo, slot, step - 1)
 
     g_out, g_gate, g_up, normed_a, q, k, v = qkv_call(
-        z, x_all, gain_a, wqkv, cos, sin, hc, kvc,
+        z, x_all, gain_a, wqkv, table, hc, kvc,
         qkv_cargo, (pack_up,), (), (g_out, g_gate, g_up),
     )
 
@@ -1220,16 +1228,25 @@
     column = lambda part, came: (wide(dyn(part, ii, 1)) + sum(wide(a) for a in came)).astype(BF)
     close = lambda own, came: wide(own) + sum(wide(a) for a in came)
 
-    dn_came = to_y(dn_pair)
-    part_down = dot_tn(flat(hidden), flat(cot_all)).astype(BF).reshape(outer, inner, frows, d)
+    dn_send = [dyn(dn_pair, (yi + j) % ys, 0) for j in range(1, ys)]
+    dn_came = [
+        lax.ppermute(a, "ctx", ctx_perm(lambda y, k: (y + j) % ys * 2 + k)) for j, a in enumerate(dn_send, 1)
+    ]
+    part_down = dot_tn(flat(after(hidden, dn_send)), flat(cot_all)).astype(BF).reshape(outer, inner, frows, d)
     par = oi % 2
-    by_parity = part_down.reshape(outer // 2, 2, inner, frows, d)
-    down_near, down_rest = dyn(by_parity, 1 - par, 1), dyn(by_parity, par, 1)
+
+    def by_parity(part):
+        part = part.reshape((outer // 2, 2) + part.shape[1:])
+        return dyn(part, 1 - par, 1), dyn(part, par, 1)
+
+    down_near, down_rest = by_parity(part_down)
     near_x = to_inner(down_near)
     rest_x = to_inner(down_rest)
     shape_g = (outer, inner, ctx, rows, f)
     part_gate = dot_tn(flat(normed_all), flat(d_gate)).astype(BF).reshape(shape_g)
-    gate_x = to_inner(part_gate)
+    gate_near, gate_rest = by_parity(part_gate)
+    gate_near_x = to_inner(gate_near)
+    gate_rest_x = to_inner(after(gate_rest, near_x))
     part_up = dot_tn(flat(normed_all), flat(after(d_up, part_gate))).astype(BF).reshape(shape_g)
     near = [j for j in steps if j in (1, outer - 1)]
     mid_way = [j for j in steps if j not in near]
@@ -1255,23 +1272,23 @@
 
     part_out = dot_tn(att_rows, d_mid_low.reshape(m * r, d)).astype(BF).reshape(dp, ys, 2, rows, d)
     rest_col = column(down_rest, after(rest_x, d_att_all))
-    gate_col = column(part_gate, after(gate_x, d_att_all))
+    gate_near_col = column(gate_near, after(gate_near_x, d_att_all))
 
     def back_cargo(cargo, moved, bufs):
-        (rest_col, gate_col, part_up, part_out, out_pair), (down_z, gate_z, up_x, po_in, out_came) = moved, bufs
+        (rest_col, gate_near_col, part_up, part_out, out_pair), (down_z, gate_z, up_x, po_in, out_came) = moved, bufs
         scatter_y(cargo, out_pair, out_came)
         scatter_inner(cargo, part_up, up_x)
         to_rest(cargo, rest_col, down_z)
-        scatter_outer(cargo, gate_col, gate_z, near)
+        to_near(cargo, gate_near_col, gate_z)
         cargo.put(part_out.at[:, :, 1 - cargo.k], po_in, cargo.ctx_dev(cargo.y, 1 - cargo.k))
 
     down_z, gate_z, up_x, po_in, out_came, dq, dkv = attend_back_call(
-        z, q, k, v, qdoc, kdoc, att, d_att_all, lse, cos, sin, hc, kvc,
+        z, q, k, v, qdoc, kdoc, att, d_att_all, lse, table, hc, kvc,
         back_cargo,
-        (rest_col, gate_col, part_up, part_out, out_pair),
+        (rest_col, gate_near_col, part_up, part_out, out_pair),
         (
-            sds((outer - 1,) + gate_col.shape[1:]),
-            sds((inner - 1, outer) + gate_col.shape[1:]),
+            sds((outer - 1,) + gate_near_col.shape[1:]),
+            sds((inner - 1, outer) + gate_near_col.shape[1:]),
             sds((dp, ys, rows, d)),
             sds((ys - 1, m, r, d)),
         ),
@@ -1280,9 +1297,10 @@
     po_both = lambda at: wide(dyn(dyn(part_out, ki, 2), at, 1)) + wide(dyn(po_in, at, 1))
     po_send = jnp.stack([po_both((yi + j) % ys).astype(BF) for j in range(1, ys)])
     po_send = po_send.reshape(ys - 1, outer, inner, rows, d)
+    gate_rest_col = column(gate_rest, after(gate_rest_x, dq))
     gate_far = [
         lax.ppermute(
-            dyn(after(gate_col, dq), (oi + j) % outer, 0), "dp", dp_perm(lambda o, i: (o + j) % outer * inner + i)
+            dyn(gate_rest_col, (oi + j) % outer // 2, 0), "dp", dp_perm(lambda o, i: (o + j) % outer * inner + i)
         )
         for j in mid_way
     ]
@@ -1290,8 +1308,7 @@
     part_kv = dot_tn(flat(normed_a), flat(dkv)).astype(BF).reshape(outer, inner, ctx, rows, 2 * kvc * LANES)
     up_col = column(part_up, [up_x[j] for j in range(inner - 1)])
     po = po_both(yi).astype(BF).reshape(outer, inner, rows, d)
-    gate_near = [gate_z[j - 1] for j in near]
-    gate_mine = close(dyn(gate_col, oi, 0), gate_near + gate_far).astype(BF)
+    gate_mine = close(dyn(gate_rest_col, oi // 2, 0), [gate_z[j - 1] for j in near] + gate_far).astype(BF)
 
     outputs, input_grad, grad_out, q_all, kv_all, gate_all, up_all = tail_call(
         z, hc, dq, dkv, wqkv, part_q, part_kv, po, po_send, up_col, gain_a, gate_mine,

time: 550 us -> 540 us (0.982)
  waiting for transfers between devices: 12.6 us -> 1.01 us
    ppermute x2, waiting for transfers between devices: 10.9 us -> 0.01 us  [the longest x1 0.01 us: per_device(): lax.ppermute(a, 'ctx', ctx_perm(lambda y, k: (y + j) % ys * 2 + k))]
  transfers between devices with their start and end apart: 5 -> 6, of which waited for: 2 -> 1; matrix products, arithmetic and copies ran while one was open for 9% -> 12% of each run, Pallas kernels for 5% -> 13%
where the time goes in v5:
time: 540 us; the launch traced here: 534 us
  Pallas kernels  418 us (77%)
  matrix products  46.5 us (9%)
  local copies, waits for them, and re-layouts  35.8 us (7%)
  other arithmetic  25.4 us (5%)
  starting transfers between devices  5.42 us (1%)
    pallas_call x5, Pallas kernels, fused_call(): pl.pallas_call(kernel, name=name, grid=grid, in_specs=list(in_specs) + [h...  155 us
    pallas_call x3, Pallas kernels, communicate(): pl.pallas_call(kernel, name=name, out_shape=list(outs), in_specs=[hbm] *...  128 us
    pallas_call x1, Pallas kernels, tail_call(): pl.pallas_call(functools.partial(tail_kernel, z, hc), name='tail', in_spe...  83.4 us
    pallas_call x1, Pallas kernels, mlp_call(): pl.pallas_call(functools.partial(mlp_kernel, z), name='mlp', grid=(2, z.y...  51.6 us
    dot_general x6, matrix products, dot_tn(): lax.dot_general(a, b, (((0,), (0,)), ((), ())), preferred_element_type=F32)  46.5 us
  transfers between devices with their start and end apart: 6, of which 1 were waited for; matrix products, arithmetic and copies ran while one was open for 12% of the time, Pallas kernels for 13%

profile of v5, /device:TPU:0, one launch (start us, length us, event | category | flops | bytes accessed | tf_op | source)
XLA Modules:
  0.0 534.1 jit_solution(8210670419408343750)
XLA Ops:
  0.7 1.3 reshape.248
  2.1 0.9 reshape.249.refs_6_.refs_4_
  3.0 1.3 reshape.243
  6.3 0.9 reshape.247.refs_5_
  7.3 0.6 fusion.16.refs_3_
  7.9 0.8 maximum_bitcast_fusion.refs_2_
  8.7 58.8 %gather_first.1 = (bf16[4,2,256,1536]{3,2,1,0:T(8,128)(2,1)}, s32[4,2,256]{2,1,0:T(2,128)}, bf16[8,4,48,1024]{3,2,1,0:T(8,128)(2,1)}, f32[8,4,8,128]{3,2,1,0:T(8...) custom-call(bf16[2,256,1536]{2,1,0:T(8,128)(2,1)} %x_hbm.1, ...), custom_call_target="tpu_custom_call" | custom-call | tf_op jit(solution)/shard_map/gather_first/pallas_call | solution.py:160
  67.5 1.1 slice_reduce_fusion
  68.6 0.7 reshape_squeeze.6.refs_1_.gain_ref
  69.3 1.3 reshape.253.refs_4_
  70.6 2.1 copy.92.refs_3_
  72.6 0.7 reshape_squeeze.7.refs_2_.refs_4_
  73.3 1.9 multiply_cosine_fusion
  75.2 1.0 select_maximum_fusion
  76.3 23.0 %qkv.1 = (bf16[8,2,2,48,1536]{4,3,2,1,0:T(8,128)(2,1)}, bf16[8,4,48,1024]{3,2,1,0:T(8,128)(2,1)}, bf16[8,4,48,1024]{3,2,1,0:T(8,128)(2,1)}, bf16[4,2,256,1536]{3...) custom-call(bf16[4,2,256,1536]{3,2,1,0:T(8,128)(2,1)} %get-tuple-ele, ...), custom_call_target="tpu_custom_call", output_to_operand_aliasing={{0}: (5, {}), {1}: (6, {}), {2}: (7, {})} | custom-call | tf_op jit(solution)/shard_map/qkv/pallas_call | solution.py:296
  99.2 29.2 %attend.1 = (bf16[8,2,2,48,1536]{4,3,2,1,0:T(8,128)(2,1)}, bf16[8,4,48,1024]{3,2,1,0:T(8,128)(2,1)}, bf16[8,4,48,1024]{3,2,1,0:T(8,128)(2,1)}, bf16[4,2,256,1536...) custom-call(bf16[4,2,256,512]{3,2,1,0:T(8,128)(2,1)} %get-tuple-elem, ...), custom_call_target="tpu_custom_call", output_to_operand_aliasing={{0}: (6, {}), {1}: (7, {}), {2}: (8, {})} | custom-call | tf_op jit(solution)/shard_map/attend/pallas_call | solution.py:296
  128.5 27.8 %exchange_heads.1 = (bf16[8,2,2,48,1536]{4,3,2,1,0:T(8,128)(2,1)}, bf16[8,4,48,1024]{3,2,1,0:T(8,128)(2,1)}, bf16[8,4,48,1024]{3,2,1,0:T(8,128)(2,1)}, bf16[8,12...) custom-call(bf16[4,2,256,384]{3,2,1,0:T(8,128)(2,1)} %get-tuple-elem, ...), custom_call_target="tpu_custom_call", output_to_operand_aliasing={{0}: (2, {}), {1}: (3, {}), {2}: (4, {}), {3}: (5, {}), {4}... | custom-call | tf_op jit(solution)/shard_map/exchange_heads/pallas_call | solution.py:160
  156.3 34.6 %mix.1 = (bf16[8,4,48,1024]{3,2,1,0:T(8,128)(2,1)}, bf16[8,4,48,1024]{3,2,1,0:T(8,128)(2,1)}, bf16[8,128,1536]{2,1,0:T(8,128)(2,1)}, bf16[4,2,256,1536]{3,2,1,0:...) custom-call(bf16[4,2,256,384]{3,2,1,0:T(8,128)(2,1)} %get-tuple-elem, ...), custom_call_target="tpu_custom_call", output_to_operand_aliasing={{0}: (5, {}), {1}: (6, {}), {2}: (7, {}), {3}: (8, {})} | custom-call | tf_op jit(solution)/shard_map/mix/pallas_call | solution.py:296
  190.9 41.8 %gather_third.1 = (bf16[8,4,48,1024]{3,2,1,0:T(8,128)(2,1)}, bf16[8,128,1536]{2,1,0:T(8,128)(2,1)}, bf16[4,2,256,1536]{3,2,1,0:T(8,128)(2,1)}, bf16[4,2,256,1536]{3,2,1,0:T(8,128)(2,1)}) custom-call(bf16[2,256,1536]{2,1,0:T(8,128)(2,1)} %get-tuple-element.103.refs_0_, ...), custom_call_target="tpu_custom_call", output_to_operand_aliasing={{0}: (1, {}), {1}: (2, {}), {2}: (3, {})} | custom-call | tf_op jit(solution)/shard_map/gather_third/pallas_call | solution.py:160
  232.7 51.6 %mlp.1 = (bf16[4,2,256,1024]{3,2,1,0:T(8,128)(2,1)}, bf16[4,2,256,1024]{3,2,1,0:T(8,128)(2,1)}, bf16[4,2,256,1024]{3,2,1,0:T(8,128)(2,1)}, bf16[2,2,256,1536]{3,2,1,0:T(8,128)(2,1)}, bf16[2,2,256,1536]{3,2,1,0:T(8,128)(2,1)}) custom-call(bf16[4,2,256,1536]{3,2,1,0:T(8,128)(2,1)} %get-tuple-element.107.x_ref, ...), custom_call_target="tpu_custom_call" | custom-call | tf_op jit(solution)/shard_map/mlp/pallas_call | solution.py:745
  284.3 2.7 dynamic-slice_bitcast_fusion.1
  287.0 1.6 collective-permute-start
  288.6 10.4 %bitcast_convert_fusion.3 = bf16[1024,1536]{1,0:T(8,128)(2,1)S(1)} fusion(bf16[4,2,256,1024]{3,2,1,0:T(8,128)(2,1)} %get-tuple-element.115, bf16[4,2,256,1536]{3,2,1,0:T(8,128)(2,1)} %get-tuple-element.108.cot_ref), kind=kOutput, calls=%fused_computation.3 | convolution fusion | flops 6444023808 | bytes 13631488 | tf_op jit(solution)/shard_map/dot_general | solution.py:40
  299.0 1.2 dynamic-slice_bitcast_fusion.4
  300.8 0.6 copy-done.5
  301.4 10.7 %bitcast_convert_fusion.1 = bf16[1536,1024]{1,0:T(8,128)(2,1)S(1)} fusion(bf16[4,2,256,1536]{3,2,1,0:T(8,128)(2,1)} %get-tuple-element.107.x_ref, bf16[4,2,256,1024]{3,2,1,0:T(8,128)(2,1)} %get-tuple-element.121), kind=kOutput, calls=%fused_computation.1 | convolution fusion | flops 6444023808 | bytes 13631488 | tf_op jit(solution)/shard_map/dot_general | solution.py:40
  312.1 1.0 dynamic-slice_bitcast_fusion.3
  313.0 0.5 collective-permute-start.3
  313.6 1.5 collective-permute-start.2
  315.1 8.2 %bitcast_convert_fusion.2 = bf16[1536,1024]{1,0:T(8,128)(2,1)} fusion(bf16[4,2,256,1536]{3,2,1,0:T(8,128)(2,1)S(1)} %bitcast.167, bf16[4,2,256,1024]{3,2,1,0:T(8,128)(2,1)S(1)} %copy-done.25), kind=kOutput, calls=%fused_computation.2 | convolution fusion | flops 6444023808 | bytes 13631488 | tf_op jit(solution)/shard_map/dot_general | solution.py:40
  323.4 1.0 dynamic-slice_bitcast_fusion.2
  324.4 0.5 collective-permute-start.4
  325.0 2.4 fusion.8.refs_6_
  327.4 26.3 %turn.1 = (bf16[3,128,1536]{2,1,0:T(8,128)(2,1)}, f32[2,256,1536]{2,1,0:T(8,128)}, bf16[2,256,1536]{2,1,0:T(8,128)(2,1)}, bf16[4,2,256,384]{3,2,1,0:T(8,128)(2,1)}) custom-call(bf16[2,2,256,1536]{3,2,1,0:T(8,128)(2,1)} %get-tuple-element.112.refs_0_, bf16[2,256,1536]{2,1,0:T(8,128)(2,1)} %collective-permute-done.refs_1_, ...), custom_call_target="tpu_custom_call" | custom-call | tf_op jit(solution)/shard_map/turn/pallas_call | solution.py:296
  353.7 1.0 collective-permute-done.2
  354.7 2.4 fusion.7.refs_9_
  357.1 2.3 fusion.6.refs_10_
  359.5 4.5 bitcast_convert_fusion
  363.9 41.8 %attend_back.1 = (bf16[3,128,1536]{2,1,0:T(8,128)(2,1)}, bf16[3,4,48,1024]{3,2,1,0:T(8,128)(2,1)}, bf16[1,4,4,48,1024]{4,3,2,1,0:T(8,128)(2,1)}, bf16[8,2,48,153...) custom-call(bf16[4,2,256,512]{3,2,1,0:T(8,128)(2,1)} %get-tuple-elem, ...), custom_call_target="tpu_custom_call", output_to_operand_aliasing={{0}: (14, {})} | custom-call | tf_op jit(solution)/shard_map/attend_back/pallas_call | solution.py:296
  405.8 1.6 fusion.5
  407.4 0.8 collective-permute-start.5
  408.4 0.7 copy-done.7
  409.1 7.7 %fusion.1 = bf16[1536,512]{1,0:T(8,128)(2,1)} fusion(bf16[4,2,256,1536]{3,2,1,0:T(8,128)(2,1)} %get-tuple-element.129, bf16[4,2,256,512]{3,2,1,0:T(8,128)(2,1)S(1)} %copy-done.7), kind=kOutput, calls=%fused_computation.8 | convolution fusion | flops 3222011904 | bytes 9961472 | tf_op jit(solution)/shard_map/dot_general | solution.py:40
  416.8 5.0 fusion.2
  422.0 1.4 fusion.3.po_send
  423.5 1.4 fusion.4.po_own
  424.8 1.1 add_bitcast_fusion
  425.9 0.7 copy-done.9
  426.6 1.9 fusion.up_ref
  428.5 1.0 fusion.9.gate_hbm
  429.5 83.4 %tail.1 = (f32[2,256,1536]{2,1,0:T(8,128)}, f32[2,256,1536]{2,1,0:T(8,128)}, f32[48,1536]{1,0:T(8,128)}, bf16[4,48,512]{2,1,0:T(8,128)(2,1)}, bf16[4,48,512]{2,1...) custom-call(bf16[4,2,256,512]{3,2,1,0:T(8,128)(2,1)} %get-tuple-element.127.dq_hbm, ...), custom_call_target="tpu_custom_call" | custom-call | tf_op jit(solution)/shard_map/tail/pallas_call | solution.py:939
  512.9 1.1 copy.119
  514.6 1.2 reshape.298
  516.5 1.2 reshape.300
  518.5 0.8 reshape.294
  519.7 0.8 reshape.296
  520.7 1.2 slice_convert_fusion
  521.9 2.2 reshape.307
  524.2 1.2 multiply_reduce_fusion.2
  525.4 1.9 multiply_reduce_fusion
  528.5 1.7 copy.151
  530.2 1.4 copy-done.3
  531.5 1.7 copy.152
  533.2 0.7 copy.153
  (113 shorter events, 7.0 us)
Async XLA Ops:
  0.6 4.4 copy-start.19
  0.7 5.1 copy-start.17
  0.7 5.3 copy-start.10
  4.3 2.9 copy-start.23
  4.4 2.9 copy-start.24
  287.0 40.4 %collective-permute-start = (bf16[2,256,1536]{2,1,0:T(8,128)(2,1)}, bf16[2,256,1536]{2,1,0:T(8,128)(2,1)}, u32[]{:S(2)}, u32[]{:S(2)}) collective-permute-start(bf16[2,256,1536]{2,1,0:T(8,128)(2,1)} %dynamic-slice_bitcast_fusion.1), channel_id=1, source_target_pairs={{0,2},{1,3},{2,0},{3,1},{4,6},{5,7},{6,4},{7,5},{8,10},{9,11},{10,... | collective-permute-start | bytes 4718600 | tf_op jit(solution)/shard_map/ppermute | solution.py:1233
  299.0 2.4 copy-start.5
  299.0 16.1 %slice-start.2 = ((s8[6291456]{0:T(1024)(128)(4,1)}), s8[4194304]{0:T(1024)(128)(4,1)S(1)}, s32[]{:S(2)}) async-start(s8[6291456]{0:T(1024)(128)(4,1)} %bitcast.166), calls=%async_computation.2 | async-start | bytes 8388608
  300.3 23.2 %collective-permute-start.1 = (bf16[2,128,1536]{2,1,0:T(8,128)(2,1)}, bf16[2,128,1536]{2,1,0:T(8,128)(2,1)}, u32[]{:S(2)}, u32[]{:S(2)}) collective-permute-start(bf16[2,128,1536]{2,1,0:T(8,128)(2,1)} %get-tuple-element.150), channel_id=1, source_target_pairs={{0,4},{4,0},{8,12},{12,8},{16,20},{20,16},{24,28},{28,24},{1,5},{5... | collective-permute-start | bytes 2359304 | tf_op jit(solution)/shard_map/ppermute | solution.py:1222
  301.4 13.7 %slice-start.3 = ((s8[6291456]{0:T(1024)(128)(4,1)}), s8[2097152]{0:T(1024)(128)(4,1)S(1)}, s32[]{:S(2)}) async-start(s8[6291456]{0:T(1024)(128)(4,1)} %bitcast.166), calls=%async_computation.3 | async-start | bytes 4194304
  301.4 13.7 %copy-start.25 = (bf16[4,2,256,1024]{3,2,1,0:T(8,128)(2,1)S(1)}, bf16[4,2,256,1024]{3,2,1,0:T(8,128)(2,1)}, u32[]{:S(2)}) copy-start(bf16[4,2,256,1024]{3,2,1,0:T(8,128)(2,1)} %get-tuple-element.116) | copy-start | bytes 12582916
  313.0 40.7 %collective-permute-start.3 = (bf16[2,4,48,1024]{3,2,1,0:T(8,128)(2,1)}, bf16[2,4,48,1024]{3,2,1,0:T(8,128)(2,1)}, u32[]{:S(2)}, u32[]{:S(2)}) collective-permute-start(bf16[2,4,48,1024]{3,2,1,0:T(8,128)(2,1)} %dynamic-slice_bitcast_fusion.3), channel_id=1, source_target_pairs={{0,4},{4,0},{8,12},{12,8},{16,20},{20,16},{24,28},{28,24},{1,5},{5... | collective-permute-start | bytes 2359304 | tf_op jit(solution)/shard_map/ppermute | solution.py:1222
  313.6 41.1 %collective-permute-start.2 = (bf16[2,128,1536]{2,1,0:T(8,128)(2,1)}, bf16[2,128,1536]{2,1,0:T(8,128)(2,1)}, u32[]{:S(2)}, u32[]{:S(2)}) collective-permute-start(bf16[2,128,1536]{2,1,0:T(8,128)(2,1)} %get-tuple-element.149), channel_id=1, source_target_pairs={{0,4},{4,0},{8,12},{12,8},{16,20},{20,16},{24,28},{28,24},{1,5},{5... | collective-permute-start | bytes 2359304 | tf_op jit(solution)/shard_map/ppermute | solution.py:1222
  324.4 81.4 %collective-permute-start.4 = (bf16[2,4,48,1024]{3,2,1,0:T(8,128)(2,1)}, bf16[2,4,48,1024]{3,2,1,0:T(8,128)(2,1)}, u32[]{:S(2)}, u32[]{:S(2)}) collective-permute-start(bf16[2,4,48,1024]{3,2,1,0:T(8,128)(2,1)} %dynamic-slice_bitcast_fusion.2), channel_id=1, source_target_pairs={{0,4},{4,0},{8,12},{12,8},{16,20},{20,16},{24,28},{28,24},{1,5},{5... | collective-permute-start | bytes 2359304 | tf_op jit(solution)/shard_map/ppermute | solution.py:1222
  353.7 5.8 %copy-start.26 = (bf16[2,256,1536]{2,1,0:T(8,128)(2,1)S(1)}, bf16[2,256,1536]{2,1,0:T(8,128)(2,1)}, u32[]{:S(2)}) copy-start(bf16[2,256,1536]{2,1,0:T(8,128)(2,1)} %get-tuple-element.123) | copy-start | bytes 4718596
  353.7 5.8 %copy-start.27 = (bf16[2,256,1536]{2,1,0:T(8,128)(2,1)S(1)}, bf16[2,256,1536]{2,1,0:T(8,128)(2,1)}, u32[]{:S(2)}) copy-start(bf16[2,256,1536]{2,1,0:T(8,128)(2,1)} %get-tuple-element.124) | copy-start | bytes 4718596
  405.8 2.4 copy-start.6
  407.4 1.7 copy-start.7
  407.4 21.0 %collective-permute-start.5 = (bf16[4,48,1024]{2,1,0:T(8,128)(2,1)S(1)}, bf16[4,48,1024]{2,1,0:T(8,128)(2,1)S(1)}, u32[]{:S(2)}, u32[]{:S(2)}) collective-permute-start(bf16[4,48,1024]{2,1,0:T(8,128)(2,1)S(1)} %dynamic-slice_bitcast_fusion.6), channel_id=1, source_target_pairs={{0,16},{4,20},{8,24},{12,28},{16,0},{20,4},{24,8},{28,12},{1,17},{... | collective-permute-start | bytes 1179656 | tf_op jit(solution)/shard_map/ppermute | solution.py:1302
  408.2 8.6 %slice-start.4 = ((s8[6291456]{0:T(1024)(128)(4,1)}), s8[4194304]{0:T(1024)(128)(4,1)S(1)}, s32[]{:S(2)}) async-start(s8[6291456]{0:T(1024)(128)(4,1)} %bitcast.197), calls=%async_computation.4 | async-start | bytes 8388608
  409.1 7.8 %copy-start.8 = (bf16[4,2,256,512]{3,2,1,0:T(8,128)(2,1)S(1)}, bf16[4,2,256,512]{3,2,1,0:T(8,128)(2,1)}, u32[]{:S(2)}) copy-start(bf16[4,2,256,512]{3,2,1,0:T(8,128)(2,1)} %get-tuple-element.128.dkv_hbm) | copy-start | bytes 6291460
  409.1 7.8 %slice-start.5 = ((s8[6291456]{0:T(1024)(128)(4,1)}), s8[2097152]{0:T(1024)(128)(4,1)S(1)}, s32[]{:S(2)}) async-start(s8[6291456]{0:T(1024)(128)(4,1)} %bitcast.197), calls=%async_computation.5 | async-start | bytes 4194304
  409.1 12.8 %slice-start = ((s8[4718592]{0:T(1024)(128)(4,1)}), s8[4194304]{0:T(1024)(128)(4,1)S(1)}, s32[]{:S(2)}) async-start(s8[4718592]{0:T(1024)(128)(4,1)} %bitcast.161), calls=%async_computation | async-start | bytes 8388608
  416.8 5.0 slice-start.1
  422.0 2.8 copy-start.1
  422.0 2.8 copy-start.2
  423.5 2.4 copy-start
  423.5 3.1 copy-start.9
  424.8 3.6 copy-start.14
  512.9 2.9 copy-start.15
  515.8 1.9 copy-start.21
  516.5 4.0 copy-start.22
  520.7 7.8 %copy-start.4 = (f32[2,256,1536]{2,1,0:T(8,128)S(1)}, f32[2,256,1536]{2,1,0:T(8,128)}, u32[]{:S(2)}) copy-start(f32[2,256,1536]{2,1,0:T(8,128)} %get-tuple-element.172) | copy-start | bytes 9437188
  521.9 5.9 %copy-start.18 = (bf16[48,768]{1,0:T(8,128)(2,1)S(1)}, bf16[48,768]{1,0:T(8,128)(2,1)}, u32[]{:S(2)}) copy-start(bf16[48,768]{1,0:T(8,128)(2,1)} %param.17) | copy-start | bytes 221188
  524.1 3.7 copy-start.12
  524.1 3.7 copy-start.13
  524.1 3.7 copy-start.20
  524.2 5.9 %copy-start.11 = (f32[6,8,4,384]{3,1,2,0:T(8,128)}, f32[6,8,4,384]{3,1,2,0:T(8,128)S(1)}, u32[]{:S(2)}) copy-start(f32[6,8,4,384]{3,1,2,0:T(8,128)S(1)} %copy.118) | copy-start | bytes 884740
  528.5 3.0 copy-start.3
  531.5 1.7 copy-start.16
